TPU v7x, 32 devices: a whole 2x2x4 slice. The times are simulated.
32 devices in a mesh: row: 8 (over y, x, core), col: 4 (over z).
Axes of the slice: x: 2, y: 2, z: 4, core: 2. Of those that a mesh axis runs over, the one named last changes fastest.
Arguments:
- tile_u: float32 [8, 16, 2048, 128], P('row', 'col'), may hold values from -6 to 6
- tile_v: float32 [8, 16, 2048, 128], P('row', 'col'), may hold values from -1.5 to 1.5
- row_panel_u: float32 [8, 2048, 128], P('row', 'col'), may hold values from -6 to 6
- row_panel_v: float32 [8, 2048, 128], P('row', 'col'), may hold values from -0.125 to 0.125
- col_panel_u: float32 [16, 2048, 128], P('row', 'col'), may hold values from -6 to 6
- col_panel_v: float32 [16, 2048, 128], P('row', 'col'), may hold values from -0.125 to 0.125
- diag_inverse: float32 [2048, 2048], P('col'), may hold values from -0.15 to 2, as said below
- sketch: float32 [2048, 128], replicated, may hold values from -0.125 to 0.125
Outputs:
- new_u: float32 [8, 16, 2048, 128], P('row', 'col')
- new_v: float32 [8, 16, 2048, 128], P('row', 'col')
Inputs may be any that keep to these rules, and one draw needn't show every extreme that they name: `diag_inverse`: lower triangular; the diagonal lies between 0.5 and 2, the entries below it between -0.15 and 0.15.
All inputs are finite; a program needn't handle non-finite values.
Results may differ from a plain program's by a relative error of at most 0.0003.
Values sent between devices are 32-bit elements; how exact they have to be, the bound alone decides.
No kernel may reach another device: no remote copies, remote signals or barrier semaphores. Data moves between devices by JAX's collectives and lax.ppermute only.
A program may use at most 128 MiB of HBM per device.

v0:
```python
import math

import jax
import jax.numpy as jnp
from jax import lax
from jax.sharding import PartitionSpec as P

highest = lax.Precision.HIGHEST


def body(tile_u, tile_v, row_panel_u, row_panel_v, col_panel_u, col_panel_v, diag_inverse, sketch):
    first = jnp.einsum(
        "ab,tbk->tak",
        diag_inverse,
        lax.all_gather(row_panel_v, "col", axis=1, tiled=True),
        precision=highest,
    )
    second = jnp.einsum(
        "ab,tbk->tak",
        diag_inverse,
        lax.all_gather(col_panel_v, "col", axis=1, tiled=True),
        precision=highest,
    )
    col_u_rows, col_v_rows = (
        lax.all_gather(col_panel_u, "row", axis=0, tiled=True),
        lax.all_gather(second, "row", axis=0, tiled=True),
    )
    row_u_full = lax.all_gather(row_panel_u, "col", axis=1, tiled=True)
    col_u_full = lax.all_to_all(col_u_rows, "col", split_axis=0, concat_axis=1, tiled=True)
    partial_cores = jnp.einsum("iak,jal->ijkl", first, col_v_rows, precision=highest)
    cores = lax.psum_scatter(partial_cores, "col", scatter_dimension=1, tiled=True)
    branch = -jnp.einsum("iak,ijkl->ijal", row_u_full, cores, precision=highest)
    left_side = jnp.concatenate([tile_u, branch], axis=-1)
    right_side = jnp.concatenate([tile_v, col_u_full[None]], axis=-1)
    projected = jnp.einsum("ijar,ak->ijrk", right_side, sketch, precision=highest)
    sample = jnp.einsum("ijar,ijrk->ijak", left_side, projected, precision=highest)
    gram_matrix = jnp.einsum("ijak,ijal->ijkl", sample, sample, precision=highest)
    factor = jnp.linalg.cholesky(gram_matrix)
    solved_t = jax.scipy.linalg.solve_triangular(factor, jnp.swapaxes(sample, -1, -2), lower=True)
    basis = jnp.swapaxes(solved_t, -1, -2)
    coefficients = jnp.einsum("ijar,ijak->ijrk", left_side, basis, precision=highest)
    scaling = math.sqrt(tile_u.shape[2])
    new_v = jnp.einsum("ijar,ijrk->ijak", right_side, coefficients, precision=highest) / scaling
    return (basis * scaling, new_v)


def solution(mesh):
    in_specs = (
        P("row", "col", None, None),
        P("row", "col", None, None),
        P("row", "col", None),
        P("row", "col", None),
        P("row", "col", None),
        P("row", "col", None),
        P("col", None),
        P(),
    )
    out_specs = (P("row", "col", None, None), P("row", "col", None, None))
    return jax.shard_map(body, mesh=mesh, in_specs=in_specs, out_specs=out_specs, check_vma=False)
```

profile of v0, /device:TPU:0, one launch (start us, length us, event | category | flops | bytes accessed | tf_op | source)
XLA Modules:
  0.0 438.9 jit_solution(14853244521627657069)
XLA Ops:
  7.2 0.0 copy-start
  7.2 0.0 all-gather.6.cloned.1.call-start
  7.2 2.1 copy.31
  9.3 0.0 all-gather.6.cloned.1.call-update
  9.4 0.0 all-gather.14.cloned.1.call-start
  9.4 0.7 all-gather.14.cloned.1.call-update
  10.1 0.0 all-gather.10.cloned.1.call-start
  10.2 0.7 all-gather.10.cloned.1.call-update
  10.9 0.0 all-gather.8.cloned.1.call-start
  10.9 47.6 %all-gather.6.cloned.1.call-done = f32[2,2048,128]{1,2,0:T(8,128)} async-done(((f32[2,512,128]{1,2,0:T(8,128)}), f32[2,2048,128]{1,2,0:T(8,128)}) %all-gather.6.cloned.1.call-update) | async-done | bytes 2097168 | tf_op jit(solution)/shard_map/all_gather | solution.py:21
  58.5 6.2 %fusion.8 = f32[2,512,128]{1,2,0:T(8,128)S(1)} fusion(f32[2,2048,128]{1,2,0:T(8,128)} %all-gather.6.cloned.1.call-done, f32[512,2048]{1,0:T(8,128)} %param.14), kind=kOutput, calls=%fused_computation.14 | convolution fusion | flops 3221225472 | bytes 6815744 | tf_op jit(solution)/shard_map/ab,tbk->tak/dot_general | solution.py:18
  64.8 1.0 copy.32
  65.8 0.0 all-gather.8.cloned.1.call-update
  65.8 30.0 %all-gather.14.cloned.1.call-done = f32[16,512,128]{2,1,0:T(8,128)} async-done(((f32[2,512,128]{2,1,0:T(8,128)}), f32[16,512,128]{2,1,0:T(8,128)}) %all-gather.14.cloned.1.call-update) | async-done | bytes 4194320 | tf_op jit(solution)/shard_map/all_gather | solution.py:25
  95.9 4.8 %all-to-all-start = ((f32[16,512,128]{2,1,0:T(8,128)}), f32[16,512,128]{2,1,0:T(8,128)}, u32[]{:S(2)}, u32[]{:S(2)}) async-start(f32[16,512,128]{2,1,0:T(8,128)} %all-gather.14.cloned.1.call-done), calls=%async_computation.1 | async-start | bytes 8388608 | tf_op jit(solution)/shard_map/all_to_all | solution.py:29
  100.7 0.0 all-gather.12.cloned.1.call-start
  100.8 0.5 all-gather.12.cloned.1.call-update
  101.3 0.2 reduce-scatter.2.cloned.1.call-start
  101.5 52.2 %all-gather.10.cloned.1.call-done = f32[1,2048,128]{2,1,0:T(8,128)} async-done(((f32[1,512,128]{2,1,0:T(8,128)}), f32[1,2048,128]{2,1,0:T(8,128)}) %all-gather.10.cloned.1.call-update) | async-done | bytes 1048592 | tf_op jit(solution)/shard_map/all_gather | solution.py:15
  153.7 7.0 %convolution_bitcast_fusion.1 = f32[512,128,1]{0,1,2:T(8,128)S(1)} fusion(f32[512,2048]{1,0:T(8,128)} %param.14, f32[1,2048,128]{2,1,0:T(8,128)} %all-gather.10.cloned.1.call-done), kind=kOutput, calls=%fused_computation.15 | convolution fusion | flops 1610612736 | bytes 5505024 | tf_op jit(solution)/shard_map/ab,tbk->tak/dot_general | solution.py:12
  160.7 30.1 %all-gather.8.cloned.1.call-done = f32[16,512,128]{2,1,0:T(8,128)} async-done(((f32[2,512,128]{2,1,0:T(8,128)}), f32[16,512,128]{2,1,0:T(8,128)}) %all-gather.8.cloned.1.call-update) | async-done | bytes 4194320 | tf_op jit(solution)/shard_map/all_gather | solution.py:26
  190.7 9.8 %convolution_bitcast_fusion = f32[1,16,128,128]{2,3,1,0:T(8,128)} fusion(f32[16,512,128]{2,1,0:T(8,128)} %all-gather.8.cloned.1.call-done, f32[512,128,1]{0,1,2:T(8,128)S(1)} %convolution_bitcast_fusion.1), kind=kOutput, calls=%fused_computation.13 | convolution fusion | flops 1610612736 | bytes 5505024 | tf_op jit(solution)/shard_map/iak,jal->ijkl/dot_general | solution.py:30
  200.6 0.0 reduce-scatter.2.cloned.1.call-update
  200.6 5.7 %copy.35 = f32[1,4,2048,128]{2,3,1,0:T(8,128)} copy(f32[1,4,2048,128]{3,2,1,0:T(8,128)} %param.8) | data formatting | bytes 8388608 | tf_op args[0]
  206.3 5.4 %copy.37 = f32[1,4,2048,128]{2,3,1,0:T(8,128)} copy(f32[1,4,2048,128]{3,2,1,0:T(8,128)} %param.9) | data formatting | bytes 8388608 | tf_op args[1]
  211.8 16.7 %all-gather.12.cloned.1.call-done = f32[1,2048,128]{2,1,0:T(8,128)} async-done(((f32[1,512,128]{2,1,0:T(8,128)}), f32[1,2048,128]{2,1,0:T(8,128)}) %all-gather.12.cloned.1.call-update) | async-done | bytes 1048592 | tf_op jit(solution)/shard_map/all_gather | solution.py:28
  228.5 28.2 %reduce-scatter.2.cloned.1.call-done = f32[1,4,128,128]{2,3,1,0:T(8,128)} async-done(((f32[1,16,128,128]{2,3,1,0:T(8,128)}), f32[1,4,128,128]{2,3,1,0:T(8,128)}) %reduce-scatter.2.cloned.1.call-update) | async-done | bytes 262160 | tf_op jit(solution)/shard_map/reduce_scatter | solution.py:31
  256.7 6.7 %negate_bitcast_fusion = f32[1,4,2048,128]{2,3,1,0:T(8,128)} fusion(f32[1,2048,128]{2,1,0:T(8,128)} %all-gather.12.cloned.1.call-done, f32[1,4,128,128]{2,3,1,0:T(8,128)} %reduce-scatter.2.cloned.1.call-done), kind=kOutput, calls=%fused_computation.12 | convolution fusion | flops 1611661312 | bytes 5505024 | tf_op jit(solution)/shard_map/iak,ijkl->ijal/dot_general | solution.py:32
  263.4 0.0 all-to-all-done
  263.4 5.4 %copy.36 = f32[4,4,512,128]{2,0,3,1:T(4,128)} copy(f32[4,4,512,128]{3,2,1,0:T(8,128)} %bitcast.15) | data formatting | bytes 8388608 | tf_op jit(solution)/shard_map/all_to_all | solution.py:29
  268.9 6.0 %broadcast_in_dim.9 = f32[1,4,2048,128]{2,3,1,0:T(8,128)} reshape(f32[4,4,512,128]{2,1,3,0:T(4,128)} %bitcast.83) | data formatting | bytes 8388608 | tf_op jit(solution)/shard_map/broadcast_in_dim | solution.py:34
  274.9 0.0 copy-done
  274.9 0.0 copy-start.3
  274.9 0.0 copy-start.5
  274.9 9.7 %fusion.1 = f32[4,256,128]{2,1,0:T(8,128)S(1)} fusion(f32[1,4,2048,128]{2,3,1,0:T(8,128)} %broadcast_in_dim.9, f32[1,4,2048,128]{2,3,1,0:T(8,128)} %copy.37, f32[2048,128]{1,0:T(8,128)S(1)} %copy-done), kind=kOutput, calls=%fused_computation.3 | convolution fusion | flops 3223322624 | bytes 9961472 | tf_op jit(solution)/shard_map/ijar,ak->ijrk/dot_general | solution.py:35
  284.6 0.0 copy-done.3
  284.7 0.0 copy-done.5
  284.7 14.0 %fusion.3 = f32[4,2048,128]{2,1,0:T(8,128)S(1)} fusion(f32[4,256,128]{2,1,0:T(8,128)S(1)} %fusion.1, f32[1,4,2048,128]{2,3,1,0:T(8,128)S(1)} %copy-done.5, f32[1,4,2048,128]{2,3,1,0:T(8,128)S(1)} %copy-done.3), kind=kOutput, calls=%fused_computation.5 | convolution fusion | flops 3223322624 | bytes 13107200 | tf_op jit(solution)/shard_map/ijar,ijrk->ijak/dot_general | solution.py:36
  298.7 0.0 copy-start.2
  298.7 6.9 %fusion.21 = f32[4,128,128]{1,2,0:T(8,128)S(1)} fusion(f32[4,2048,128]{2,1,0:T(8,128)S(1)} %fusion.3), kind=kOutput, calls=%fused_computation.32 | convolution fusion | flops 1610612736 | bytes 4456448 | tf_op jit(solution)/shard_map/ijak,ijal->ijkl/dot_general | solution.py:37
  305.7 0.0 copy-done.2
  305.7 0.1 copy.41
  305.9 47.1 %custom-call.8 = f32[1,4,128,128]{3,2,1,0:T(8,128)S(1)} custom-call(f32[1,4,128,128]{3,2,1,0:T(8,128)S(1)} %fusion.14), custom_call_target="Cholesky" | custom-call | tf_op jit(solution)/shard_map/jit(cholesky)/cholesky | solution.py:38
  353.0 0.1 compare_reduce_fusion
  353.1 0.1 select_bitcast_fusion
  353.3 39.3 %custom-call.9 = f32[4,1,128,128]{2,3,1,0:T(8,128)S(1)} custom-call(f32[4,1,128,128]{3,2,1,0:T(8,128)S(1)} %select_bitcast_fusion), custom_call_target="InvertDiagBlocksLowerTriangular" | custom-call | tf_op jit(solution)/shard_map/jit(_solve_triangular)/vmap()/triangular_solve | solution.py:39
  392.6 0.0 copy-start.4
  392.6 0.0 copy-start.6
  392.6 5.9 %fusion.4 = f32[4,128,2048]{2,1,0:T(8,128)S(1)} fusion(f32[4,2048,128]{2,1,0:T(8,128)} %copy-done.2, f32[4,1,128,128]{2,3,1,0:T(8,128)S(1)} %custom-call.9), kind=kOutput, calls=%fused_computation.6 | convolution fusion | flops 1610612736 | bytes 8650752 | tf_op jit(solution)/shard_map/jit(_solve_triangular)/vmap()/triangular_solve | solution.py:39
  398.5 0.0 copy-done.4
  398.5 0.0 copy-done.6
  398.5 7.4 %fusion.2 = f32[4,256,128]{2,1,0:T(8,128)S(1)} fusion(f32[4,128,2048]{2,1,0:T(8,128)S(1)} %fusion.4, f32[1,4,2048,128]{2,3,1,0:T(8,128)S(1)} %copy-done.6, f32[1,4,2048,128]{2,3,1,0:T(8,128)S(1)} %copy-done.4), kind=kOutput, calls=%fused_computation.4 | convolution fusion | flops 3223322624 | bytes 13107200 | tf_op jit(solution)/shard_map/ijar,ijak->ijrk/dot_general | solution.py:41
  405.9 0.0 copy-start.7
  405.9 0.0 copy-start.8
  405.9 2.5 multiply_bitcast_fusion.1
  408.5 1.1 copy-done.7
  409.6 1.3 copy-done.8
  410.9 0.0 copy-start.1
  410.9 15.5 %multiply_bitcast_fusion = f32[1,4,2048,128]{3,2,1,0:T(8,128)} fusion(f32[4,256,128]{2,1,0:T(8,128)S(1)} %fusion.2, f32[1,4,2048,128]{2,3,1,0:T(8,128)S(1)} %copy-done.8, f32[1,4,2048,128]{2,3,1,0:T(8,128)S(1)} %copy-done.7), kind=kOutput, calls=%fused_computation.10 | convolution fusion | flops 3224371200 | bytes 13107200 | tf_op jit(solution)/shard_map/ijar,ijrk->ijak/dot_general | solution.py:43
  426.4 5.3 %copy.45 = f32[1,4,2048,128]{3,2,1,0:T(8,128)} copy(f32[1,4,2048,128]{2,3,1,0:T(8,128)} %multiply_bitcast_fusion.1) | data formatting | bytes 8388608
  431.7 0.0 copy-done.1
  (4 shorter events, 0.1 us)
Async XLA Ops:
  7.2 267.7 %copy-start = (f32[2048,128]{1,0:T(8,128)S(1)}, f32[2048,128]{1,0:T(8,128)}, u32[]{:S(2)}) copy-start(f32[2048,128]{1,0:T(8,128)} %param.15) | copy-start | bytes 3145732
  7.2 51.4 %all-gather.6.cloned.1.call-start = ((), (), s32[]{:S(2)}) async-start(), calls=%async_computation.2 | async-start | bytes 2621440 | tf_op jit(solution)/shard_map/all_gather | solution.py:21
  9.4 86.5 %all-gather.14.cloned.1.call-start = ((), (), s32[]{:S(2)}) async-start(), calls=%async_computation.7 | async-start | bytes 4718592 | tf_op jit(solution)/shard_map/all_gather | solution.py:25
  10.1 143.6 %all-gather.10.cloned.1.call-start = ((), (), s32[]{:S(2)}) async-start(), calls=%async_computation.4 | async-start | bytes 1310720 | tf_op jit(solution)/shard_map/all_gather | solution.py:15
  10.9 179.9 %all-gather.8.cloned.1.call-start = ((), (), s32[]{:S(2)}) async-start(), calls=%async_computation.3 | async-start | bytes 4718592 | tf_op jit(solution)/shard_map/all_gather | solution.py:26
  95.9 167.6 %all-to-all-start = ((f32[16,512,128]{2,1,0:T(8,128)}), f32[16,512,128]{2,1,0:T(8,128)}, u32[]{:S(2)}, u32[]{:S(2)}) async-start(f32[16,512,128]{2,1,0:T(8,128)} %all-gather.14.cloned.1.call-done), calls=%async_computation.1 | async-start | bytes 8388608 | tf_op jit(solution)/shard_map/all_to_all | solution.py:29
  100.7 127.8 %all-gather.12.cloned.1.call-start = ((), (), s32[]{:S(2)}) async-start(), calls=%async_computation.6 | async-start | bytes 1310720 | tf_op jit(solution)/shard_map/all_gather | solution.py:28
  101.3 155.4 %reduce-scatter.2.cloned.1.call-start = ((), (), s32[]{:S(2)}) async-start(), calls=%async_computation.5 | async-start | bytes 1310720 | tf_op jit(solution)/shard_map/reduce_scatter | solution.py:31
  274.9 9.7 %copy-start.3 = (f32[1,4,2048,128]{2,3,1,0:T(8,128)S(1)}, f32[1,4,2048,128]{2,3,1,0:T(8,128)}, u32[]{:S(2)}) copy-start(f32[1,4,2048,128]{2,3,1,0:T(8,128)} %copy.35) | copy-start | bytes 12582916
  274.9 9.7 %copy-start.5 = (f32[1,4,2048,128]{2,3,1,0:T(8,128)S(1)}, f32[1,4,2048,128]{2,3,1,0:T(8,128)}, u32[]{:S(2)}) copy-start(f32[1,4,2048,128]{2,3,1,0:T(8,128)} %negate_bitcast_fusion) | copy-start | bytes 12582916
  298.7 7.0 %copy-start.2 = (f32[4,2048,128]{2,1,0:T(8,128)}, f32[4,2048,128]{2,1,0:T(8,128)S(1)}, u32[]{:S(2)}) copy-start(f32[4,2048,128]{2,1,0:T(8,128)S(1)} %fusion.3) | copy-start | bytes 12582916
  392.6 5.9 %copy-start.4 = (f32[1,4,2048,128]{2,3,1,0:T(8,128)S(1)}, f32[1,4,2048,128]{2,3,1,0:T(8,128)}, u32[]{:S(2)}) copy-start(f32[1,4,2048,128]{2,3,1,0:T(8,128)} %copy.35) | copy-start | bytes 12582916
  392.6 5.9 %copy-start.6 = (f32[1,4,2048,128]{2,3,1,0:T(8,128)S(1)}, f32[1,4,2048,128]{2,3,1,0:T(8,128)}, u32[]{:S(2)}) copy-start(f32[1,4,2048,128]{2,3,1,0:T(8,128)} %negate_bitcast_fusion) | copy-start | bytes 12582916
  405.9 3.7 copy-start.7
  405.9 5.0 %copy-start.8 = (f32[1,4,2048,128]{2,3,1,0:T(8,128)S(1)}, f32[1,4,2048,128]{2,3,1,0:T(8,128)}, u32[]{:S(2)}) copy-start(f32[1,4,2048,128]{2,3,1,0:T(8,128)} %broadcast_in_dim.9) | copy-start | bytes 12582916
  410.9 20.9 %copy-start.1 = (f32[2048,128]{1,0:T(8,128)S(1)}, f32[2048,128]{1,0:T(8,128)}, u32[]{:S(2)}) copy-start(f32[2048,128]{1,0:T(8,128)} %param.15) | copy-start | bytes 3145732
Sparse Core Ops, SparseCore 0:
  10.1 48.3 all-gather.5
  60.4 35.3 all-gather.13
  97.4 56.2 all-gather.9
  156.0 34.6 all-gather.7
  192.1 36.3 all-gather.11
  231.2 25.4 reduce-scatter.1
where the time goes:
time: 442 us; the launch traced here: 439 us
  waiting for transfers between devices  207 us (47%)
  other arithmetic  89.3 us (20%)
  matrix products  89.2 us (20%)
  local copies, waits for them, and re-layouts  33.7 us (8%)
  between operations  14.6 us (3%)
  starting transfers between devices  5.25 us (1%)
    all_gather x1, waiting for transfers between devices, body(): lax.all_gather(row_panel_v, 'col', axis=1, tiled=True)  52.2 us
    all_gather x1, waiting for transfers between devices, body(): lax.all_gather(col_panel_v, 'col', axis=1, tiled=True)  47.6 us
    another operation x4, other arithmetic, body(): factor = jnp.linalg.cholesky(gram_matrix)  47.3 us
    another operation x3, other arithmetic, body(): jax.scipy.linalg.solve_triangular(factor, jnp.swapaxes(sample, -1, -2), l...  39.4 us
    all_gather x1, waiting for transfers between devices, body(): lax.all_gather(second, 'row', axis=0, tiled=True)  30.1 us
    all_gather x1, waiting for transfers between devices, body(): lax.all_gather(col_panel_u, 'row', axis=0, tiled=True)  30 us
    reduce_scatter x1, waiting for transfers between devices, body(): lax.psum_scatter(partial_cores, 'col', scatter_dimension=1, tiled=True)  28.2 us
    unnamed x22, local copies, waits for them, and re-layouts  21 us
  transfers between devices with their start and end apart: 7, of which 6 were waited for; matrix products, arithmetic and copies ran while one was open for 10% of the time, Pallas kernels for 0%

commit v1 on v0

v1 whole, which is shorter than its diff:
```python
import functools
import math

import jax
import jax.numpy as jnp
from jax import lax
from jax.experimental import pallas as pl
from jax.experimental.pallas import tpu as pltpu
from jax.sharding import PartitionSpec as P

f32, bf16 = jnp.float32, jnp.bfloat16
ANY, VMEM = pl.ANY, pltpu.VMEM
NT = (((1,), (1,)), ((), ()))
NN = (((1,), (0,)), ((), ()))
TN = (((0,), (0,)), ((), ()))


def mm(a, b, dims):
    return lax.dot_general(a, b, dims, preferred_element_type=f32)


def halves(x):
    hi = x.astype(bf16)
    return hi, (x - hi.astype(f32)).astype(bf16)


def beside(x):
    return jnp.concatenate(halves(x), axis=1)


def doubled_rows(x):
    both = beside(x)
    return jnp.concatenate([both, both], axis=0)


def doubled_columns(x):
    hi, lo = halves(x)
    return jnp.concatenate([jnp.concatenate([hi, hi], axis=1), jnp.concatenate([lo, lo], axis=1)], axis=0)


def fold(x):
    w = x.shape[1] // 2
    return x[:, :w] + x[:, w:]


def product(a, b):
    return fold(mm(beside(a), doubled_rows(b), NN))


def product_nt(a, b):
    return fold(mm(beside(a), doubled_columns(b), NT))


def product_tn(a, b):
    x = fold(mm(beside(a), beside(b), TN))
    h = x.shape[0] // 2
    return x[:h] + x[h:]


def thirds(x):
    a = x.astype(bf16).astype(f32)
    r = x - a
    b = r.astype(bf16).astype(f32)
    return a, b, r - b


def eliminate(work, tiles, k):
    b = 8
    row = lax.broadcasted_iota(jnp.int32, (b, k), 0)
    for top in range(0, k, b):
        left, right, cols, scale = [], [], [], []
        for t in range(tiles):
            x = work[t, top : top + b, :]
            left.append(x[:, :k])
            right.append(x[:, k:])
            cols.append([jnp.broadcast_to(x[:, top + j : top + j + 1], (b, k)) for j in range(b)])
            scale.append(jnp.zeros((b, k), f32))
        for j in range(b):
            for t in range(tiles):
                pivot = jnp.broadcast_to(cols[t][j][j : j + 1, :], (b, k))
                inverse = 1.0 / pivot
                scale[t] = jnp.where(row == j, inverse, scale[t])
                if j + 1 < b:
                    m = jnp.where(row > j, cols[t][j] * inverse, 0.0)
                    for u in range(j + 1, b):
                        cols[t][u] = cols[t][u] - m * cols[t][u][j : j + 1, :]
                    left[t] = left[t] - m * left[t][j : j + 1, :]
                    right[t] = right[t] - m * right[t][j : j + 1, :]
        for t in range(tiles):
            work[t, top : top + b, k:] = right[t] * jnp.sqrt(scale[t])
        if top + b < k:
            for t in range(tiles):
                p0, p1, p2 = thirds(left[t] * scale[t])
                q0, q1, q2 = thirds(jnp.concatenate([left[t], right[t]], axis=1))
                p = jnp.concatenate([p0, p1, p0, p2, p0, p1], axis=0).astype(bf16)
                q = jnp.concatenate([q0, q0, q1, q0, q2, q1], axis=0).astype(bf16)
                update = mm(p, q, TN)
                work[t, top + b :, :] = work[t, top + b :, :] - update[top + b :, :]


def rows_loop(n, step, body):
    def one(i, carry):
        body(pl.ds(pl.multiple_of(i * step, step), step))
        return carry

    lax.fori_loop(0, n // step, one, 0)


def sketched(u_ref, v_ref, s_ref, out_ref):
    rhs = doubled_rows(product_tn(v_ref[0], s_ref[...]))

    def body(at):
        out_ref[0, at, :] = fold(mm(beside(u_ref[0, at, :]), rhs, NN))

    rows_loop(u_ref.shape[1], 512, body)


def sketch_tiles(tile_u, tile_v, sketch):
    tiles, n, k = tile_u.shape
    block = pl.BlockSpec((1, n, k), lambda i: (i, 0, 0))
    return pl.pallas_call(
        sketched,
        grid=(tiles,),
        in_specs=[block, block, pl.BlockSpec((n, k), lambda i: (0, 0))],
        out_specs=block,
        out_shape=jax.ShapeDtypeStruct(tile_u.shape, f32),
        cost_estimate=pl.CostEstimate(flops=6 * tiles * n * k * k * 2, bytes_accessed=12 * tiles * n * k, transcendentals=0),
        name="sketch_tiles",
    )(tile_u, tile_v, sketch)


def projected(v_ref, s_ref, out_ref):
    out_ref[0] = product_tn(v_ref[0], s_ref[...])


def project(v, sketch):
    tiles, n, k = v.shape
    return pl.pallas_call(
        projected,
        grid=(tiles,),
        in_specs=[pl.BlockSpec((1, n, k), lambda i: (i, 0, 0)), pl.BlockSpec((n, k), lambda i: (0, 0))],
        out_specs=pl.BlockSpec((1, k, k), lambda i: (i, 0, 0)),
        out_shape=jax.ShapeDtypeStruct((tiles, k, k), f32),
        cost_estimate=pl.CostEstimate(flops=6 * tiles * n * k * k, bytes_accessed=4 * tiles * n * k, transcendentals=0),
        name="project",
    )(v, sketch)


def recompress_kernel(tiles, n, k, cores, small, row_u, base, tile_u, tile_v, col_u, new_u, new_v,
                      s, tu, tv, cu, ru, work, cross, back, row_parts, sem):
    root = math.sqrt(n)
    copies = [pltpu.make_async_copy(row_u, ru, sem.at[0])]
    for t in range(tiles):
        copies.append(pltpu.make_async_copy(base.at[t], s.at[t], sem.at[1 + t]))
        copies.append(pltpu.make_async_copy(tile_u.at[t], tu.at[t], sem.at[1 + tiles + t]))
    late = []
    for t in range(tiles):
        late.append(pltpu.make_async_copy(tile_v.at[t], tv.at[t], sem.at[1 + 2 * tiles + t]))
        late.append(pltpu.make_async_copy(col_u.at[t], cu.at[t], sem.at[1 + 3 * tiles + t]))
    for c in copies + late:
        c.start()
    copies[0].wait()

    def split(at):
        row_parts[at, :] = beside(ru[at, :])

    rows_loop(n, 512, split)
    for t in range(tiles):
        copies[1 + 2 * t].wait()
        copies[2 + 2 * t].wait()
        rhs = doubled_rows(-product(cores[t], small[t]))

        def update(at, t=t, rhs=rhs):
            s[t, at, :] = s[t, at, :] + fold(mm(row_parts[at, :], rhs, NN))

        rows_loop(n, 512, update)
        work[t] = jnp.zeros((k, 2 * k), f32)
        cross[t] = jnp.zeros((k, 2 * k), f32)

        def gather(at, t=t):
            part = beside(s[t, at, :])
            x = mm(part, jnp.concatenate([part, beside(tu[t, at, :]), row_parts[at, :]], axis=1), TN)
            x = x[:k] + x[k:]
            work[t, :, :k] += fold(x[:, : 2 * k])
            cross[t, :, :k] += fold(x[:, 2 * k : 4 * k])
            cross[t, :, k:] += fold(x[:, 4 * k :])

        rows_loop(n, 512, gather)
    eye = jnp.where(
        lax.broadcasted_iota(jnp.int32, (k, k), 0) == lax.broadcasted_iota(jnp.int32, (k, k), 1), 1.0, 0.0
    ).astype(f32)
    for t in range(tiles):
        work[t, :, k:] = eye
    eliminate(work, tiles, k)
    outs = []
    for t in range(tiles):
        inverse = work[t, :, k:]
        y = product(inverse, cross[t]) * (1.0 / root)
        c1 = y[:, :k]
        c2 = -product(y[:, k:], cores[t])
        late[2 * t].wait()
        late[2 * t + 1].wait()
        by = doubled_columns(inverse * root)
        c12 = jnp.concatenate([doubled_columns(c1), doubled_columns(c2)], axis=1)

        def finish(at, t=t, by=by, c12=c12):
            s[t, at, :] = fold(mm(beside(s[t, at, :]), by, NT))
            lhs = jnp.concatenate([beside(tv[t, at, :]), beside(cu[t, at, :])], axis=1)
            tv[t, at, :] = fold(mm(lhs, c12, NT))

        rows_loop(n, 512, finish)
        outs.append(pltpu.make_async_copy(s.at[t], new_u.at[t], sem.at[1 + 4 * tiles + t]))
        outs.append(pltpu.make_async_copy(tv.at[t], new_v.at[t], sem.at[1 + 5 * tiles + t]))
        outs[-2].start()
        outs[-1].start()
    for c in outs:
        c.wait()


def recompress(cores, small, row_u, base, tile_u, tile_v, col_u):
    tiles, n, k = tile_u.shape
    any_ = pl.BlockSpec(memory_space=ANY)
    vmem = pl.BlockSpec(memory_space=VMEM)
    full = lambda: VMEM((tiles, n, k), f32)
    return pl.pallas_call(
        functools.partial(recompress_kernel, tiles, n, k),
        in_specs=[vmem, vmem] + [any_] * 5,
        out_specs=[any_, any_],
        out_shape=[jax.ShapeDtypeStruct(tile_u.shape, f32)] * 2,
        scratch_shapes=[
            full(), full(), full(), full(), VMEM((n, k), f32),
            VMEM((tiles, k, 2 * k), f32), VMEM((tiles, k, 2 * k), f32), VMEM((tiles, k, 2 * k), f32),
            VMEM((n, 2 * k), bf16),
            pltpu.SemaphoreType.DMA((1 + 6 * tiles,)),
        ],
        compiler_params=pltpu.CompilerParams(vmem_limit_bytes=40 * 1024 * 1024),
        cost_estimate=pl.CostEstimate(flops=24 * tiles * n * k * k, bytes_accessed=28 * tiles * n * k, transcendentals=0),
        name="recompress",
    )(cores, small, row_u, base, tile_u, tile_v, col_u)


highest = lax.Precision.HIGHEST


def body(tile_u, tile_v, row_panel_u, row_panel_v, col_panel_u, col_panel_v, diag_inverse, sketch):
    first = jnp.einsum(
        "ab,tbk->tak",
        diag_inverse,
        lax.all_gather(row_panel_v, "col", axis=1, tiled=True),
        precision=highest,
    )
    second = jnp.einsum(
        "ab,tbk->tak",
        diag_inverse,
        lax.all_gather(col_panel_v, "col", axis=1, tiled=True),
        precision=highest,
    )
    col_u_rows, col_v_rows = (
        lax.all_gather(col_panel_u, "row", axis=0, tiled=True),
        lax.all_gather(second, "row", axis=0, tiled=True),
    )
    row_u_full = lax.all_gather(row_panel_u, "col", axis=1, tiled=True)
    col_u_full = lax.all_to_all(col_u_rows, "col", split_axis=0, concat_axis=1, tiled=True)
    partial_cores = jnp.einsum("iak,jal->ijkl", first, col_v_rows, precision=highest)
    cores = lax.psum_scatter(partial_cores, "col", scatter_dimension=1, tiled=True)
    base = sketch_tiles(tile_u[0], tile_v[0], sketch)
    small = project(col_u_full, sketch)
    new_u, new_v = recompress(cores[0], small, row_u_full[0], base, tile_u[0], tile_v[0], col_u_full)
    return new_u[None], new_v[None]


def solution(mesh):
    in_specs = (
        P("row", "col", None, None),
        P("row", "col", None, None),
        P("row", "col", None),
        P("row", "col", None),
        P("row", "col", None),
        P("row", "col", None),
        P("col", None),
        P(),
    )
    out_specs = (P("row", "col", None, None), P("row", "col", None, None))
    return jax.shard_map(body, mesh=mesh, in_specs=in_specs, out_specs=out_specs, check_vma=False)
```

time: 442 us -> 302 us (0.68)
  other arithmetic: 89.3 us -> 0 us
  matrix products: 89.2 us -> 19.6 us
  Pallas kernels: 0 us -> 43 us
  local copies, waits for them, and re-layouts: 33.7 us -> 14.2 us
    another operation x7 -> x0, other arithmetic: 86.7 us -> none  [the longest x4 47.3 us: body(): factor = jnp.linalg.cholesky(gram_matrix)]
    dot_general x6 -> x0, matrix products: 60.3 us -> none  [the longest x1 15.5 us: body(): jnp.einsum('ijar,ijrk->ijak', right_side, coefficients, precision=highest)]
    pallas_call x0 -> x3, Pallas kernels: none -> 43 us  [the longest x1 28.6 us: recompress(): pl.pallas_call(functools.partial(recompress_kernel, tiles, n, k), in_spec...]
    all_to_all x1, waiting for transfers between devices: 0.01 us -> 22.6 us  [body(): lax.all_to_all(col_u_rows, 'col', split_axis=0, concat_axis=1, tiled=True)]
    all_gather x1, waiting for transfers between devices: 16.7 us -> 0.01 us  [body(): row_u_full = lax.all_gather(row_panel_u, 'col', axis=1, tiled=True)]
    unnamed x22 -> x12, local copies, waits for them, and re-layouts: 21 us -> 9.69 us
    reduce_scatter x1, waiting for transfers between devices: 28.2 us -> 18.8 us  [body(): lax.psum_scatter(partial_cores, 'col', scatter_dimension=1, tiled=True)]
    broadcast_in_dim x1 -> x0, local copies, waits for them, and re-layouts: 6.05 us -> none  [body(): right_side = jnp.concatenate([tile_v, col_u_full[None]], axis=-1)]
  transfers between devices with their start and end apart: 7 -> 7, of which waited for: 6 -> 6; matrix products, arithmetic and copies ran while one was open for 10% -> 8% of each run, Pallas kernels for 0% -> 5%
where the time goes in v1:
time: 302 us; the launch traced here: 301 us
  waiting for transfers between devices  205 us (68%)
  Pallas kernels  43 us (14%)
  matrix products  19.6 us (6%)
  local copies, waits for them, and re-layouts  14.2 us (5%)
  between operations  14.2 us (5%)
  starting transfers between devices  5.11 us (2%)
    all_gather x1, waiting for transfers between devices, body(): lax.all_gather(row_panel_v, 'col', axis=1, tiled=True)  52.4 us
    all_gather x1, waiting for transfers between devices, body(): lax.all_gather(col_panel_v, 'col', axis=1, tiled=True)  48.5 us
    all_gather x1, waiting for transfers between devices, body(): lax.all_gather(col_panel_u, 'row', axis=0, tiled=True)  30.2 us
    all_gather x1, waiting for transfers between devices, body(): lax.all_gather(second, 'row', axis=0, tiled=True)  30.1 us
    pallas_call x1, Pallas kernels, recompress(): pl.pallas_call(functools.partial(recompress_kernel, tiles, n, k), in_spec...  28.6 us
    all_to_all x1, waiting for transfers between devices, body(): lax.all_to_all(col_u_rows, 'col', split_axis=0, concat_axis=1, tiled=True)  22.6 us
    reduce_scatter x1, waiting for transfers between devices, body(): lax.psum_scatter(partial_cores, 'col', scatter_dimension=1, tiled=True)  18.8 us
    unnamed x12, local copies, waits for them, and re-layouts  9.69 us
  transfers between devices with their start and end apart: 7, of which 6 were waited for; matrix products, arithmetic and copies ran while one was open for 8% of the time, Pallas kernels for 5%

profile of v1, /device:TPU:0, one launch (start us, length us, event | category | flops | bytes accessed | tf_op | source)
XLA Modules:
  0.0 301.3 jit_solution(13319001425025532151)
XLA Ops:
  7.2 0.0 all-gather.6.cloned.1.call-start
  7.2 0.7 all-gather.6.cloned.1.call-update
  7.9 0.0 all-gather.12.cloned.1.call-start
  7.9 0.7 all-gather.12.cloned.1.call-update
  8.6 0.0 all-gather.10.cloned.1.call-start
  8.7 0.7 all-gather.10.cloned.1.call-update
  9.4 0.0 all-gather.8.cloned.1.call-start
  9.4 48.5 %all-gather.6.cloned.1.call-done = f32[2,2048,128]{2,1,0:T(8,128)} async-done(((f32[2,512,128]{2,1,0:T(8,128)}), f32[2,2048,128]{2,1,0:T(8,128)}) %all-gather.6.cloned.1.call-update) | async-done | bytes 2097168 | tf_op jit(solution)/shard_map/all_gather | solution.py:255
  58.0 7.1 %fusion.2 = f32[2,512,128]{2,1,0:T(8,128)} fusion(f32[2,2048,128]{2,1,0:T(8,128)} %all-gather.6.cloned.1.call-done, f32[512,2048]{1,0:T(8,128)} %param.14), kind=kOutput, calls=%fused_computation.3 | convolution fusion | flops 3221225472 | bytes 6815744 | tf_op jit(solution)/shard_map/ab,tbk->tak/dot_general | solution.py:252
  65.1 0.0 all-gather.8.cloned.1.call-update
  65.1 30.2 %all-gather.12.cloned.1.call-done = f32[16,512,128]{2,1,0:T(8,128)} async-done(((f32[2,512,128]{2,1,0:T(8,128)}), f32[16,512,128]{2,1,0:T(8,128)}) %all-gather.12.cloned.1.call-update) | async-done | bytes 4194320 | tf_op jit(solution)/shard_map/all_gather | solution.py:259
  95.3 4.9 %all-to-all-start = ((f32[16,512,128]{2,1,0:T(8,128)}), f32[16,512,128]{2,1,0:T(8,128)}, u32[]{:S(2)}, u32[]{:S(2)}) async-start(f32[16,512,128]{2,1,0:T(8,128)} %all-gather.12.cloned.1.call-done), calls=%async_computation.1 | async-start | bytes 8388608 | tf_op jit(solution)/shard_map/all_to_all | solution.py:263
  100.2 0.0 all-gather.14.cloned.1.call-start
  100.2 0.5 all-gather.14.cloned.1.call-update
  100.7 0.0 reduce-scatter.2.cloned.1.call-start
  100.8 52.4 %all-gather.10.cloned.1.call-done = f32[1,2048,128]{2,1,0:T(8,128)} async-done(((f32[1,512,128]{2,1,0:T(8,128)}), f32[1,2048,128]{2,1,0:T(8,128)}) %all-gather.10.cloned.1.call-update) | async-done | bytes 1048592 | tf_op jit(solution)/shard_map/all_gather | solution.py:249
  153.1 7.0 %convolution_bitcast_fusion.1 = f32[512,128,1]{0,1,2:T(8,128)S(1)} fusion(f32[512,2048]{1,0:T(8,128)} %param.14, f32[1,2048,128]{2,1,0:T(8,128)} %all-gather.10.cloned.1.call-done), kind=kOutput, calls=%fused_computation.4 | convolution fusion | flops 1610612736 | bytes 5505024 | tf_op jit(solution)/shard_map/ab,tbk->tak/dot_general | solution.py:246
  160.1 30.1 %all-gather.8.cloned.1.call-done = f32[16,512,128]{2,1,0:T(8,128)} async-done(((f32[2,512,128]{2,1,0:T(8,128)}), f32[16,512,128]{2,1,0:T(8,128)}) %all-gather.8.cloned.1.call-update) | async-done | bytes 4194320 | tf_op jit(solution)/shard_map/all_gather | solution.py:260
  190.2 5.6 %convolution_bitcast_fusion = f32[1,16,128,128]{3,2,1,0:T(8,128)} fusion(f32[16,512,128]{2,1,0:T(8,128)} %all-gather.8.cloned.1.call-done, f32[512,128,1]{0,1,2:T(8,128)S(1)} %convolution_bitcast_fusion.1), kind=kOutput, calls=%fused_computation.2 | convolution fusion | flops 1610612736 | bytes 5505024 | tf_op jit(solution)/shard_map/iak,jal->ijkl/dot_general | solution.py:264
  195.7 0.0 reduce-scatter.2.cloned.1.call-update
  195.8 9.4 %sketch_tiles.1.base = f32[4,2048,128]{2,1,0:T(8,128)} custom-call(f32[4,2048,128]{2,1,0:T(8,128)} %bitcast.36, f32[4,2048,128]{2,1,0:T(8,128)} %bitcast.38, f32[2048,128]{1,0:T(8,128)} %s_ref.3), custom_call_target="tpu_custom_call" | custom-call | flops 1610612736 | bytes 12582912 | tf_op jit(solution)/shard_map/sketch_tiles/pallas_call | solution.py:121
  205.2 22.6 %all-to-all-done = f32[16,512,128]{2,1,0:T(8,128)} async-done(((f32[16,512,128]{2,1,0:T(8,128)}), f32[16,512,128]{2,1,0:T(8,128)}, u32[]{:S(2)}, u32[]{:S(2)}) %all-to-all-start) | async-done | bytes 4194336 | tf_op jit(solution)/shard_map/all_to_all | solution.py:263
  227.8 4.5 %copy.16 = f32[4,4,512,128]{3,2,0,1:T(8,128)} copy(f32[4,4,512,128]{3,2,1,0:T(8,128)} %bitcast.10) | data formatting | bytes 8388608 | tf_op jit(solution)/shard_map/all_to_all | solution.py:263
  232.3 5.1 %project.1.small = f32[4,128,128]{2,1,0:T(8,128)} custom-call(f32[4,2048,128]{2,1,0:T(8,128)} %bitcast.42, f32[2048,128]{1,0:T(8,128)} %s_ref.3), custom_call_target="tpu_custom_call" | custom-call | flops 805306368 | bytes 4194304 | tf_op jit(solution)/shard_map/project/pallas_call | solution.py:138
  237.4 0.0 all-gather.14.cloned.1.call-done
  237.4 18.8 %reduce-scatter.2.cloned.1.call-done = f32[1,4,128,128]{3,2,1,0:T(8,128)} async-done(((f32[1,16,128,128]{3,2,1,0:T(8,128)}), f32[1,4,128,128]{3,2,1,0:T(8,128)}) %reduce-scatter.2.cloned.1.call-update) | async-done | bytes 262160 | tf_op jit(solution)/shard_map/reduce_scatter | solution.py:265
  256.2 0.0 copy-start
  256.2 2.2 copy-done
  258.4 0.0 copy-start.1
  258.4 2.2 copy-done.1
  260.6 0.0 copy-start.2
  260.6 2.2 copy-done.2
  262.7 0.0 copy-start.3
  262.7 0.9 copy-done.3
  263.7 0.0 copy-start.4
  263.7 1.2 copy-done.4
  264.9 0.0 copy-start.5
  264.9 0.9 copy-done.5
  265.9 28.6 %recompress.1 = (f32[4,2048,128]{2,1,0:T(8,128)}, f32[4,2048,128]{2,1,0:T(8,128)}) custom-call(f32[4,128,128]{2,1,0:T(8,128)S(1)} %bitcast.41, f32[4,128,128]{2,1,0:T(8,128)S(1)} %copy-done.3, f32[2048,128]{1,0:T(8,128)S(1)} %bitcast.40, f32[4,2048,128]{2,1,0:T(8,128)S(1)} %copy-done.2, f32[4,2048,128]{2,1,0:T(8,128)S(1)} %bitcast.37, ...), custom_call_target="tpu_custom_call" | custom-call | flops 3221225472 | bytes 29360128 | tf_op jit(solution)/shard_map/recompress/pallas_call | solution.py:225
Async XLA Ops:
  7.2 50.8 %all-gather.6.cloned.1.call-start = ((), (), s32[]{:S(2)}) async-start(), calls=%async_computation.2 | async-start | bytes 2621440 | tf_op jit(solution)/shard_map/all_gather | solution.py:255
  7.9 87.4 %all-gather.12.cloned.1.call-start = ((), (), s32[]{:S(2)}) async-start(), calls=%async_computation.6 | async-start | bytes 4718592 | tf_op jit(solution)/shard_map/all_gather | solution.py:259
  8.6 144.5 %all-gather.10.cloned.1.call-start = ((), (), s32[]{:S(2)}) async-start(), calls=%async_computation.4 | async-start | bytes 1310720 | tf_op jit(solution)/shard_map/all_gather | solution.py:249
  9.4 180.8 %all-gather.8.cloned.1.call-start = ((), (), s32[]{:S(2)}) async-start(), calls=%async_computation.3 | async-start | bytes 4718592 | tf_op jit(solution)/shard_map/all_gather | solution.py:260
  95.3 132.5 %all-to-all-start = ((f32[16,512,128]{2,1,0:T(8,128)}), f32[16,512,128]{2,1,0:T(8,128)}, u32[]{:S(2)}, u32[]{:S(2)}) async-start(f32[16,512,128]{2,1,0:T(8,128)} %all-gather.12.cloned.1.call-done), calls=%async_computation.1 | async-start | bytes 8388608 | tf_op jit(solution)/shard_map/all_to_all | solution.py:263
  100.2 137.3 %all-gather.14.cloned.1.call-start = ((), (), s32[]{:S(2)}) async-start(), calls=%async_computation.7 | async-start | bytes 1310720 | tf_op jit(solution)/shard_map/all_gather | solution.py:262
  100.7 155.4 %reduce-scatter.2.cloned.1.call-start = ((), (), s32[]{:S(2)}) async-start(), calls=%async_computation.5 | async-start | bytes 1310720 | tf_op jit(solution)/shard_map/reduce_scatter | solution.py:265
  256.2 2.2 copy-start
  258.4 2.2 copy-start.1
  260.6 2.2 copy-start.2
  262.7 0.9 copy-start.3
  263.7 1.2 copy-start.4
  264.9 0.9 copy-start.5
Sparse Core Ops, SparseCore 0:
  9.5 48.3 all-gather.5
  59.8 35.3 all-gather.11
  96.8 56.2 all-gather.9
  155.5 34.6 all-gather.7
  191.6 36.3 all-gather.13
  230.7 25.4 reduce-scatter.1

commit v2 on v1

--- a/solution.py
+++ b/solution.py
@@ -45,10 +45,6 @@
 
 def product(a, b):
     return fold(mm(beside(a), doubled_rows(b), NN))
-
-
-def product_nt(a, b):
-    return fold(mm(beside(a), doubled_columns(b), NT))
 
 
 def product_tn(a, b):
@@ -129,45 +125,133 @@
     )(tile_u, tile_v, sketch)
 
 
-def projected(v_ref, s_ref, out_ref):
-    out_ref[0] = product_tn(v_ref[0], s_ref[...])
-
-
-def project(v, sketch):
-    tiles, n, k = v.shape
-    return pl.pallas_call(
-        projected,
-        grid=(tiles,),
-        in_specs=[pl.BlockSpec((1, n, k), lambda i: (i, 0, 0)), pl.BlockSpec((n, k), lambda i: (0, 0))],
-        out_specs=pl.BlockSpec((1, k, k), lambda i: (i, 0, 0)),
-        out_shape=jax.ShapeDtypeStruct((tiles, k, k), f32),
-        cost_estimate=pl.CostEstimate(flops=6 * tiles * n * k * k, bytes_accessed=4 * tiles * n * k, transcendentals=0),
+def block_of(c, d, n):
+    return lax.rem(c - d + n, n)
+
+
+def project_kernel(n_col, at, mine, other, s_ref, full, small):
+    r, c = at[0], at[1]
+    chip, core = lax.shift_right_logical(r, 1), lax.rem(r, 2)
+    chips, _, pair, piece, _ = mine.shape
+    for src, parity in ((mine, core), (other, 1 - core)):
+        for e in range(chips):
+            for d in range(n_col):
+                start = block_of(c, d, n_col) * (chips * piece) + (chip ^ e) * piece
+                rows = pl.ds(pl.multiple_of(start, piece), piece)
+                for t in range(pair):
+                    full[parity * pair + t, rows, :] = src[e, d, t]
+    for j in range(full.shape[0]):
+        small[j] = product_tn(full[j], s_ref[...])
+
+
+def project(n_col, at, mine, other, sketch):
+    chips, _, pair, piece, k = mine.shape
+    tiles, n = 2 * pair, chips * n_col * piece
+    vmem = pl.BlockSpec(memory_space=VMEM)
+    return pl.pallas_call(
+        functools.partial(project_kernel, n_col),
+        in_specs=[pl.BlockSpec(memory_space=pltpu.SMEM)] + [vmem] * 3,
+        out_specs=[vmem] * 2,
+        out_shape=[jax.ShapeDtypeStruct((tiles, n, k), f32), jax.ShapeDtypeStruct((tiles, k, k), f32)],
+        cost_estimate=pl.CostEstimate(flops=6 * tiles * n * k * k, bytes_accessed=8 * tiles * n * k, transcendentals=0),
         name="project",
-    )(v, sketch)
-
-
-def recompress_kernel(tiles, n, k, cores, small, row_u, base, tile_u, tile_v, col_u, new_u, new_v,
-                      s, tu, tv, cu, ru, work, cross, back, row_parts, sem):
+    )(at, mine, other, sketch)
+
+
+def solve_kernel(n_col, at, diag, *refs):
+    xs, outs = refs[:n_col], refs[n_col:]
+    c = at[1]
+    rows = diag.shape[0]
+    solved = None
+    for d in range(n_col):
+        cols = pl.ds(pl.multiple_of(jnp.maximum(c - d, 0) * rows, rows), rows)
+        part = product(diag[:, cols], xs[d][...])
+        solved = part if solved is None else solved + part
+    for d in range(n_col):
+        cols = pl.ds(pl.multiple_of(jnp.maximum(c - d, 0) * rows, rows), rows)
+        outs[d][...] = product_tn(solved, diag[:, cols])
+
+
+def solve(at, diag, xs):
+    n_col = len(xs)
+    rows, k = xs[0].shape
+    vmem = pl.BlockSpec(memory_space=VMEM)
+    return pl.pallas_call(
+        functools.partial(solve_kernel, n_col),
+        in_specs=[pl.BlockSpec(memory_space=pltpu.SMEM)] + [vmem] * (1 + n_col),
+        out_specs=[vmem] * n_col,
+        out_shape=[jax.ShapeDtypeStruct((k, rows), f32)] * n_col,
+        cost_estimate=pl.CostEstimate(flops=12 * n_col * rows * rows * k, bytes_accessed=4 * n_col * rows * rows, transcendentals=0),
+        name="solve",
+    )(at, diag, *xs)
+
+
+def cores_kernel(n_col, at, *refs):
+    parts, (mine, other), outs = refs[:n_col], refs[n_col : n_col + 2], refs[n_col + 2 :]
+    r, c = at[0], at[1]
+    chip, core = lax.shift_right_logical(r, 1), lax.rem(r, 2)
+    total = parts[0][...]
+    for p in parts[1:]:
+        total = total + p[...]
+    lhs = beside(total)
+    pair = mine.shape[1]
+    for d in range(n_col):
+        e = chip ^ lax.rem(c + d, n_col)
+        for src, parity in ((mine, core), (other, 1 - core)):
+            for t in range(pair):
+                outs[d][parity * pair + t] = fold(mm(lhs, doubled_rows(src[e, t]), NN))
+
+
+def partial_cores(at, parts, mine, other):
+    n_col = len(parts)
+    k, rows = parts[0].shape
+    pair = mine.shape[1]
+    vmem = pl.BlockSpec(memory_space=VMEM)
+    return pl.pallas_call(
+        functools.partial(cores_kernel, n_col),
+        in_specs=[pl.BlockSpec(memory_space=pltpu.SMEM)] + [vmem] * (n_col + 2),
+        out_specs=[vmem] * n_col,
+        out_shape=[jax.ShapeDtypeStruct((2 * pair, k, k), f32)] * n_col,
+        cost_estimate=pl.CostEstimate(flops=12 * n_col * pair * rows * k * k, bytes_accessed=8 * n_col * pair * rows * k, transcendentals=0),
+        name="partial_cores",
+    )(at, *parts, mine, other)
+
+
+def recompress_kernel(tiles, n, k, n_col, at, *refs):
+    core_parts, row_us = refs[:n_col], refs[n_col : 2 * n_col]
+    small, base, tile_u, tile_v, col_u, new_u, new_v = refs[2 * n_col : 2 * n_col + 7]
+    s, tu, tv, cu, ru, work, cross, cores, row_parts, sem, row_sem = refs[2 * n_col + 7 :]
+    c = at[1]
     root = math.sqrt(n)
-    copies = [pltpu.make_async_copy(row_u, ru, sem.at[0])]
-    for t in range(tiles):
-        copies.append(pltpu.make_async_copy(base.at[t], s.at[t], sem.at[1 + t]))
-        copies.append(pltpu.make_async_copy(tile_u.at[t], tu.at[t], sem.at[1 + tiles + t]))
+    blk = n // n_col
+    row_copies = []
+    for d in range(n_col):
+        rows = pl.ds(pl.multiple_of(block_of(c, d, n_col) * blk, blk), blk)
+        row_copies.append(pltpu.make_async_copy(row_us[d], ru.at[rows], row_sem.at[d]))
+    copies = []
+    for t in range(tiles):
+        copies.append(pltpu.make_async_copy(base.at[t], s.at[t], sem.at[t]))
+        copies.append(pltpu.make_async_copy(tile_u.at[t], tu.at[t], sem.at[tiles + t]))
     late = []
     for t in range(tiles):
-        late.append(pltpu.make_async_copy(tile_v.at[t], tv.at[t], sem.at[1 + 2 * tiles + t]))
-        late.append(pltpu.make_async_copy(col_u.at[t], cu.at[t], sem.at[1 + 3 * tiles + t]))
-    for c in copies + late:
-        c.start()
-    copies[0].wait()
+        late.append(pltpu.make_async_copy(tile_v.at[t], tv.at[t], sem.at[2 * tiles + t]))
+        late.append(pltpu.make_async_copy(col_u.at[t], cu.at[t], sem.at[3 * tiles + t]))
+    for x in row_copies + copies + late:
+        x.start()
+    total = core_parts[0][...]
+    for p in core_parts[1:]:
+        total = total + p[...]
+    cores[...] = total
+    for x in row_copies:
+        x.wait()
 
     def split(at):
         row_parts[at, :] = beside(ru[at, :])
 
     rows_loop(n, 512, split)
     for t in range(tiles):
-        copies[1 + 2 * t].wait()
-        copies[2 + 2 * t].wait()
+        copies[2 * t].wait()
+        copies[2 * t + 1].wait()
         rhs = doubled_rows(-product(cores[t], small[t]))
 
         def update(at, t=t, rhs=rhs):
@@ -209,67 +293,87 @@
             tv[t, at, :] = fold(mm(lhs, c12, NT))
 
         rows_loop(n, 512, finish)
-        outs.append(pltpu.make_async_copy(s.at[t], new_u.at[t], sem.at[1 + 4 * tiles + t]))
-        outs.append(pltpu.make_async_copy(tv.at[t], new_v.at[t], sem.at[1 + 5 * tiles + t]))
+        outs.append(pltpu.make_async_copy(s.at[t], new_u.at[t], sem.at[4 * tiles + t]))
+        outs.append(pltpu.make_async_copy(tv.at[t], new_v.at[t], sem.at[5 * tiles + t]))
         outs[-2].start()
         outs[-1].start()
-    for c in outs:
-        c.wait()
-
-
-def recompress(cores, small, row_u, base, tile_u, tile_v, col_u):
+    for x in outs:
+        x.wait()
+
+
+def recompress(at, core_parts, row_us, small, base, tile_u, tile_v, col_u):
     tiles, n, k = tile_u.shape
+    n_col = len(core_parts)
     any_ = pl.BlockSpec(memory_space=ANY)
     vmem = pl.BlockSpec(memory_space=VMEM)
     full = lambda: VMEM((tiles, n, k), f32)
     return pl.pallas_call(
-        functools.partial(recompress_kernel, tiles, n, k),
-        in_specs=[vmem, vmem] + [any_] * 5,
+        functools.partial(recompress_kernel, tiles, n, k, n_col),
+        in_specs=[pl.BlockSpec(memory_space=pltpu.SMEM)] + [vmem] * n_col + [any_] * n_col + [vmem] + [any_] * 4,
         out_specs=[any_, any_],
         out_shape=[jax.ShapeDtypeStruct(tile_u.shape, f32)] * 2,
         scratch_shapes=[
             full(), full(), full(), full(), VMEM((n, k), f32),
-            VMEM((tiles, k, 2 * k), f32), VMEM((tiles, k, 2 * k), f32), VMEM((tiles, k, 2 * k), f32),
+            VMEM((tiles, k, 2 * k), f32), VMEM((tiles, k, 2 * k), f32), VMEM((tiles, k, k), f32),
             VMEM((n, 2 * k), bf16),
-            pltpu.SemaphoreType.DMA((1 + 6 * tiles,)),
+            pltpu.SemaphoreType.DMA((6 * tiles,)), pltpu.SemaphoreType.DMA((n_col,)),
         ],
-        compiler_params=pltpu.CompilerParams(vmem_limit_bytes=40 * 1024 * 1024),
         cost_estimate=pl.CostEstimate(flops=24 * tiles * n * k * k, bytes_accessed=28 * tiles * n * k, transcendentals=0),
         name="recompress",
-    )(cores, small, row_u, base, tile_u, tile_v, col_u)
-
-
-highest = lax.Precision.HIGHEST
-
-
-def body(tile_u, tile_v, row_panel_u, row_panel_v, col_panel_u, col_panel_v, diag_inverse, sketch):
-    first = jnp.einsum(
-        "ab,tbk->tak",
-        diag_inverse,
-        lax.all_gather(row_panel_v, "col", axis=1, tiled=True),
-        precision=highest,
+    )(at, *core_parts, *row_us, small, base, tile_u, tile_v, col_u)
+
+
+def step(n_row, n_col, tile_u, tile_v, row_panel_u, row_panel_v, col_panel_u, col_panel_v, diag_inverse, sketch):
+    chips = n_row // 2
+    r, c = lax.axis_index("row"), lax.axis_index("col")
+    at = jnp.stack([r, c]).astype(jnp.int32)
+    chip = lax.shift_right_logical(r, 1)
+
+    def partner(x, m):
+        return lax.ppermute(x, "row", [(a, a ^ m) for a in range(n_row)])
+
+    def shift(x, pairs):
+        return lax.ppermute(x, "col", pairs)
+
+    def up(x, d):
+        return shift(x, [(a, a + d) for a in range(n_col - d)])
+
+    def down(x, d):
+        return shift(x, [(a, a - d) for a in range(d, n_col)])
+
+    def around(x, d):
+        return shift(x, [(a, (a + d) % n_col) for a in range(n_col)])
+
+    def pick(x, i, axis=0):
+        return lax.dynamic_index_in_dim(x, i, axis, keepdims=False)
+
+    row_v = row_panel_v[0]
+    below = [row_v] + [up(row_v, d) for d in range(1, n_col)]
+    col_v_mine = jnp.stack([col_panel_v] + [partner(col_panel_v, 2 * e) for e in range(1, chips)])
+    row_u = row_panel_u[0]
+    row_us = [row_u] + [around(row_u, d) for d in range(1, n_col)]
+    pair, rows, k = col_panel_u.shape
+    cut = col_panel_u.reshape(pair, chips, rows // chips, k)
+    cuts = jnp.stack([pick(cut, chip, 1)] + [partner(pick(cut, chip ^ e, 1), 2 * e) for e in range(1, chips)])
+    col_v_other = partner(col_v_mine, 1)
+    planes = jnp.stack(
+        [pick(cuts, chip ^ c)] + [around(pick(cuts, chip ^ lax.rem(c + d, n_col)), d) for d in range(1, n_col)]
     )
-    second = jnp.einsum(
-        "ab,tbk->tak",
-        diag_inverse,
-        lax.all_gather(col_panel_v, "col", axis=1, tiled=True),
-        precision=highest,
-    )
-    col_u_rows, col_v_rows = (
-        lax.all_gather(col_panel_u, "row", axis=0, tiled=True),
-        lax.all_gather(second, "row", axis=0, tiled=True),
-    )
-    row_u_full = lax.all_gather(row_panel_u, "col", axis=1, tiled=True)
-    col_u_full = lax.all_to_all(col_u_rows, "col", split_axis=0, concat_axis=1, tiled=True)
-    partial_cores = jnp.einsum("iak,jal->ijkl", first, col_v_rows, precision=highest)
-    cores = lax.psum_scatter(partial_cores, "col", scatter_dimension=1, tiled=True)
     base = sketch_tiles(tile_u[0], tile_v[0], sketch)
-    small = project(col_u_full, sketch)
-    new_u, new_v = recompress(cores[0], small, row_u_full[0], base, tile_u[0], tile_v[0], col_u_full)
+    sums = solve(at, diag_inverse, below)
+    parts = [sums[0]] + [down(sums[d], d) for d in range(1, n_col)]
+    gathered = [planes] + [partner(planes, 2 * e) for e in range(1, chips)]
+    col_u_mine = jnp.stack(gathered)
+    col_u_other = partner(col_u_mine, 1)
+    col_u, small = project(n_col, at, col_u_mine, col_u_other, sketch)
+    cores = partial_cores(at, parts, col_v_mine, col_v_other)
+    core_parts = [cores[0]] + [around(cores[d], d) for d in range(1, n_col)]
+    new_u, new_v = recompress(at, core_parts, row_us, small, base, tile_u[0], tile_v[0], col_u)
     return new_u[None], new_v[None]
 
 
 def solution(mesh):
+    n_row, n_col = mesh.shape["row"], mesh.shape["col"]
     in_specs = (
         P("row", "col", None, None),
         P("row", "col", None, None),
@@ -281,4 +385,8 @@
         P(),
     )
     out_specs = (P("row", "col", None, None), P("row", "col", None, None))
+
+    def body(*args):
+        return step(n_row, n_col, *args)
+
     return jax.shard_map(body, mesh=mesh, in_specs=in_specs, out_specs=out_specs, check_vma=False)

time: 302 us -> 208 us (0.69)
  waiting for transfers between devices: 205 us -> 82.6 us
  starting transfers between devices: 5.11 us -> 56.8 us
  matrix products: 19.6 us -> 0 us
  Pallas kernels: 43 us -> 58.9 us
  between operations: 14.2 us -> 1.03 us
  local copies, waits for them, and re-layouts: 14.2 us -> 3.54 us
    all_gather x5 -> x0, waiting for transfers between devices: 161 us -> none  [the longest x1 52.4 us: body(): lax.all_gather(row_panel_v, 'col', axis=1, tiled=True)]
    ppermute x0 -> x26, waiting for transfers between devices: none -> 82.6 us  [the longest x15 45.5 us: shift(): return lax.ppermute(x, 'col', pairs)]
    ppermute x0 -> x26, starting transfers between devices: none -> 56.8 us  [the longest x15 42.3 us: shift(): return lax.ppermute(x, 'col', pairs)]
    all_to_all x1 -> x0, waiting for transfers between devices: 22.6 us -> none  [body(): lax.all_to_all(col_u_rows, 'col', split_axis=0, concat_axis=1, tiled=True)]
    dot_general x3 -> x0, matrix products: 19.6 us -> none  [the longest x1 7.12 us: body(): jnp.einsum('ab,tbk->tak', diag_inverse, lax.all_gather(col_panel_v, 'col'...]
    reduce_scatter x1 -> x0, waiting for transfers between devices: 18.8 us -> none  [body(): lax.psum_scatter(partial_cores, 'col', scatter_dimension=1, tiled=True)]
    pallas_call x2 -> x4, Pallas kernels: 33.6 us -> 49.7 us  [the longest x1 34.7 us: recompress(): pl.pallas_call(functools.partial(recompress_kernel, tiles, n, k, n_col),...]
    unnamed x12 -> x26, local copies, waits for them, and re-layouts: 9.69 us -> 2.3 us
  transfers between devices with their start and end apart: 7 -> 26, of which waited for: 6 -> 11; matrix products, arithmetic and copies ran while one was open for 8% -> 1% of each run, Pallas kernels for 5% -> 12%
where the time goes in v2:
time: 208 us; the launch traced here: 205 us
  waiting for transfers between devices  82.6 us (40%)
  Pallas kernels  58.9 us (28%)
  starting transfers between devices  56.8 us (27%)
  local copies, waits for them, and re-layouts  3.54 us (2%)
  other arithmetic  2.4 us (1%)
    ppermute x15, waiting for transfers between devices, shift(): return lax.ppermute(x, 'col', pairs)  45.5 us
    ppermute x15, starting transfers between devices, shift(): return lax.ppermute(x, 'col', pairs)  42.3 us
    ppermute x11, waiting for transfers between devices, partner(): return lax.ppermute(x, 'row', [(a, a ^ m) for a in range(n_row)])  37.1 us
    pallas_call x1, Pallas kernels, recompress(): pl.pallas_call(functools.partial(recompress_kernel, tiles, n, k, n_col),...  34.7 us
    ppermute x11, starting transfers between devices, partner(): return lax.ppermute(x, 'row', [(a, a ^ m) for a in range(n_row)])  14.5 us
    pallas_call x1, Pallas kernels, sketch_tiles(): pl.pallas_call(sketched, grid=(tiles,), in_specs=[block, block, pl.BlockS...  9.28 us
    pallas_call x1, Pallas kernels, solve(): pl.pallas_call(functools.partial(solve_kernel, n_col), in_specs=[pl.Block...  5.6 us
    pallas_call x1, Pallas kernels, project(): pl.pallas_call(functools.partial(project_kernel, n_col), in_specs=[pl.Blo...  4.81 us
  transfers between devices with their start and end apart: 26, of which 11 were waited for; matrix products, arithmetic and copies ran while one was open for 1% of the time, Pallas kernels for 12%

profile of v2, /device:TPU:0, one launch (start us, length us, event | category | flops | bytes accessed | tf_op | source)
XLA Modules:
  0.0 205.4 jit_solution(4357624686524864041)
XLA Ops:
  0.6 0.0 copy-start.1
  0.7 1.2 dynamic-slice_bitcast_fusion.6
  1.9 3.1 %collective-permute-start.17 = (f32[2,128,128]{2,1,0:T(8,128)S(1)}, f32[2,128,128]{2,1,0:T(8,128)S(1)}, u32[]{:S(2)}, u32[]{:S(2)}) collective-permute-start(f32[2,128,128]{2,1,0:T(8,128)S(1)} %get-tuple-element.33), channel_id=1, source_target_pairs={{0,16},{4,20},{8,24},{12,28},{16,0},{20,4},{24,8},{28,12},{1,17},{... | collective-permute-start | bytes 393224 | tf_op jit(solution)/shard_map/ppermute | solution.py:333
  4.9 1.5 collective-permute-start.16
  6.4 0.0 collective-permute-start.18
  6.5 1.9 collective-permute-start.6
  8.4 0.0 collective-permute-done.17
  8.4 2.9 %collective-permute-done.16 = f32[2,128,128]{2,1,0:T(8,128)S(1)} collective-permute-done((f32[2,128,128]{2,1,0:T(8,128)S(1)}, f32[2,128,128]{2,1,0:T(8,128)S(1)}, u32[]{:S(2)}, u32[]{:S(2)}) %collective-permute-start.16) | collective-permute-done | bytes 131104 | tf_op jit(solution)/shard_map/ppermute | solution.py:333
  11.3 2.4 %collective-permute-done.18 = f32[2,128,128]{2,1,0:T(8,128)S(1)} collective-permute-done((f32[2,128,128]{2,1,0:T(8,128)S(1)}, f32[2,128,128]{2,1,0:T(8,128)S(1)}, u32[]{:S(2)}, u32[]{:S(2)}) %collective-permute-start.18) | collective-permute-done | bytes 131104 | tf_op jit(solution)/shard_map/ppermute | solution.py:333
  13.8 3.7 %collective-permute-start.21 = (f32[2,128,128]{2,1,0:T(8,128)S(1)}, f32[2,128,128]{2,1,0:T(8,128)S(1)}, u32[]{:S(2)}, u32[]{:S(2)}) collective-permute-start(f32[2,128,128]{2,1,0:T(8,128)S(1)} %get-tuple-element.29), channel_id=1, source_target_pairs={{0,3},{1,0},{2,1},{3,2},{4,7},{5,4},{6,5},{7,6},{8,11},{9,8},{10,9... | collective-permute-start | bytes 393224 | tf_op jit(solution)/shard_map/ppermute | solution.py:336
  17.4 0.0 collective-permute-start.20
  17.4 1.0 collective-permute-start.19
  18.5 2.8 %collective-permute-start.8 = (f32[2,512,128]{2,1,0:T(8,128)S(1)}, f32[2,512,128]{2,1,0:T(8,128)S(1)}, u32[]{:S(2)}, u32[]{:S(2)}) collective-permute-start(f32[2,512,128]{2,1,0:T(8,128)S(1)} %copy-done.1), channel_id=1, source_target_pairs={{0,24},{4,28},{8,16},{12,20},{16,8},{20,12},{24,0},{28,4},{1,25},{... | collective-permute-start | bytes 1572872 | tf_op jit(solution)/shard_map/ppermute | solution.py:333
  21.3 0.0 collective-permute-done.21
  21.3 1.5 collective-permute-start.7
  22.8 4.9 %collective-permute-done.20 = f32[2,128,128]{2,1,0:T(8,128)S(1)} collective-permute-done((f32[2,128,128]{2,1,0:T(8,128)S(1)}, f32[2,128,128]{2,1,0:T(8,128)S(1)}, u32[]{:S(2)}, u32[]{:S(2)}) %collective-permute-start.20) | collective-permute-done | bytes 131104 | tf_op jit(solution)/shard_map/ppermute | solution.py:336
  27.7 0.0 collective-permute-done.19
  27.7 0.1 fusion
  27.8 0.9 collective-permute-start.23
  28.7 1.5 collective-permute-start.22
  30.2 0.0 collective-permute-done.6
  30.2 1.2 collective-permute-start.24
  31.4 4.8 %collective-permute-done.8 = f32[2,512,128]{2,1,0:T(8,128)S(1)} collective-permute-done((f32[2,512,128]{2,1,0:T(8,128)S(1)}, f32[2,512,128]{2,1,0:T(8,128)S(1)}, u32[]{:S(2)}, u32[]{:S(2)}) %collective-permute-start.8) | collective-permute-done | bytes 524320 | tf_op jit(solution)/shard_map/ppermute | solution.py:333
  36.2 11.0 %collective-permute-done.7 = f32[2,512,128]{2,1,0:T(8,128)S(1)} collective-permute-done((f32[2,512,128]{2,1,0:T(8,128)S(1)}, f32[2,512,128]{2,1,0:T(8,128)S(1)}, u32[]{:S(2)}, u32[]{:S(2)}) %collective-permute-start.7) | collective-permute-done | bytes 524320 | tf_op jit(solution)/shard_map/ppermute | solution.py:333
  47.2 1.5 pad_maximum_fusion.refs_4_
  48.7 0.0 collective-permute-start.9
  48.7 16.0 %collective-permute-done.23 = f32[4,2,128,128]{3,2,1,0:T(8,128)S(1)} collective-permute-done((f32[4,2,128,128]{3,2,1,0:T(8,128)S(1)}, f32[4,2,128,128]{3,2,1,0:T(8,128)S(1)}, u32[]{:S(2)}, u32[]{:S(2)}) %collective-permute-start.23) | collective-permute-done | bytes 524320 | tf_op jit(solution)/shard_map/ppermute | solution.py:333
  64.7 0.0 collective-permute-done.22
  64.7 0.0 collective-permute-done.24
  64.7 0.2 pad_maximum_fusion.1.mine
  64.9 0.0 copy-start
  64.9 0.1 collective-permute-start.25
  65.0 0.6 copy-done.9
  65.6 6.0 %collective-permute-start.2 = (f32[512,128]{1,0:T(8,128)S(1)}, f32[512,128]{1,0:T(8,128)S(1)}, u32[]{:S(2)}, u32[]{:S(2)}) collective-permute-start(f32[512,128]{1,0:T(8,128)S(1)} %bitcast.71), channel_id=1, source_target_pairs={{0,3},{4,7},{8,11},{12,15},{16,19},{20,23},{24,27},{28,31}} | collective-permute-start | bytes 786440 | tf_op jit(solution)/shard_map/ppermute | solution.py:336
  71.7 1.3 collective-permute-start.1
  73.0 2.5 %collective-permute-start = (f32[512,128]{1,0:T(8,128)S(1)}, f32[512,128]{1,0:T(8,128)S(1)}, u32[]{:S(2)}, u32[]{:S(2)}) collective-permute-start(f32[512,128]{1,0:T(8,128)S(1)} %bitcast.73), channel_id=1, source_target_pairs={{0,1},{1,2},{2,3},{4,5},{5,6},{6,7},{8,9},{9,10},{10,11},{12,13},{... | collective-permute-start | bytes 786440 | tf_op jit(solution)/shard_map/ppermute | solution.py:336
  75.5 0.6 pad_add_fusion.at
  76.1 2.4 %collective-permute-done.2.refs_3_ = f32[512,128]{1,0:T(8,128)S(1)} collective-permute-done((f32[512,128]{1,0:T(8,128)S(1)}, f32[512,128]{1,0:T(8,128)S(1)}, u32[]{:S(2)}, u32[]{:S(2)}) %collective-permute-start.2) | collective-permute-done | bytes 262176 | tf_op jit(solution)/shard_map/ppermute | solution.py:336
  78.4 5.6 %collective-permute-done.1.refs_2_ = f32[512,128]{1,0:T(8,128)S(1)} collective-permute-done((f32[512,128]{1,0:T(8,128)S(1)}, f32[512,128]{1,0:T(8,128)S(1)}, u32[]{:S(2)}, u32[]{:S(2)}) %collective-permute-start.1) | collective-permute-done | bytes 262176 | tf_op jit(solution)/shard_map/ppermute | solution.py:336
  84.1 4.5 %collective-permute-done.refs_1_ = f32[512,128]{1,0:T(8,128)S(1)} collective-permute-done((f32[512,128]{1,0:T(8,128)S(1)}, f32[512,128]{1,0:T(8,128)S(1)}, u32[]{:S(2)}, u32[]{:S(2)}) %collective-permute-start) | collective-permute-done | bytes 262176 | tf_op jit(solution)/shard_map/ppermute | solution.py:336
  88.6 0.7 copy-done.12
  89.3 5.6 %solve.1 = (f32[128,512]{1,0:T(8,128)}, f32[128,512]{1,0:T(8,128)}, f32[128,512]{1,0:T(8,128)}, f32[128,512]{1,0:T(8,128)}) custom-call(s32[2]{0:T(128)} %pad_add_fusion.at, f32[512,2048]{1,0:T(8,128)} %diag.1, f32[512,128]{1,0:T(8,128)} %bitcast.70, f32[512,128]{1,0:T(8,128)} %copy-done.12, f32[512,128]{1,0:T(8,128)} %copy-done.11, f32[512,128]{1,0:T(8,128)} %copy-done.10), custom_call_target="tpu_custom_call" | custom-call | flops 1610612736 | bytes 4194304 | tf_op jit(solution)/shard_map/solve/pallas_call | solution.py:179
  94.9 1.3 collective-permute-start.3
  96.2 1.3 collective-permute-start.4
  97.5 1.3 collective-permute-start.5
  98.8 11.7 %collective-permute-done.3.refs_1_ = f32[128,512]{1,0:T(8,128)S(1)} collective-permute-done((f32[128,512]{1,0:T(8,128)}, f32[128,512]{1,0:T(8,128)S(1)}, u32[]{:S(2)}, u32[]{:S(2)}) %collective-permute-start.3) | collective-permute-done | bytes 262176 | tf_op jit(solution)/shard_map/ppermute | solution.py:336
  110.5 3.7 %collective-permute-start.15 = (f32[512,128]{1,0:T(8,128)S(1)}, f32[512,128]{1,0:T(8,128)S(1)}, u32[]{:S(2)}, u32[]{:S(2)}) collective-permute-start(f32[512,128]{1,0:T(8,128)S(1)} %bitcast.59), channel_id=1, source_target_pairs={{0,3},{1,0},{2,1},{3,2},{4,7},{5,4},{6,5},{7,6},{8,11},{9,8},{10,9... | collective-permute-start | bytes 786440 | tf_op jit(solution)/shard_map/ppermute | solution.py:336
  114.2 16.3 %collective-permute-done.4.refs_2_ = f32[128,512]{1,0:T(8,128)} collective-permute-done((f32[128,512]{1,0:T(8,128)}, f32[128,512]{1,0:T(8,128)}, u32[]{:S(2)}, u32[]{:S(2)}) %collective-permute-start.4) | collective-permute-done | bytes 262176 | tf_op jit(solution)/shard_map/ppermute | solution.py:336
  130.5 0.0 collective-permute-start.14
  130.5 0.0 collective-permute-done.5.refs_3_
  130.5 0.0 collective-permute-start.13
  130.5 4.6 %partial_cores.1 = (f32[4,128,128]{2,1,0:T(8,128)}, f32[4,128,128]{2,1,0:T(8,128)}, f32[4,128,128]{2,1,0:T(8,128)}, f32[4,128,128]{2,1,0:T(8,128)}) custom-call(s32[2]{0:T(128)} %pad_add_fusion.at, f32[128,512]{1,0:T(8,128)} %get-tuple-element.14.refs_0_, f32[128,512]{1,0:T(8,128)} %copy-done.8, f32[128,512]{1,0:T(8,128)} %collective-permute-done.4.refs_2_, ...), custom_call_target="tpu_custom_call" | custom-call | flops 805306368 | bytes 4194304 | tf_op jit(solution)/shard_map/partial_cores/pallas_call | solution.py:210
  135.1 3.4 %collective-permute-start.10 = (f32[4,128,128]{2,1,0:T(8,128)}, f32[4,128,128]{2,1,0:T(8,128)S(1)}, u32[]{:S(2)}, u32[]{:S(2)}) collective-permute-start(f32[4,128,128]{2,1,0:T(8,128)} %get-tuple-element.19), channel_id=1, source_target_pairs={{0,1},{1,2},{2,3},{3,0},{4,5},{5,6},{6,7},{7,4},{8,9},{9,10},{10,1... | collective-permute-start | bytes 786440 | tf_op jit(solution)/shard_map/ppermute | solution.py:336
  138.6 0.0 collective-permute-done.15.refs_7_
  138.6 13.5 %collective-permute-start.11 = (f32[4,128,128]{2,1,0:T(8,128)}, f32[4,128,128]{2,1,0:T(8,128)}, u32[]{:S(2)}, u32[]{:S(2)}) collective-permute-start(f32[4,128,128]{2,1,0:T(8,128)} %get-tuple-element.20), channel_id=1, source_target_pairs={{0,2},{1,3},{2,0},{3,1},{4,6},{5,7},{6,4},{7,5},{8,10},{9,11},{10,... | collective-permute-start | bytes 786440 | tf_op jit(solution)/shard_map/ppermute | solution.py:336
  152.0 3.4 %collective-permute-start.12 = (f32[4,128,128]{2,1,0:T(8,128)}, f32[4,128,128]{2,1,0:T(8,128)S(1)}, u32[]{:S(2)}, u32[]{:S(2)}) collective-permute-start(f32[4,128,128]{2,1,0:T(8,128)} %get-tuple-element.21), channel_id=1, source_target_pairs={{0,3},{1,0},{2,1},{3,2},{4,7},{5,4},{6,5},{7,6},{8,11},{9,8},{10,9... | collective-permute-start | bytes 786440 | tf_op jit(solution)/shard_map/ppermute | solution.py:336
  155.4 9.3 %sketch_tiles.1.refs_9_ = f32[4,2048,128]{2,1,0:T(8,128)} custom-call(f32[4,2048,128]{2,1,0:T(8,128)} %bitcast.46, f32[4,2048,128]{2,1,0:T(8,128)} %bitcast.48, f32[2048,128]{1,0:T(8,128)} %s_ref.3), custom_call_target="tpu_custom_call" | custom-call | flops 1610612736 | bytes 12582912 | tf_op jit(solution)/shard_map/sketch_tiles/pallas_call | solution.py:117
  164.7 4.8 %project.1 = (f32[4,2048,128]{2,1,0:T(8,128)}, f32[4,128,128]{2,1,0:T(8,128)}) custom-call(s32[2]{0:T(128)} %pad_add_fusion.at, f32[4,4,2,128,128]{4,3,2,1,0:T(8,128)} %copy-done, f32[4,4,2,128,128]{4,3,2,1,0:T(8,128)} %collective-permute-done.25.other, f32[2048,128]{1,0:T(8,128)} %s_ref.3), custom_call_target="tpu_custom_call" | custom-call | flops 805306368 | bytes 8388608 | tf_op jit(solution)/shard_map/project/pallas_call | solution.py:151
  169.5 0.0 collective-permute-done.10.refs_1_
  169.6 0.7 copy-done.4
  170.2 0.1 copy-done.5
  170.4 0.1 copy-done.6
  170.4 0.1 copy-done.7
  170.5 34.7 %recompress.1 = (f32[4,2048,128]{2,1,0:T(8,128)}, f32[4,2048,128]{2,1,0:T(8,128)}) custom-call(s32[2]{0:T(128)} %pad_add_fusion.at, f32[4,128,128]{2,1,0:T(8,128)} %get-tuple-element.18.refs_0_, f32[4,128,128]{2,1,0:T(8,128)} %copy-done.6, f32[4,128,128]{2,1,0:T(8,128)} %collective-permute-done.11.refs_2_, f32[4,128,128]{2,1,0:T(8,128)} %copy-done.7, ...), custom_call_target="tpu_custom_call" | custom-call | flops 3221225472 | bytes 29360128 | tf_op jit(solution)/shard_map/recompress/pallas_call | solution.py:310
  (26 shorter events, 0.1 us)
Async XLA Ops:
  0.6 17.8 %copy-start.1 = (f32[2,512,128]{2,1,0:T(8,128)S(1)}, f32[2,512,128]{2,1,0:T(8,128)}, u32[]{:S(2)}) copy-start(f32[2,512,128]{2,1,0:T(8,128)} %param.13) | copy-start | bytes 1572868
  1.9 6.6 %collective-permute-start.17 = (f32[2,128,128]{2,1,0:T(8,128)S(1)}, f32[2,128,128]{2,1,0:T(8,128)S(1)}, u32[]{:S(2)}, u32[]{:S(2)}) collective-permute-start(f32[2,128,128]{2,1,0:T(8,128)S(1)} %get-tuple-element.33), channel_id=1, source_target_pairs={{0,16},{4,20},{8,24},{12,28},{16,0},{20,4},{24,8},{28,12},{1,17},{... | collective-permute-start | bytes 393224 | tf_op jit(solution)/shard_map/ppermute | solution.py:333
  4.9 6.4 %collective-permute-start.16 = (f32[2,128,128]{2,1,0:T(8,128)S(1)}, f32[2,128,128]{2,1,0:T(8,128)S(1)}, u32[]{:S(2)}, u32[]{:S(2)}) collective-permute-start(f32[2,128,128]{2,1,0:T(8,128)S(1)} %get-tuple-element.34), channel_id=1, source_target_pairs={{0,8},{4,12},{8,0},{12,4},{16,24},{20,28},{24,16},{28,20},{1,9},{5... | collective-permute-start | bytes 393224 | tf_op jit(solution)/shard_map/ppermute | solution.py:333
  6.4 7.3 %collective-permute-start.18 = (f32[2,128,128]{2,1,0:T(8,128)S(1)}, f32[2,128,128]{2,1,0:T(8,128)S(1)}, u32[]{:S(2)}, u32[]{:S(2)}) collective-permute-start(f32[2,128,128]{2,1,0:T(8,128)S(1)} %get-tuple-element.35), channel_id=1, source_target_pairs={{0,24},{4,28},{8,16},{12,20},{16,8},{20,12},{24,0},{28,4},{1,25},{... | collective-permute-start | bytes 393224 | tf_op jit(solution)/shard_map/ppermute | solution.py:333
  6.5 23.8 %collective-permute-start.6 = (f32[2,512,128]{2,1,0:T(8,128)}, f32[2,512,128]{2,1,0:T(8,128)S(1)}, u32[]{:S(2)}, u32[]{:S(2)}) collective-permute-start(f32[2,512,128]{2,1,0:T(8,128)} %param.13), channel_id=1, source_target_pairs={{0,8},{4,12},{8,0},{12,4},{16,24},{20,28},{24,16},{28,20},{1,9},{5... | collective-permute-start | bytes 1572872 | tf_op jit(solution)/shard_map/ppermute | solution.py:333
  13.8 7.5 %collective-permute-start.21 = (f32[2,128,128]{2,1,0:T(8,128)S(1)}, f32[2,128,128]{2,1,0:T(8,128)S(1)}, u32[]{:S(2)}, u32[]{:S(2)}) collective-permute-start(f32[2,128,128]{2,1,0:T(8,128)S(1)} %get-tuple-element.29), channel_id=1, source_target_pairs={{0,3},{1,0},{2,1},{3,2},{4,7},{5,4},{6,5},{7,6},{8,11},{9,8},{10,9... | collective-permute-start | bytes 393224 | tf_op jit(solution)/shard_map/ppermute | solution.py:336
  17.4 10.3 %collective-permute-start.20 = (f32[2,128,128]{2,1,0:T(8,128)S(1)}, f32[2,128,128]{2,1,0:T(8,128)S(1)}, u32[]{:S(2)}, u32[]{:S(2)}) collective-permute-start(f32[2,128,128]{2,1,0:T(8,128)S(1)} %get-tuple-element.30), channel_id=1, source_target_pairs={{0,2},{1,3},{2,0},{3,1},{4,6},{5,7},{6,4},{7,5},{8,10},{9,11},{10,... | collective-permute-start | bytes 393224 | tf_op jit(solution)/shard_map/ppermute | solution.py:336
  17.4 10.3 %collective-permute-start.19 = (f32[2,128,128]{2,1,0:T(8,128)S(1)}, f32[2,128,128]{2,1,0:T(8,128)S(1)}, u32[]{:S(2)}, u32[]{:S(2)}) collective-permute-start(f32[2,128,128]{2,1,0:T(8,128)S(1)} %get-tuple-element.31), channel_id=1, source_target_pairs={{0,1},{1,2},{2,3},{3,0},{4,5},{5,6},{6,7},{7,4},{8,9},{9,10},{10,1... | collective-permute-start | bytes 393224 | tf_op jit(solution)/shard_map/ppermute | solution.py:336
  18.5 17.7 %collective-permute-start.8 = (f32[2,512,128]{2,1,0:T(8,128)S(1)}, f32[2,512,128]{2,1,0:T(8,128)S(1)}, u32[]{:S(2)}, u32[]{:S(2)}) collective-permute-start(f32[2,512,128]{2,1,0:T(8,128)S(1)} %copy-done.1), channel_id=1, source_target_pairs={{0,24},{4,28},{8,16},{12,20},{16,8},{20,12},{24,0},{28,4},{1,25},{... | collective-permute-start | bytes 1572872 | tf_op jit(solution)/shard_map/ppermute | solution.py:333
  21.3 26.0 %collective-permute-start.7 = (f32[2,512,128]{2,1,0:T(8,128)S(1)}, f32[2,512,128]{2,1,0:T(8,128)S(1)}, u32[]{:S(2)}, u32[]{:S(2)}) collective-permute-start(f32[2,512,128]{2,1,0:T(8,128)S(1)} %copy-done.1), channel_id=1, source_target_pairs={{0,16},{4,20},{8,24},{12,28},{16,0},{20,4},{24,8},{28,12},{1,17},{... | collective-permute-start | bytes 1572872 | tf_op jit(solution)/shard_map/ppermute | solution.py:333
  27.8 36.8 %collective-permute-start.23 = (f32[4,2,128,128]{3,2,1,0:T(8,128)S(1)}, f32[4,2,128,128]{3,2,1,0:T(8,128)S(1)}, u32[]{:S(2)}, u32[]{:S(2)}) collective-permute-start(f32[4,2,128,128]{3,2,1,0:T(8,128)S(1)} %get-tuple-element.27), channel_id=1, source_target_pairs={{0,16},{4,20},{8,24},{12,28},{16,0},{20,4},{24,8},{28,12},{1,17},{... | collective-permute-start | bytes 1572872 | tf_op jit(solution)/shard_map/ppermute | solution.py:333
  28.7 35.9 %collective-permute-start.22 = (f32[4,2,128,128]{3,2,1,0:T(8,128)S(1)}, f32[4,2,128,128]{3,2,1,0:T(8,128)S(1)}, u32[]{:S(2)}, u32[]{:S(2)}) collective-permute-start(f32[4,2,128,128]{3,2,1,0:T(8,128)S(1)} %get-tuple-element.27), channel_id=1, source_target_pairs={{0,8},{4,12},{8,0},{12,4},{16,24},{20,28},{24,16},{28,20},{1,9},{5... | collective-permute-start | bytes 1572872 | tf_op jit(solution)/shard_map/ppermute | solution.py:333
  30.2 34.4 %collective-permute-start.24 = (f32[4,2,128,128]{3,2,1,0:T(8,128)S(1)}, f32[4,2,128,128]{3,2,1,0:T(8,128)S(1)}, u32[]{:S(2)}, u32[]{:S(2)}) collective-permute-start(f32[4,2,128,128]{3,2,1,0:T(8,128)S(1)} %get-tuple-element.27), channel_id=1, source_target_pairs={{0,24},{4,28},{8,16},{12,20},{16,8},{20,12},{24,0},{28,4},{1,25},{... | collective-permute-start | bytes 1572872 | tf_op jit(solution)/shard_map/ppermute | solution.py:333
  48.7 81.8 %collective-permute-start.9 = (f32[4,2,512,128]{3,2,1,0:T(8,128)}, f32[4,2,512,128]{3,2,1,0:T(8,128)}, u32[]{:S(2)}, u32[]{:S(2)}) collective-permute-start(f32[4,2,512,128]{3,2,1,0:T(8,128)} %pad_maximum_fusion.refs_4_), channel_id=1, source_target_pairs={{0,4},{4,0},{8,12},{12,8},{16,20},{20,16},{24,28},{28,24},{1,5},{5... | collective-permute-start | bytes 6291464 | tf_op jit(solution)/shard_map/ppermute | solution.py:333
  64.7 1.0 copy-start.9
  64.9 30.0 %copy-start = (f32[4,4,2,128,128]{4,3,2,1,0:T(8,128)}, f32[4,4,2,128,128]{4,3,2,1,0:T(8,128)S(1)}, u32[]{:S(2)}) copy-start(f32[4,4,2,128,128]{4,3,2,1,0:T(8,128)S(1)} %pad_maximum_fusion.1.mine) | copy-start | bytes 6291460
  64.9 87.1 %collective-permute-start.25 = (f32[4,4,2,128,128]{4,3,2,1,0:T(8,128)S(1)}, f32[4,4,2,128,128]{4,3,2,1,0:T(8,128)}, u32[]{:S(2)}, u32[]{:S(2)}) collective-permute-start(f32[4,4,2,128,128]{4,3,2,1,0:T(8,128)S(1)} %pad_maximum_fusion.1.mine), channel_id=1, source_target_pairs={{0,4},{4,0},{8,12},{12,8},{16,20},{20,16},{24,28},{28,24},{1,5},{5... | collective-permute-start | bytes 6291464 | tf_op jit(solution)/shard_map/ppermute | solution.py:333
  65.6 12.8 %collective-permute-start.2 = (f32[512,128]{1,0:T(8,128)S(1)}, f32[512,128]{1,0:T(8,128)S(1)}, u32[]{:S(2)}, u32[]{:S(2)}) collective-permute-start(f32[512,128]{1,0:T(8,128)S(1)} %bitcast.71), channel_id=1, source_target_pairs={{0,3},{4,7},{8,11},{12,15},{16,19},{20,23},{24,27},{28,31}} | collective-permute-start | bytes 786440 | tf_op jit(solution)/shard_map/ppermute | solution.py:336
  71.7 12.4 %collective-permute-start.1 = (f32[512,128]{1,0:T(8,128)S(1)}, f32[512,128]{1,0:T(8,128)S(1)}, u32[]{:S(2)}, u32[]{:S(2)}) collective-permute-start(f32[512,128]{1,0:T(8,128)S(1)} %bitcast.72), channel_id=1, source_target_pairs={{0,2},{1,3},{4,6},{5,7},{8,10},{9,11},{12,14},{13,15},{16,18},{17,... | collective-permute-start | bytes 786440 | tf_op jit(solution)/shard_map/ppermute | solution.py:336
  73.0 15.6 %collective-permute-start = (f32[512,128]{1,0:T(8,128)S(1)}, f32[512,128]{1,0:T(8,128)S(1)}, u32[]{:S(2)}, u32[]{:S(2)}) collective-permute-start(f32[512,128]{1,0:T(8,128)S(1)} %bitcast.73), channel_id=1, source_target_pairs={{0,1},{1,2},{2,3},{4,5},{5,6},{6,7},{8,9},{9,10},{10,11},{12,13},{... | collective-permute-start | bytes 786440 | tf_op jit(solution)/shard_map/ppermute | solution.py:336
  76.1 34.5 %copy-start.2 = (f32[1,512,128]{2,1,0:T(8,128)S(1)}, f32[1,512,128]{2,1,0:T(8,128)}, u32[]{:S(2)}) copy-start(f32[1,512,128]{2,1,0:T(8,128)} %param.10) | copy-start | bytes 786436
  78.4 10.1 %copy-start.10 = (f32[512,128]{1,0:T(8,128)}, f32[512,128]{1,0:T(8,128)S(1)}, u32[]{:S(2)}) copy-start(f32[512,128]{1,0:T(8,128)S(1)} %collective-permute-done.2.refs_3_) | copy-start | bytes 786436
  84.1 4.5 %copy-start.11 = (f32[512,128]{1,0:T(8,128)}, f32[512,128]{1,0:T(8,128)S(1)}, u32[]{:S(2)}) copy-start(f32[512,128]{1,0:T(8,128)S(1)} %collective-permute-done.1.refs_2_) | copy-start | bytes 786436
  88.6 0.7 copy-start.12
  94.9 15.6 %collective-permute-start.3 = (f32[128,512]{1,0:T(8,128)}, f32[128,512]{1,0:T(8,128)S(1)}, u32[]{:S(2)}, u32[]{:S(2)}) collective-permute-start(f32[128,512]{1,0:T(8,128)} %get-tuple-element.15), channel_id=1, source_target_pairs={{1,0},{2,1},{3,2},{5,4},{6,5},{7,6},{9,8},{10,9},{11,10},{13,12},{... | collective-permute-start | bytes 786440 | tf_op jit(solution)/shard_map/ppermute | solution.py:336
  96.2 34.3 %collective-permute-start.4 = (f32[128,512]{1,0:T(8,128)}, f32[128,512]{1,0:T(8,128)}, u32[]{:S(2)}, u32[]{:S(2)}) collective-permute-start(f32[128,512]{1,0:T(8,128)} %get-tuple-element.16), channel_id=1, source_target_pairs={{2,0},{3,1},{6,4},{7,5},{10,8},{11,9},{14,12},{15,13},{18,16},{19,... | collective-permute-start | bytes 786440 | tf_op jit(solution)/shard_map/ppermute | solution.py:336
  97.5 33.0 %collective-permute-start.5 = (f32[128,512]{1,0:T(8,128)}, f32[128,512]{1,0:T(8,128)}, u32[]{:S(2)}, u32[]{:S(2)}) collective-permute-start(f32[128,512]{1,0:T(8,128)} %get-tuple-element.17), channel_id=1, source_target_pairs={{3,0},{7,4},{11,8},{15,12},{19,16},{23,20},{27,24},{31,28}} | collective-permute-start | bytes 786440 | tf_op jit(solution)/shard_map/ppermute | solution.py:336
  110.5 20.0 %copy-start.8 = (f32[128,512]{1,0:T(8,128)}, f32[128,512]{1,0:T(8,128)S(1)}, u32[]{:S(2)}) copy-start(f32[128,512]{1,0:T(8,128)S(1)} %collective-permute-done.3.refs_1_) | copy-start | bytes 786436
  110.5 28.0 %collective-permute-start.15 = (f32[512,128]{1,0:T(8,128)S(1)}, f32[512,128]{1,0:T(8,128)S(1)}, u32[]{:S(2)}, u32[]{:S(2)}) collective-permute-start(f32[512,128]{1,0:T(8,128)S(1)} %bitcast.59), channel_id=1, source_target_pairs={{0,3},{1,0},{2,1},{3,2},{4,7},{5,4},{6,5},{7,6},{8,11},{9,8},{10,9... | collective-permute-start | bytes 786440 | tf_op jit(solution)/shard_map/ppermute | solution.py:336
  130.5 39.0 %collective-permute-start.14 = (f32[512,128]{1,0:T(8,128)S(1)}, f32[512,128]{1,0:T(8,128)S(1)}, u32[]{:S(2)}, u32[]{:S(2)}) collective-permute-start(f32[512,128]{1,0:T(8,128)S(1)} %bitcast.60), channel_id=1, source_target_pairs={{0,2},{1,3},{2,0},{3,1},{4,6},{5,7},{6,4},{7,5},{8,10},{9,11},{10,... | collective-permute-start | bytes 786440 | tf_op jit(solution)/shard_map/ppermute | solution.py:336
  130.5 39.0 %collective-permute-start.13 = (f32[512,128]{1,0:T(8,128)S(1)}, f32[512,128]{1,0:T(8,128)S(1)}, u32[]{:S(2)}, u32[]{:S(2)}) collective-permute-start(f32[512,128]{1,0:T(8,128)S(1)} %bitcast.61), channel_id=1, source_target_pairs={{0,1},{1,2},{2,3},{3,0},{4,5},{5,6},{6,7},{7,4},{8,9},{9,10},{10,1... | collective-permute-start | bytes 786440 | tf_op jit(solution)/shard_map/ppermute | solution.py:336
  135.1 34.4 %collective-permute-start.10 = (f32[4,128,128]{2,1,0:T(8,128)}, f32[4,128,128]{2,1,0:T(8,128)S(1)}, u32[]{:S(2)}, u32[]{:S(2)}) collective-permute-start(f32[4,128,128]{2,1,0:T(8,128)} %get-tuple-element.19), channel_id=1, source_target_pairs={{0,1},{1,2},{2,3},{3,0},{4,5},{5,6},{6,7},{7,4},{8,9},{9,10},{10,1... | collective-permute-start | bytes 786440 | tf_op jit(solution)/shard_map/ppermute | solution.py:336
  138.6 26.1 %copy-start.3 = (f32[512,128]{1,0:T(8,128)}, f32[512,128]{1,0:T(8,128)S(1)}, u32[]{:S(2)}) copy-start(f32[512,128]{1,0:T(8,128)S(1)} %collective-permute-done.15.refs_7_) | copy-start | bytes 786436
  138.6 31.0 %collective-permute-start.11 = (f32[4,128,128]{2,1,0:T(8,128)}, f32[4,128,128]{2,1,0:T(8,128)}, u32[]{:S(2)}, u32[]{:S(2)}) collective-permute-start(f32[4,128,128]{2,1,0:T(8,128)} %get-tuple-element.20), channel_id=1, source_target_pairs={{0,2},{1,3},{2,0},{3,1},{4,6},{5,7},{6,4},{7,5},{8,10},{9,11},{10,... | collective-permute-start | bytes 786440 | tf_op jit(solution)/shard_map/ppermute | solution.py:336
  152.0 17.5 %collective-permute-start.12 = (f32[4,128,128]{2,1,0:T(8,128)}, f32[4,128,128]{2,1,0:T(8,128)S(1)}, u32[]{:S(2)}, u32[]{:S(2)}) collective-permute-start(f32[4,128,128]{2,1,0:T(8,128)} %get-tuple-element.21), channel_id=1, source_target_pairs={{0,3},{1,0},{2,1},{3,2},{4,7},{5,4},{6,5},{7,6},{8,11},{9,8},{10,9... | collective-permute-start | bytes 786440 | tf_op jit(solution)/shard_map/ppermute | solution.py:336
  169.5 0.7 copy-start.4
  169.5 0.8 copy-start.5
  169.5 0.9 copy-start.6
  169.6 0.9 copy-start.7

commit v3 on v2

--- a/solution.py
+++ b/solution.py
@@ -102,11 +102,17 @@
     lax.fori_loop(0, n // step, one, 0)
 
 
-def sketched(u_ref, v_ref, s_ref, out_ref):
-    rhs = doubled_rows(product_tn(v_ref[0], s_ref[...]))
+def sketched(u_ref, v_ref, s_ref, out_ref, u_parts, v_parts):
+    v = beside(v_ref[0])
+    v_parts[0] = v
+    x = fold(mm(v, beside(s_ref[...]), TN))
+    h = x.shape[0] // 2
+    rhs = doubled_rows(x[:h] + x[h:])
 
     def body(at):
-        out_ref[0, at, :] = fold(mm(beside(u_ref[0, at, :]), rhs, NN))
+        u = beside(u_ref[0, at, :])
+        u_parts[0, at, :] = u
+        out_ref[0, at, :] = fold(mm(u, rhs, NN))
 
     rows_loop(u_ref.shape[1], 512, body)
 
@@ -114,13 +120,14 @@
 def sketch_tiles(tile_u, tile_v, sketch):
     tiles, n, k = tile_u.shape
     block = pl.BlockSpec((1, n, k), lambda i: (i, 0, 0))
+    parts = pl.BlockSpec((1, n, 2 * k), lambda i: (i, 0, 0))
     return pl.pallas_call(
         sketched,
         grid=(tiles,),
         in_specs=[block, block, pl.BlockSpec((n, k), lambda i: (0, 0))],
-        out_specs=block,
-        out_shape=jax.ShapeDtypeStruct(tile_u.shape, f32),
-        cost_estimate=pl.CostEstimate(flops=6 * tiles * n * k * k * 2, bytes_accessed=12 * tiles * n * k, transcendentals=0),
+        out_specs=[block, parts, parts],
+        out_shape=[jax.ShapeDtypeStruct(tile_u.shape, f32)] + [jax.ShapeDtypeStruct((tiles, n, 2 * k), bf16)] * 2,
+        cost_estimate=pl.CostEstimate(flops=6 * tiles * n * k * k * 2, bytes_accessed=20 * tiles * n * k, transcendentals=0),
         name="sketch_tiles",
     )(tile_u, tile_v, sketch)
 
@@ -139,9 +146,12 @@
                 start = block_of(c, d, n_col) * (chips * piece) + (chip ^ e) * piece
                 rows = pl.ds(pl.multiple_of(start, piece), piece)
                 for t in range(pair):
-                    full[parity * pair + t, rows, :] = src[e, d, t]
+                    full[parity * pair + t, rows, :] = beside(src[e, d, t])
+    rhs = beside(s_ref[...])
     for j in range(full.shape[0]):
-        small[j] = product_tn(full[j], s_ref[...])
+        x = fold(mm(full[j], rhs, TN))
+        h = x.shape[0] // 2
+        small[j] = x[:h] + x[h:]
 
 
 def project(n_col, at, mine, other, sketch):
@@ -152,7 +162,7 @@
         functools.partial(project_kernel, n_col),
         in_specs=[pl.BlockSpec(memory_space=pltpu.SMEM)] + [vmem] * 3,
         out_specs=[vmem] * 2,
-        out_shape=[jax.ShapeDtypeStruct((tiles, n, k), f32), jax.ShapeDtypeStruct((tiles, k, k), f32)],
+        out_shape=[jax.ShapeDtypeStruct((tiles, n, 2 * k), bf16), jax.ShapeDtypeStruct((tiles, k, k), f32)],
         cost_estimate=pl.CostEstimate(flops=6 * tiles * n * k * k, bytes_accessed=8 * tiles * n * k, transcendentals=0),
         name="project",
     )(at, mine, other, sketch)
@@ -219,8 +229,8 @@
 
 def recompress_kernel(tiles, n, k, n_col, at, *refs):
     core_parts, row_us = refs[:n_col], refs[n_col : 2 * n_col]
-    small, base, tile_u, tile_v, col_u, new_u, new_v = refs[2 * n_col : 2 * n_col + 7]
-    s, tu, tv, cu, ru, work, cross, cores, row_parts, sem, row_sem = refs[2 * n_col + 7 :]
+    small, base, u_parts, v_parts, w_parts, new_u, new_v = refs[2 * n_col : 2 * n_col + 7]
+    s, tu, tv, cu, sp, out, ru, work, cross, cores, row_parts, sem, row_sem = refs[2 * n_col + 7 :]
     c = at[1]
     root = math.sqrt(n)
     blk = n // n_col
@@ -228,15 +238,23 @@
     for d in range(n_col):
         rows = pl.ds(pl.multiple_of(block_of(c, d, n_col) * blk, blk), blk)
         row_copies.append(pltpu.make_async_copy(row_us[d], ru.at[rows], row_sem.at[d]))
-    copies = []
+    early, late, outs = [], [], []
     for t in range(tiles):
-        copies.append(pltpu.make_async_copy(base.at[t], s.at[t], sem.at[t]))
-        copies.append(pltpu.make_async_copy(tile_u.at[t], tu.at[t], sem.at[tiles + t]))
-    late = []
-    for t in range(tiles):
-        late.append(pltpu.make_async_copy(tile_v.at[t], tv.at[t], sem.at[2 * tiles + t]))
-        late.append(pltpu.make_async_copy(col_u.at[t], cu.at[t], sem.at[3 * tiles + t]))
-    for x in row_copies + copies + late:
+        early.append((
+            pltpu.make_async_copy(base.at[t], s.at[t], sem.at[t]),
+            pltpu.make_async_copy(u_parts.at[t], tu.at[t], sem.at[tiles + t]),
+        ))
+        late.append((
+            pltpu.make_async_copy(v_parts.at[t], tv.at[t], sem.at[2 * tiles + t]),
+            pltpu.make_async_copy(w_parts.at[t], cu.at[t], sem.at[3 * tiles + t]),
+        ))
+        outs.append((
+            pltpu.make_async_copy(s.at[t], new_u.at[t], sem.at[4 * tiles + t]),
+            pltpu.make_async_copy(out.at[t], new_v.at[t], sem.at[5 * tiles + t]),
+        ))
+    for x in row_copies:
+        x.start()
+    for x in early[0] + early[1]:
         x.start()
     total = core_parts[0][...]
     for p in core_parts[1:]:
@@ -250,77 +268,77 @@
 
     rows_loop(n, 512, split)
     for t in range(tiles):
-        copies[2 * t].wait()
-        copies[2 * t + 1].wait()
+        for x in early[t]:
+            x.wait()
+        for x in (early + late)[t + 2]:
+            x.start()
         rhs = doubled_rows(-product(cores[t], small[t]))
-
-        def update(at, t=t, rhs=rhs):
-            s[t, at, :] = s[t, at, :] + fold(mm(row_parts[at, :], rhs, NN))
-
-        rows_loop(n, 512, update)
         work[t] = jnp.zeros((k, 2 * k), f32)
         cross[t] = jnp.zeros((k, 2 * k), f32)
 
-        def gather(at, t=t):
-            part = beside(s[t, at, :])
-            x = mm(part, jnp.concatenate([part, beside(tu[t, at, :]), row_parts[at, :]], axis=1), TN)
+        def gather(at, t=t, rhs=rhs):
+            part = beside(s[t, at, :] + fold(mm(row_parts[at, :], rhs, NN)))
+            sp[t, at, :] = part
+            x = mm(part, jnp.concatenate([part, tu[t, at, :], row_parts[at, :]], axis=1), TN)
             x = x[:k] + x[k:]
             work[t, :, :k] += fold(x[:, : 2 * k])
             cross[t, :, :k] += fold(x[:, 2 * k : 4 * k])
             cross[t, :, k:] += fold(x[:, 4 * k :])
 
-        rows_loop(n, 512, gather)
+        gather(pl.ds(0, n))
+    for pair in late[2:]:
+        for x in pair:
+            x.start()
     eye = jnp.where(
         lax.broadcasted_iota(jnp.int32, (k, k), 0) == lax.broadcasted_iota(jnp.int32, (k, k), 1), 1.0, 0.0
     ).astype(f32)
     for t in range(tiles):
         work[t, :, k:] = eye
     eliminate(work, tiles, k)
-    outs = []
     for t in range(tiles):
         inverse = work[t, :, k:]
         y = product(inverse, cross[t]) * (1.0 / root)
         c1 = y[:, :k]
         c2 = -product(y[:, k:], cores[t])
-        late[2 * t].wait()
-        late[2 * t + 1].wait()
         by = doubled_columns(inverse * root)
         c12 = jnp.concatenate([doubled_columns(c1), doubled_columns(c2)], axis=1)
+        for x in late[t]:
+            x.wait()
 
         def finish(at, t=t, by=by, c12=c12):
-            s[t, at, :] = fold(mm(beside(s[t, at, :]), by, NT))
-            lhs = jnp.concatenate([beside(tv[t, at, :]), beside(cu[t, at, :])], axis=1)
-            tv[t, at, :] = fold(mm(lhs, c12, NT))
-
-        rows_loop(n, 512, finish)
-        outs.append(pltpu.make_async_copy(s.at[t], new_u.at[t], sem.at[4 * tiles + t]))
-        outs.append(pltpu.make_async_copy(tv.at[t], new_v.at[t], sem.at[5 * tiles + t]))
-        outs[-2].start()
-        outs[-1].start()
-    for x in outs:
-        x.wait()
-
-
-def recompress(at, core_parts, row_us, small, base, tile_u, tile_v, col_u):
-    tiles, n, k = tile_u.shape
+            s[t, at, :] = fold(mm(sp[t, at, :], by, NT))
+            lhs = jnp.concatenate([tv[t, at, :], cu[t, at, :]], axis=1)
+            out[t, at, :] = fold(mm(lhs, c12, NT))
+
+        finish(pl.ds(0, n))
+        for x in outs[t]:
+            x.start()
+    for pair in outs:
+        for x in pair:
+            x.wait()
+
+
+def recompress(at, core_parts, row_us, small, base, u_parts, v_parts, w_parts):
+    tiles, n, k = base.shape
     n_col = len(core_parts)
     any_ = pl.BlockSpec(memory_space=ANY)
     vmem = pl.BlockSpec(memory_space=VMEM)
     full = lambda: VMEM((tiles, n, k), f32)
+    split = lambda: VMEM((tiles, n, 2 * k), bf16)
     return pl.pallas_call(
         functools.partial(recompress_kernel, tiles, n, k, n_col),
         in_specs=[pl.BlockSpec(memory_space=pltpu.SMEM)] + [vmem] * n_col + [any_] * n_col + [vmem] + [any_] * 4,
         out_specs=[any_, any_],
-        out_shape=[jax.ShapeDtypeStruct(tile_u.shape, f32)] * 2,
+        out_shape=[jax.ShapeDtypeStruct(base.shape, f32)] * 2,
         scratch_shapes=[
-            full(), full(), full(), full(), VMEM((n, k), f32),
+            full(), split(), split(), split(), split(), full(), VMEM((n, k), f32),
             VMEM((tiles, k, 2 * k), f32), VMEM((tiles, k, 2 * k), f32), VMEM((tiles, k, k), f32),
             VMEM((n, 2 * k), bf16),
             pltpu.SemaphoreType.DMA((6 * tiles,)), pltpu.SemaphoreType.DMA((n_col,)),
         ],
         cost_estimate=pl.CostEstimate(flops=24 * tiles * n * k * k, bytes_accessed=28 * tiles * n * k, transcendentals=0),
         name="recompress",
-    )(at, *core_parts, *row_us, small, base, tile_u, tile_v, col_u)
+    )(at, *core_parts, *row_us, small, base, u_parts, v_parts, w_parts)
 
 
 def step(n_row, n_col, tile_u, tile_v, row_panel_u, row_panel_v, col_panel_u, col_panel_v, diag_inverse, sketch):
@@ -351,24 +369,25 @@
     below = [row_v] + [up(row_v, d) for d in range(1, n_col)]
     col_v_mine = jnp.stack([col_panel_v] + [partner(col_panel_v, 2 * e) for e in range(1, chips)])
     row_u = row_panel_u[0]
-    row_us = [row_u] + [around(row_u, d) for d in range(1, n_col)]
+    rises = [up(row_u, d) for d in range(1, n_col)]
+    falls = [down(row_u, d) for d in range(1, n_col)]
+    row_us = [row_u] + [jnp.where(c >= d, rises[d - 1], falls[n_col - d - 1]) for d in range(1, n_col)]
     pair, rows, k = col_panel_u.shape
     cut = col_panel_u.reshape(pair, chips, rows // chips, k)
     cuts = jnp.stack([pick(cut, chip, 1)] + [partner(pick(cut, chip ^ e, 1), 2 * e) for e in range(1, chips)])
     col_v_other = partner(col_v_mine, 1)
-    planes = jnp.stack(
-        [pick(cuts, chip ^ c)] + [around(pick(cuts, chip ^ lax.rem(c + d, n_col)), d) for d in range(1, n_col)]
-    )
-    base = sketch_tiles(tile_u[0], tile_v[0], sketch)
+    moved = [pick(cuts, chip ^ c)] + [around(pick(cuts, chip ^ lax.rem(c + d, n_col)), d) for d in range(1, n_col)]
+    planes = lax.optimization_barrier(jnp.stack(moved))
+    base, u_parts, v_parts = sketch_tiles(tile_u[0], tile_v[0], sketch)
     sums = solve(at, diag_inverse, below)
     parts = [sums[0]] + [down(sums[d], d) for d in range(1, n_col)]
     gathered = [planes] + [partner(planes, 2 * e) for e in range(1, chips)]
     col_u_mine = jnp.stack(gathered)
     col_u_other = partner(col_u_mine, 1)
-    col_u, small = project(n_col, at, col_u_mine, col_u_other, sketch)
+    w_parts, small = project(n_col, at, col_u_mine, col_u_other, sketch)
     cores = partial_cores(at, parts, col_v_mine, col_v_other)
     core_parts = [cores[0]] + [around(cores[d], d) for d in range(1, n_col)]
-    new_u, new_v = recompress(at, core_parts, row_us, small, base, tile_u[0], tile_v[0], col_u)
+    new_u, new_v = recompress(at, core_parts, row_us, small, base, u_parts, v_parts, w_parts)
     return new_u[None], new_v[None]
 
 

time: 208 us -> 190 us (0.913)
  waiting for transfers between devices: 82.6 us -> 66.5 us
  Pallas kernels: 58.9 us -> 51.3 us
  starting transfers between devices: 56.8 us -> 60.4 us
  other arithmetic: 2.4 us -> 4.6 us
    ppermute x15 -> x18, waiting for transfers between devices: 45.5 us -> 30.6 us  [shift(): return lax.ppermute(x, 'col', pairs)]
    pallas_call x1, Pallas kernels: 34.7 us -> 24.8 us  [recompress(): pl.pallas_call(functools.partial(recompress_kernel, tiles, n, k, n_col),...]
    ppermute x15 -> x18, starting transfers between devices: 42.3 us -> 47 us  [shift(): return lax.ppermute(x, 'col', pairs)]
    select_n x0 -> x3, other arithmetic: none -> 2.25 us  [step(): jnp.where(c >= d, rises[d - 1], falls[n_col - d - 1])]
  transfers between devices with their start and end apart: 26 -> 29, of which waited for: 11 -> 14; matrix products, arithmetic and copies ran while one was open for 1% -> 2% of each run, Pallas kernels for 12% -> 14%
where the time goes in v3:
time: 190 us; the launch traced here: 187 us
  waiting for transfers between devices  66.5 us (35%)
  starting transfers between devices  60.4 us (32%)
  Pallas kernels  51.3 us (27%)
  other arithmetic  4.6 us (2%)
  local copies, waits for them, and re-layouts  3.41 us (2%)
    ppermute x18, starting transfers between devices, shift(): return lax.ppermute(x, 'col', pairs)  47 us
    ppermute x11, waiting for transfers between devices, partner(): return lax.ppermute(x, 'row', [(a, a ^ m) for a in range(n_row)])  35.9 us
    ppermute x18, waiting for transfers between devices, shift(): return lax.ppermute(x, 'col', pairs)  30.6 us
    pallas_call x1, Pallas kernels, recompress(): pl.pallas_call(functools.partial(recompress_kernel, tiles, n, k, n_col),...  24.8 us
    ppermute x11, starting transfers between devices, partner(): return lax.ppermute(x, 'row', [(a, a ^ m) for a in range(n_row)])  13.5 us
    pallas_call x1, Pallas kernels, sketch_tiles(): pl.pallas_call(sketched, grid=(tiles,), in_specs=[block, block, pl.BlockS...  11.2 us
    pallas_call x1, Pallas kernels, solve(): pl.pallas_call(functools.partial(solve_kernel, n_col), in_specs=[pl.Block...  5.67 us
    pallas_call x1, Pallas kernels, project(): pl.pallas_call(functools.partial(project_kernel, n_col), in_specs=[pl.Blo...  5.04 us
  transfers between devices with their start and end apart: 29, of which 14 were waited for; matrix products, arithmetic and copies ran while one was open for 2% of the time, Pallas kernels for 14%

profile of v3, /device:TPU:0, one launch (start us, length us, event | category | flops | bytes accessed | tf_op | source)
XLA Modules:
  0.0 187.2 jit_solution(16776749813686048309)
XLA Ops:
  0.6 0.0 copy-start.1
  0.7 1.2 dynamic-slice_bitcast_fusion.6
  1.9 3.1 %collective-permute-start.20 = (f32[2,128,128]{2,1,0:T(8,128)S(1)}, f32[2,128,128]{2,1,0:T(8,128)S(1)}, u32[]{:S(2)}, u32[]{:S(2)}) collective-permute-start(f32[2,128,128]{2,1,0:T(8,128)S(1)} %get-tuple-element.37), channel_id=1, source_target_pairs={{0,16},{4,20},{8,24},{12,28},{16,0},{20,4},{24,8},{28,12},{1,17},{... | collective-permute-start | bytes 393224 | tf_op jit(solution)/shard_map/ppermute | solution.py:351
  4.9 1.5 collective-permute-start.19
  6.4 0.0 collective-permute-start.21
  6.5 1.9 %collective-permute-start.6 = (f32[2,512,128]{2,1,0:T(8,128)}, f32[2,512,128]{2,1,0:T(8,128)S(1)}, u32[]{:S(2)}, u32[]{:S(2)}) collective-permute-start(f32[2,512,128]{2,1,0:T(8,128)} %param.13), channel_id=1, source_target_pairs={{0,8},{4,12},{8,0},{12,4},{16,24},{20,28},{24,16},{28,20},{1,9},{5... | collective-permute-start | bytes 1572872 | tf_op jit(solution)/shard_map/ppermute | solution.py:351
  8.4 0.0 collective-permute-done.20
  8.4 2.9 %collective-permute-done.19 = f32[2,128,128]{2,1,0:T(8,128)S(1)} collective-permute-done((f32[2,128,128]{2,1,0:T(8,128)S(1)}, f32[2,128,128]{2,1,0:T(8,128)S(1)}, u32[]{:S(2)}, u32[]{:S(2)}) %collective-permute-start.19) | collective-permute-done | bytes 131104 | tf_op jit(solution)/shard_map/ppermute | solution.py:351
  11.3 2.4 %collective-permute-done.21 = f32[2,128,128]{2,1,0:T(8,128)S(1)} collective-permute-done((f32[2,128,128]{2,1,0:T(8,128)S(1)}, f32[2,128,128]{2,1,0:T(8,128)S(1)}, u32[]{:S(2)}, u32[]{:S(2)}) %collective-permute-start.21) | collective-permute-done | bytes 131104 | tf_op jit(solution)/shard_map/ppermute | solution.py:351
  13.8 3.7 %collective-permute-start.24 = (f32[2,128,128]{2,1,0:T(8,128)S(1)}, f32[2,128,128]{2,1,0:T(8,128)S(1)}, u32[]{:S(2)}, u32[]{:S(2)}) collective-permute-start(f32[2,128,128]{2,1,0:T(8,128)S(1)} %get-tuple-element.33), channel_id=1, source_target_pairs={{0,3},{1,0},{2,1},{3,2},{4,7},{5,4},{6,5},{7,6},{8,11},{9,8},{10,9... | collective-permute-start | bytes 393224 | tf_op jit(solution)/shard_map/ppermute | solution.py:354
  17.4 2.8 %collective-permute-start.8 = (f32[2,512,128]{2,1,0:T(8,128)S(1)}, f32[2,512,128]{2,1,0:T(8,128)S(1)}, u32[]{:S(2)}, u32[]{:S(2)}) collective-permute-start(f32[2,512,128]{2,1,0:T(8,128)S(1)} %copy-done.1), channel_id=1, source_target_pairs={{0,24},{4,28},{8,16},{12,20},{16,8},{20,12},{24,0},{28,4},{1,25},{... | collective-permute-start | bytes 1572872 | tf_op jit(solution)/shard_map/ppermute | solution.py:351
  20.2 0.5 collective-permute-start.7
  20.8 0.0 collective-permute-start.23
  20.8 0.6 collective-permute-done.24
  21.3 1.0 collective-permute-start.22
  22.3 4.4 %collective-permute-done.23 = f32[2,128,128]{2,1,0:T(8,128)S(1)} collective-permute-done((f32[2,128,128]{2,1,0:T(8,128)S(1)}, f32[2,128,128]{2,1,0:T(8,128)S(1)}, u32[]{:S(2)}, u32[]{:S(2)}) %collective-permute-start.23) | collective-permute-done | bytes 131104 | tf_op jit(solution)/shard_map/ppermute | solution.py:354
  26.7 1.9 collective-permute-done.22
  28.6 1.8 collective-permute-start.27
  30.4 1.1 collective-permute-start.26
  31.6 0.0 collective-permute-done.6
  31.6 0.6 collective-permute-start.25
  32.2 4.1 %collective-permute-done.8 = f32[2,512,128]{2,1,0:T(8,128)S(1)} collective-permute-done((f32[2,512,128]{2,1,0:T(8,128)S(1)}, f32[2,512,128]{2,1,0:T(8,128)S(1)}, u32[]{:S(2)}, u32[]{:S(2)}) %collective-permute-start.8) | collective-permute-done | bytes 524320 | tf_op jit(solution)/shard_map/ppermute | solution.py:351
  36.3 20.6 %collective-permute-done.7 = f32[2,512,128]{2,1,0:T(8,128)S(1)} collective-permute-done((f32[2,512,128]{2,1,0:T(8,128)S(1)}, f32[2,512,128]{2,1,0:T(8,128)S(1)}, u32[]{:S(2)}, u32[]{:S(2)}) %collective-permute-start.7) | collective-permute-done | bytes 524320 | tf_op jit(solution)/shard_map/ppermute | solution.py:351
  56.9 1.5 pad_maximum_fusion.refs_4_
  58.3 0.0 collective-permute-done.27
  58.3 5.9 %collective-permute-done.26 = f32[4,2,128,128]{3,2,1,0:T(8,128)S(1)} collective-permute-done((f32[4,2,128,128]{3,2,1,0:T(8,128)S(1)}, f32[4,2,128,128]{3,2,1,0:T(8,128)S(1)}, u32[]{:S(2)}, u32[]{:S(2)}) %collective-permute-start.26) | collective-permute-done | bytes 524320 | tf_op jit(solution)/shard_map/ppermute | solution.py:351
  64.2 0.2 pad_maximum_fusion.1.mine
  64.5 0.0 copy-start
  64.5 0.1 collective-permute-start.28
  64.5 0.6 copy-done.2
  65.2 1.3 collective-permute-start.18
  66.5 3.4 %collective-permute-start.2 = (f32[512,128]{1,0:T(8,128)S(1)}, f32[512,128]{1,0:T(8,128)S(1)}, u32[]{:S(2)}, u32[]{:S(2)}) collective-permute-start(f32[512,128]{1,0:T(8,128)S(1)} %bitcast.72), channel_id=1, source_target_pairs={{0,3},{4,7},{8,11},{12,15},{16,19},{20,23},{24,27},{28,31}} | collective-permute-start | bytes 786440 | tf_op jit(solution)/shard_map/ppermute | solution.py:354
  69.9 2.0 %collective-permute-start.1 = (f32[512,128]{1,0:T(8,128)S(1)}, f32[512,128]{1,0:T(8,128)}, u32[]{:S(2)}, u32[]{:S(2)}) collective-permute-start(f32[512,128]{1,0:T(8,128)S(1)} %bitcast.73), channel_id=1, source_target_pairs={{0,2},{1,3},{4,6},{5,7},{8,10},{9,11},{12,14},{13,15},{16,18},{17,... | collective-permute-start | bytes 786440 | tf_op jit(solution)/shard_map/ppermute | solution.py:354
  71.9 3.2 %collective-permute-done.18 = f32[512,128]{1,0:T(8,128)S(1)} collective-permute-done((f32[512,128]{1,0:T(8,128)S(1)}, f32[512,128]{1,0:T(8,128)S(1)}, u32[]{:S(2)}, u32[]{:S(2)}) %collective-permute-start.18) | collective-permute-done | bytes 262176 | tf_op jit(solution)/shard_map/ppermute | solution.py:354
  75.1 1.5 collective-permute-start
  76.6 0.0 collective-permute-done.2.refs_3_
  76.6 6.2 %collective-permute-start.17 = (f32[512,128]{1,0:T(8,128)S(1)}, f32[512,128]{1,0:T(8,128)S(1)}, u32[]{:S(2)}, u32[]{:S(2)}) collective-permute-start(f32[512,128]{1,0:T(8,128)S(1)} %bitcast.58), channel_id=1, source_target_pairs={{0,3},{4,7},{8,11},{12,15},{16,19},{20,23},{24,27},{28,31}} | collective-permute-start | bytes 786440 | tf_op jit(solution)/shard_map/ppermute | solution.py:354
  82.9 0.0 collective-permute-done.1.refs_2_
  82.9 1.3 collective-permute-start.16
  84.2 0.6 pad_add_fusion.at
  84.8 3.1 %collective-permute-done.refs_1_ = f32[512,128]{1,0:T(8,128)S(1)} collective-permute-done((f32[512,128]{1,0:T(8,128)S(1)}, f32[512,128]{1,0:T(8,128)S(1)}, u32[]{:S(2)}, u32[]{:S(2)}) %collective-permute-start) | collective-permute-done | bytes 262176 | tf_op jit(solution)/shard_map/ppermute | solution.py:354
  87.9 0.7 copy-done.8
  88.6 15.1 %collective-permute-start.15 = (f32[512,128]{1,0:T(8,128)S(1)}, f32[512,128]{1,0:T(8,128)S(1)}, u32[]{:S(2)}, u32[]{:S(2)}) collective-permute-start(f32[512,128]{1,0:T(8,128)S(1)} %bitcast.60), channel_id=1, source_target_pairs={{0,2},{1,3},{4,6},{5,7},{8,10},{9,11},{12,14},{13,15},{16,18},{17,... | collective-permute-start | bytes 786440 | tf_op jit(solution)/shard_map/ppermute | solution.py:354
  103.7 5.7 %solve.1 = (f32[128,512]{1,0:T(8,128)}, f32[128,512]{1,0:T(8,128)}, f32[128,512]{1,0:T(8,128)}, f32[128,512]{1,0:T(8,128)}) custom-call(s32[2]{0:T(128)} %pad_add_fusion.at, f32[512,2048]{1,0:T(8,128)} %diag.1, f32[512,128]{1,0:T(8,128)} %bitcast.71, f32[512,128]{1,0:T(8,128)} %copy-done.8, f32[512,128]{1,0:T(8,128)} %collective-permute-done.1.refs_2_, ...), custom_call_target="tpu_custom_call" | custom-call | flops 1610612736 | bytes 4194304 | tf_op jit(solution)/shard_map/solve/pallas_call | solution.py:189
  109.4 1.3 collective-permute-start.3
  110.7 1.3 collective-permute-start.4
  112.0 11.2 %sketch_tiles.1 = (f32[4,2048,128]{2,1,0:T(8,128)}, bf16[4,2048,256]{2,1,0:T(8,128)(2,1)}, bf16[4,2048,256]{2,1,0:T(8,128)(2,1)}) custom-call(f32[4,2048,128]{2,1,0:T(8,128)} %bitcast.45, f32[4,2048,128]{2,1,0:T(8,128)} %bitcast.46, f32[2048,128]{1,0:T(8,128)} %s_ref.3), custom_call_target="tpu_custom_call" | custom-call | flops 1610612736 | bytes 20971520 | tf_op jit(solution)/shard_map/sketch_tiles/pallas_call | solution.py:124
  123.1 1.3 collective-permute-start.5
  124.4 0.7 broadcast_select_fusion.refs_7_
  125.2 1.3 collective-permute-start.14
  126.5 2.2 %collective-permute-done.4.refs_2_ = f32[128,512]{1,0:T(8,128)} collective-permute-done((f32[128,512]{1,0:T(8,128)}, f32[128,512]{1,0:T(8,128)}, u32[]{:S(2)}, u32[]{:S(2)}) %collective-permute-start.4) | collective-permute-done | bytes 262176 | tf_op jit(solution)/shard_map/ppermute | solution.py:354
  128.7 2.5 %collective-permute-start.13 = (f32[512,128]{1,0:T(8,128)S(1)}, f32[512,128]{1,0:T(8,128)}, u32[]{:S(2)}, u32[]{:S(2)}) collective-permute-start(f32[512,128]{1,0:T(8,128)S(1)} %bitcast.62), channel_id=1, source_target_pairs={{0,1},{1,2},{2,3},{4,5},{5,6},{6,7},{8,9},{9,10},{10,11},{12,13},{... | collective-permute-start | bytes 786440 | tf_op jit(solution)/shard_map/ppermute | solution.py:354
  131.2 0.8 broadcast_select_fusion.1.refs_6_
  132.0 6.1 %collective-permute-done.5.refs_3_ = f32[128,512]{1,0:T(8,128)} collective-permute-done((f32[128,512]{1,0:T(8,128)}, f32[128,512]{1,0:T(8,128)}, u32[]{:S(2)}, u32[]{:S(2)}) %collective-permute-start.5) | collective-permute-done | bytes 262176 | tf_op jit(solution)/shard_map/ppermute | solution.py:354
  138.1 4.6 %partial_cores.1 = (f32[4,128,128]{2,1,0:T(8,128)}, f32[4,128,128]{2,1,0:T(8,128)}, f32[4,128,128]{2,1,0:T(8,128)}, f32[4,128,128]{2,1,0:T(8,128)}) custom-call(s32[2]{0:T(128)} %pad_add_fusion.at, f32[128,512]{1,0:T(8,128)} %get-tuple-element.17.refs_0_, f32[128,512]{1,0:T(8,128)} %collective-permute-done.3.refs_1_, ...), custom_call_target="tpu_custom_call" | custom-call | flops 805306368 | bytes 4194304 | tf_op jit(solution)/shard_map/partial_cores/pallas_call | solution.py:220
  142.7 0.1 collective-permute-start.11
  142.8 3.7 %collective-permute-start.12 = (f32[4,128,128]{2,1,0:T(8,128)}, f32[4,128,128]{2,1,0:T(8,128)S(1)}, u32[]{:S(2)}, u32[]{:S(2)}) collective-permute-start(f32[4,128,128]{2,1,0:T(8,128)} %get-tuple-element.24), channel_id=1, source_target_pairs={{0,3},{1,0},{2,1},{3,2},{4,7},{5,4},{6,5},{7,6},{8,11},{9,8},{10,9... | collective-permute-start | bytes 786440 | tf_op jit(solution)/shard_map/ppermute | solution.py:354
  146.5 0.8 broadcast_select_fusion.2.refs_5_
  147.3 5.0 %project.1 = (bf16[4,2048,256]{2,1,0:T(8,128)(2,1)}, f32[4,128,128]{2,1,0:T(8,128)}) custom-call(s32[2]{0:T(128)} %pad_add_fusion.at, f32[4,4,2,128,128]{4,3,2,1,0:T(8,128)} %copy-done, f32[4,4,2,128,128]{4,3,2,1,0:T(8,128)} %collective-permute-done.28.other, f32[2048,128]{1,0:T(8,128)} %s_ref.3), custom_call_target="tpu_custom_call" | custom-call | flops 805306368 | bytes 8388608 | tf_op jit(solution)/shard_map/project/pallas_call | solution.py:161
  152.3 1.6 collective-permute-done.10.refs_1_
  153.9 7.5 %collective-permute-done.11.refs_2_ = f32[4,128,128]{2,1,0:T(8,128)S(1)} collective-permute-done((f32[4,128,128]{2,1,0:T(8,128)}, f32[4,128,128]{2,1,0:T(8,128)S(1)}, u32[]{:S(2)}, u32[]{:S(2)}) %collective-permute-start.11) | collective-permute-done | bytes 262176 | tf_op jit(solution)/shard_map/ppermute | solution.py:354
  161.4 0.7 copy-done.4
  162.1 0.1 copy-done.5
  162.2 24.8 %recompress.1 = (f32[4,2048,128]{2,1,0:T(8,128)}, f32[4,2048,128]{2,1,0:T(8,128)}) custom-call(s32[2]{0:T(128)} %pad_add_fusion.at, f32[4,128,128]{2,1,0:T(8,128)} %get-tuple-element.21.refs_0_, f32[4,128,128]{2,1,0:T(8,128)} %copy-done.3, f32[4,128,128]{2,1,0:T(8,128)} %copy-done.4, f32[4,128,128]{2,1,0:T(8,128)} %copy-done.5, f32[512,128]{1,0:T(8,128)} %bitcast.56, ...), custom_call_target="tpu_custom_call" | custom-call | flops 3221225472 | bytes 29360128 | tf_op jit(solution)/shard_map/recompress/pallas_call | solution.py:328
  (27 shorter events, 0.2 us)
Async XLA Ops:
  0.6 16.8 %copy-start.1 = (f32[2,512,128]{2,1,0:T(8,128)S(1)}, f32[2,512,128]{2,1,0:T(8,128)}, u32[]{:S(2)}) copy-start(f32[2,512,128]{2,1,0:T(8,128)} %param.13) | copy-start | bytes 1572868
  1.9 6.6 %collective-permute-start.20 = (f32[2,128,128]{2,1,0:T(8,128)S(1)}, f32[2,128,128]{2,1,0:T(8,128)S(1)}, u32[]{:S(2)}, u32[]{:S(2)}) collective-permute-start(f32[2,128,128]{2,1,0:T(8,128)S(1)} %get-tuple-element.37), channel_id=1, source_target_pairs={{0,16},{4,20},{8,24},{12,28},{16,0},{20,4},{24,8},{28,12},{1,17},{... | collective-permute-start | bytes 393224 | tf_op jit(solution)/shard_map/ppermute | solution.py:351
  4.9 6.4 %collective-permute-start.19 = (f32[2,128,128]{2,1,0:T(8,128)S(1)}, f32[2,128,128]{2,1,0:T(8,128)S(1)}, u32[]{:S(2)}, u32[]{:S(2)}) collective-permute-start(f32[2,128,128]{2,1,0:T(8,128)S(1)} %get-tuple-element.38), channel_id=1, source_target_pairs={{0,8},{4,12},{8,0},{12,4},{16,24},{20,28},{24,16},{28,20},{1,9},{5... | collective-permute-start | bytes 393224 | tf_op jit(solution)/shard_map/ppermute | solution.py:351
  6.4 7.3 %collective-permute-start.21 = (f32[2,128,128]{2,1,0:T(8,128)S(1)}, f32[2,128,128]{2,1,0:T(8,128)S(1)}, u32[]{:S(2)}, u32[]{:S(2)}) collective-permute-start(f32[2,128,128]{2,1,0:T(8,128)S(1)} %get-tuple-element.39), channel_id=1, source_target_pairs={{0,24},{4,28},{8,16},{12,20},{16,8},{20,12},{24,0},{28,4},{1,25},{... | collective-permute-start | bytes 393224 | tf_op jit(solution)/shard_map/ppermute | solution.py:351
  6.5 25.1 %collective-permute-start.6 = (f32[2,512,128]{2,1,0:T(8,128)}, f32[2,512,128]{2,1,0:T(8,128)S(1)}, u32[]{:S(2)}, u32[]{:S(2)}) collective-permute-start(f32[2,512,128]{2,1,0:T(8,128)} %param.13), channel_id=1, source_target_pairs={{0,8},{4,12},{8,0},{12,4},{16,24},{20,28},{24,16},{28,20},{1,9},{5... | collective-permute-start | bytes 1572872 | tf_op jit(solution)/shard_map/ppermute | solution.py:351
  13.8 7.5 %collective-permute-start.24 = (f32[2,128,128]{2,1,0:T(8,128)S(1)}, f32[2,128,128]{2,1,0:T(8,128)S(1)}, u32[]{:S(2)}, u32[]{:S(2)}) collective-permute-start(f32[2,128,128]{2,1,0:T(8,128)S(1)} %get-tuple-element.33), channel_id=1, source_target_pairs={{0,3},{1,0},{2,1},{3,2},{4,7},{5,4},{6,5},{7,6},{8,11},{9,8},{10,9... | collective-permute-start | bytes 393224 | tf_op jit(solution)/shard_map/ppermute | solution.py:354
  17.4 18.8 %collective-permute-start.8 = (f32[2,512,128]{2,1,0:T(8,128)S(1)}, f32[2,512,128]{2,1,0:T(8,128)S(1)}, u32[]{:S(2)}, u32[]{:S(2)}) collective-permute-start(f32[2,512,128]{2,1,0:T(8,128)S(1)} %copy-done.1), channel_id=1, source_target_pairs={{0,24},{4,28},{8,16},{12,20},{16,8},{20,12},{24,0},{28,4},{1,25},{... | collective-permute-start | bytes 1572872 | tf_op jit(solution)/shard_map/ppermute | solution.py:351
  20.2 36.6 %collective-permute-start.7 = (f32[2,512,128]{2,1,0:T(8,128)S(1)}, f32[2,512,128]{2,1,0:T(8,128)S(1)}, u32[]{:S(2)}, u32[]{:S(2)}) collective-permute-start(f32[2,512,128]{2,1,0:T(8,128)S(1)} %copy-done.1), channel_id=1, source_target_pairs={{0,16},{4,20},{8,24},{12,28},{16,0},{20,4},{24,8},{28,12},{1,17},{... | collective-permute-start | bytes 1572872 | tf_op jit(solution)/shard_map/ppermute | solution.py:351
  20.8 5.9 %collective-permute-start.23 = (f32[2,128,128]{2,1,0:T(8,128)S(1)}, f32[2,128,128]{2,1,0:T(8,128)S(1)}, u32[]{:S(2)}, u32[]{:S(2)}) collective-permute-start(f32[2,128,128]{2,1,0:T(8,128)S(1)} %get-tuple-element.34), channel_id=1, source_target_pairs={{0,2},{1,3},{2,0},{3,1},{4,6},{5,7},{6,4},{7,5},{8,10},{9,11},{10,... | collective-permute-start | bytes 393224 | tf_op jit(solution)/shard_map/ppermute | solution.py:354
  21.3 7.2 %collective-permute-start.22 = (f32[2,128,128]{2,1,0:T(8,128)S(1)}, f32[2,128,128]{2,1,0:T(8,128)S(1)}, u32[]{:S(2)}, u32[]{:S(2)}) collective-permute-start(f32[2,128,128]{2,1,0:T(8,128)S(1)} %get-tuple-element.35), channel_id=1, source_target_pairs={{0,1},{1,2},{2,3},{3,0},{4,5},{5,6},{6,7},{7,4},{8,9},{9,10},{10,1... | collective-permute-start | bytes 393224 | tf_op jit(solution)/shard_map/ppermute | solution.py:354
  28.6 29.7 %collective-permute-start.27 = (f32[4,2,128,128]{3,2,1,0:T(8,128)S(1)}, f32[4,2,128,128]{3,2,1,0:T(8,128)S(1)}, u32[]{:S(2)}, u32[]{:S(2)}) collective-permute-start(f32[4,2,128,128]{3,2,1,0:T(8,128)S(1)} %pad_maximum_fusion.3), channel_id=1, source_target_pairs={{0,24},{4,28},{8,16},{12,20},{16,8},{20,12},{24,0},{28,4},{1,25},{... | collective-permute-start | bytes 1572872 | tf_op jit(solution)/shard_map/ppermute | solution.py:351
  30.4 33.8 %collective-permute-start.26 = (f32[4,2,128,128]{3,2,1,0:T(8,128)S(1)}, f32[4,2,128,128]{3,2,1,0:T(8,128)S(1)}, u32[]{:S(2)}, u32[]{:S(2)}) collective-permute-start(f32[4,2,128,128]{3,2,1,0:T(8,128)S(1)} %pad_maximum_fusion.3), channel_id=1, source_target_pairs={{0,16},{4,20},{8,24},{12,28},{16,0},{20,4},{24,8},{28,12},{1,17},{... | collective-permute-start | bytes 1572872 | tf_op jit(solution)/shard_map/ppermute | solution.py:351
  31.6 32.7 %collective-permute-start.25 = (f32[4,2,128,128]{3,2,1,0:T(8,128)S(1)}, f32[4,2,128,128]{3,2,1,0:T(8,128)S(1)}, u32[]{:S(2)}, u32[]{:S(2)}) collective-permute-start(f32[4,2,128,128]{3,2,1,0:T(8,128)S(1)} %pad_maximum_fusion.3), channel_id=1, source_target_pairs={{0,8},{4,12},{8,0},{12,4},{16,24},{20,28},{24,16},{28,20},{1,9},{5... | collective-permute-start | bytes 1572872 | tf_op jit(solution)/shard_map/ppermute | solution.py:351
  58.3 79.8 %collective-permute-start.9 = (f32[4,2,512,128]{3,2,1,0:T(8,128)}, f32[4,2,512,128]{3,2,1,0:T(8,128)}, u32[]{:S(2)}, u32[]{:S(2)}) collective-permute-start(f32[4,2,512,128]{3,2,1,0:T(8,128)} %pad_maximum_fusion.refs_4_), channel_id=1, source_target_pairs={{0,4},{4,0},{8,12},{12,8},{16,20},{20,16},{24,28},{28,24},{1,5},{5... | collective-permute-start | bytes 6291464 | tf_op jit(solution)/shard_map/ppermute | solution.py:351
  64.2 1.0 copy-start.2
  64.2 2.2 %copy-start.6 = (f32[1,512,128]{2,1,0:T(8,128)S(1)}, f32[1,512,128]{2,1,0:T(8,128)}, u32[]{:S(2)}) copy-start(f32[1,512,128]{2,1,0:T(8,128)} %param.11) | copy-start | bytes 786436
  64.5 44.9 %copy-start = (f32[4,4,2,128,128]{4,3,2,1,0:T(8,128)}, f32[4,4,2,128,128]{4,3,2,1,0:T(8,128)S(1)}, u32[]{:S(2)}) copy-start(f32[4,4,2,128,128]{4,3,2,1,0:T(8,128)S(1)} %pad_maximum_fusion.1.mine) | copy-start | bytes 6291460
  64.5 82.8 %collective-permute-start.28 = (f32[4,4,2,128,128]{4,3,2,1,0:T(8,128)S(1)}, f32[4,4,2,128,128]{4,3,2,1,0:T(8,128)}, u32[]{:S(2)}, u32[]{:S(2)}) collective-permute-start(f32[4,4,2,128,128]{4,3,2,1,0:T(8,128)S(1)} %pad_maximum_fusion.1.mine), channel_id=1, source_target_pairs={{0,4},{4,0},{8,12},{12,8},{16,20},{20,16},{24,28},{28,24},{1,5},{5... | collective-permute-start | bytes 6291464 | tf_op jit(solution)/shard_map/ppermute | solution.py:351
  65.2 10.0 %collective-permute-start.18 = (f32[512,128]{1,0:T(8,128)S(1)}, f32[512,128]{1,0:T(8,128)S(1)}, u32[]{:S(2)}, u32[]{:S(2)}) collective-permute-start(f32[512,128]{1,0:T(8,128)S(1)} %bitcast.57), channel_id=1, source_target_pairs={{1,0},{2,1},{3,2},{5,4},{6,5},{7,6},{9,8},{10,9},{11,10},{13,12},{... | collective-permute-start | bytes 786440 | tf_op jit(solution)/shard_map/ppermute | solution.py:354
  66.5 10.2 %collective-permute-start.2 = (f32[512,128]{1,0:T(8,128)S(1)}, f32[512,128]{1,0:T(8,128)S(1)}, u32[]{:S(2)}, u32[]{:S(2)}) collective-permute-start(f32[512,128]{1,0:T(8,128)S(1)} %bitcast.72), channel_id=1, source_target_pairs={{0,3},{4,7},{8,11},{12,15},{16,19},{20,23},{24,27},{28,31}} | collective-permute-start | bytes 786440 | tf_op jit(solution)/shard_map/ppermute | solution.py:354
  69.9 13.0 %collective-permute-start.1 = (f32[512,128]{1,0:T(8,128)S(1)}, f32[512,128]{1,0:T(8,128)}, u32[]{:S(2)}, u32[]{:S(2)}) collective-permute-start(f32[512,128]{1,0:T(8,128)S(1)} %bitcast.73), channel_id=1, source_target_pairs={{0,2},{1,3},{4,6},{5,7},{8,10},{9,11},{12,14},{13,15},{16,18},{17,... | collective-permute-start | bytes 786440 | tf_op jit(solution)/shard_map/ppermute | solution.py:354
  75.1 12.7 %collective-permute-start = (f32[512,128]{1,0:T(8,128)S(1)}, f32[512,128]{1,0:T(8,128)S(1)}, u32[]{:S(2)}, u32[]{:S(2)}) collective-permute-start(f32[512,128]{1,0:T(8,128)S(1)} %bitcast.74), channel_id=1, source_target_pairs={{0,1},{1,2},{2,3},{4,5},{5,6},{6,7},{8,9},{9,10},{10,11},{12,13},{... | collective-permute-start | bytes 786440 | tf_op jit(solution)/shard_map/ppermute | solution.py:354
  76.6 6.3 %copy-start.7 = (f32[512,128]{1,0:T(8,128)}, f32[512,128]{1,0:T(8,128)S(1)}, u32[]{:S(2)}) copy-start(f32[512,128]{1,0:T(8,128)S(1)} %collective-permute-done.2.refs_3_) | copy-start | bytes 786436
  76.6 32.7 %collective-permute-start.17 = (f32[512,128]{1,0:T(8,128)S(1)}, f32[512,128]{1,0:T(8,128)S(1)}, u32[]{:S(2)}, u32[]{:S(2)}) collective-permute-start(f32[512,128]{1,0:T(8,128)S(1)} %bitcast.58), channel_id=1, source_target_pairs={{0,3},{4,7},{8,11},{12,15},{16,19},{20,23},{24,27},{28,31}} | collective-permute-start | bytes 786440 | tf_op jit(solution)/shard_map/ppermute | solution.py:354
  82.9 27.8 %collective-permute-start.16 = (f32[512,128]{1,0:T(8,128)S(1)}, f32[512,128]{1,0:T(8,128)S(1)}, u32[]{:S(2)}, u32[]{:S(2)}) collective-permute-start(f32[512,128]{1,0:T(8,128)S(1)} %bitcast.59), channel_id=1, source_target_pairs={{2,0},{3,1},{6,4},{7,5},{10,8},{11,9},{14,12},{15,13},{18,16},{19,... | collective-permute-start | bytes 786440 | tf_op jit(solution)/shard_map/ppermute | solution.py:354
  87.9 0.7 copy-start.8
  88.6 34.6 %collective-permute-start.15 = (f32[512,128]{1,0:T(8,128)S(1)}, f32[512,128]{1,0:T(8,128)S(1)}, u32[]{:S(2)}, u32[]{:S(2)}) collective-permute-start(f32[512,128]{1,0:T(8,128)S(1)} %bitcast.60), channel_id=1, source_target_pairs={{0,2},{1,3},{4,6},{5,7},{8,10},{9,11},{12,14},{13,15},{16,18},{17,... | collective-permute-start | bytes 786440 | tf_op jit(solution)/shard_map/ppermute | solution.py:354
  109.4 15.8 %collective-permute-start.3 = (f32[128,512]{1,0:T(8,128)}, f32[128,512]{1,0:T(8,128)}, u32[]{:S(2)}, u32[]{:S(2)}) collective-permute-start(f32[128,512]{1,0:T(8,128)} %get-tuple-element.18), channel_id=1, source_target_pairs={{1,0},{2,1},{3,2},{5,4},{6,5},{7,6},{9,8},{10,9},{11,10},{13,12},{... | collective-permute-start | bytes 786440 | tf_op jit(solution)/shard_map/ppermute | solution.py:354
  110.7 18.0 %collective-permute-start.4 = (f32[128,512]{1,0:T(8,128)}, f32[128,512]{1,0:T(8,128)}, u32[]{:S(2)}, u32[]{:S(2)}) collective-permute-start(f32[128,512]{1,0:T(8,128)} %get-tuple-element.19), channel_id=1, source_target_pairs={{2,0},{3,1},{6,4},{7,5},{10,8},{11,9},{14,12},{15,13},{18,16},{19,... | collective-permute-start | bytes 786440 | tf_op jit(solution)/shard_map/ppermute | solution.py:354
  123.1 14.9 %collective-permute-start.5 = (f32[128,512]{1,0:T(8,128)}, f32[128,512]{1,0:T(8,128)}, u32[]{:S(2)}, u32[]{:S(2)}) collective-permute-start(f32[128,512]{1,0:T(8,128)} %get-tuple-element.20), channel_id=1, source_target_pairs={{3,0},{7,4},{11,8},{15,12},{19,16},{23,20},{27,24},{31,28}} | collective-permute-start | bytes 786440 | tf_op jit(solution)/shard_map/ppermute | solution.py:354
  125.2 17.6 %collective-permute-start.14 = (f32[512,128]{1,0:T(8,128)S(1)}, f32[512,128]{1,0:T(8,128)S(1)}, u32[]{:S(2)}, u32[]{:S(2)}) collective-permute-start(f32[512,128]{1,0:T(8,128)S(1)} %bitcast.61), channel_id=1, source_target_pairs={{3,0},{7,4},{11,8},{15,12},{19,16},{23,20},{27,24},{31,28}} | collective-permute-start | bytes 786440 | tf_op jit(solution)/shard_map/ppermute | solution.py:354
  128.7 17.8 %collective-permute-start.13 = (f32[512,128]{1,0:T(8,128)S(1)}, f32[512,128]{1,0:T(8,128)}, u32[]{:S(2)}, u32[]{:S(2)}) collective-permute-start(f32[512,128]{1,0:T(8,128)S(1)} %bitcast.62), channel_id=1, source_target_pairs={{0,1},{1,2},{2,3},{4,5},{5,6},{6,7},{8,9},{9,10},{10,11},{12,13},{... | collective-permute-start | bytes 786440 | tf_op jit(solution)/shard_map/ppermute | solution.py:354
  142.7 11.2 %collective-permute-start.10 = (f32[4,128,128]{2,1,0:T(8,128)}, f32[4,128,128]{2,1,0:T(8,128)S(1)}, u32[]{:S(2)}, u32[]{:S(2)}) collective-permute-start(f32[4,128,128]{2,1,0:T(8,128)} %get-tuple-element.22), channel_id=1, source_target_pairs={{0,1},{1,2},{2,3},{3,0},{4,5},{5,6},{6,7},{7,4},{8,9},{9,10},{10,1... | collective-permute-start | bytes 786440 | tf_op jit(solution)/shard_map/ppermute | solution.py:354
  142.7 18.8 %collective-permute-start.11 = (f32[4,128,128]{2,1,0:T(8,128)}, f32[4,128,128]{2,1,0:T(8,128)S(1)}, u32[]{:S(2)}, u32[]{:S(2)}) collective-permute-start(f32[4,128,128]{2,1,0:T(8,128)} %get-tuple-element.23), channel_id=1, source_target_pairs={{0,2},{1,3},{2,0},{3,1},{4,6},{5,7},{6,4},{7,5},{8,10},{9,11},{10,... | collective-permute-start | bytes 786440 | tf_op jit(solution)/shard_map/ppermute | solution.py:354
  142.8 18.7 %collective-permute-start.12 = (f32[4,128,128]{2,1,0:T(8,128)}, f32[4,128,128]{2,1,0:T(8,128)S(1)}, u32[]{:S(2)}, u32[]{:S(2)}) collective-permute-start(f32[4,128,128]{2,1,0:T(8,128)} %get-tuple-element.24), channel_id=1, source_target_pairs={{0,3},{1,0},{2,1},{3,2},{4,7},{5,4},{6,5},{7,6},{8,11},{9,8},{10,9... | collective-permute-start | bytes 786440 | tf_op jit(solution)/shard_map/ppermute | solution.py:354
  153.9 7.5 %copy-start.3 = (f32[4,128,128]{2,1,0:T(8,128)}, f32[4,128,128]{2,1,0:T(8,128)S(1)}, u32[]{:S(2)}) copy-start(f32[4,128,128]{2,1,0:T(8,128)S(1)} %collective-permute-done.10.refs_1_) | copy-start | bytes 786436
  161.4 0.7 copy-start.4
  161.4 0.8 copy-start.5

commit v4 on v3

--- a/solution.py
+++ b/solution.py
@@ -168,32 +168,35 @@
     )(at, mine, other, sketch)
 
 
-def solve_kernel(n_col, at, diag, *refs):
+def solve_kernel(n_col, at, diag, own_u, *refs):
     xs, outs = refs[:n_col], refs[n_col:]
     c = at[1]
     rows = diag.shape[0]
     solved = None
     for d in range(n_col):
         cols = pl.ds(pl.multiple_of(jnp.maximum(c - d, 0) * rows, rows), rows)
-        part = product(diag[:, cols], xs[d][...])
+        x = xs[d][...] if d == 0 else jnp.where(c >= d, xs[d][...], 0.0)
+        part = product(diag[:, cols], x)
         solved = part if solved is None else solved + part
     for d in range(n_col):
         cols = pl.ds(pl.multiple_of(jnp.maximum(c - d, 0) * rows, rows), rows)
-        outs[d][...] = product_tn(solved, diag[:, cols])
-
-
-def solve(at, diag, xs):
+        x = product_tn(solved, diag[:, cols]).T
+        outs[d][...] = x if d == 0 else jnp.where(c >= d, x, own_u[...])
+
+
+def solve(at, diag, own_u, xs):
     n_col = len(xs)
     rows, k = xs[0].shape
     vmem = pl.BlockSpec(memory_space=VMEM)
     return pl.pallas_call(
         functools.partial(solve_kernel, n_col),
-        in_specs=[pl.BlockSpec(memory_space=pltpu.SMEM)] + [vmem] * (1 + n_col),
+        in_specs=[pl.BlockSpec(memory_space=pltpu.SMEM)] + [vmem] * (2 + n_col),
         out_specs=[vmem] * n_col,
-        out_shape=[jax.ShapeDtypeStruct((k, rows), f32)] * n_col,
+        out_shape=[jax.ShapeDtypeStruct((rows, k), f32)] * n_col,
+        compiler_params=pltpu.CompilerParams(vmem_limit_bytes=32 * 1024 * 1024),
         cost_estimate=pl.CostEstimate(flops=12 * n_col * rows * rows * k, bytes_accessed=4 * n_col * rows * rows, transcendentals=0),
         name="solve",
-    )(at, diag, *xs)
+    )(at, diag, own_u, *xs)
 
 
 def cores_kernel(n_col, at, *refs):
@@ -201,9 +204,9 @@
     r, c = at[0], at[1]
     chip, core = lax.shift_right_logical(r, 1), lax.rem(r, 2)
     total = parts[0][...]
-    for p in parts[1:]:
-        total = total + p[...]
-    lhs = beside(total)
+    for d in range(1, n_col):
+        total = total + jnp.where(c + d < n_col, parts[d][...], 0.0)
+    lhs = beside(total.T)
     pair = mine.shape[1]
     for d in range(n_col):
         e = chip ^ lax.rem(c + d, n_col)
@@ -214,7 +217,7 @@
 
 def partial_cores(at, parts, mine, other):
     n_col = len(parts)
-    k, rows = parts[0].shape
+    rows, k = parts[0].shape
     pair = mine.shape[1]
     vmem = pl.BlockSpec(memory_space=VMEM)
     return pl.pallas_call(
@@ -222,22 +225,25 @@
         in_specs=[pl.BlockSpec(memory_space=pltpu.SMEM)] + [vmem] * (n_col + 2),
         out_specs=[vmem] * n_col,
         out_shape=[jax.ShapeDtypeStruct((2 * pair, k, k), f32)] * n_col,
+        compiler_params=pltpu.CompilerParams(vmem_limit_bytes=32 * 1024 * 1024),
         cost_estimate=pl.CostEstimate(flops=12 * n_col * pair * rows * k * k, bytes_accessed=8 * n_col * pair * rows * k, transcendentals=0),
         name="partial_cores",
     )(at, *parts, mine, other)
 
 
 def recompress_kernel(tiles, n, k, n_col, at, *refs):
-    core_parts, row_us = refs[:n_col], refs[n_col : 2 * n_col]
-    small, base, u_parts, v_parts, w_parts, new_u, new_v = refs[2 * n_col : 2 * n_col + 7]
-    s, tu, tv, cu, sp, out, ru, work, cross, cores, row_parts, sem, row_sem = refs[2 * n_col + 7 :]
+    core_parts, first, second = refs[:n_col], refs[n_col : 2 * n_col], refs[2 * n_col : 3 * n_col]
+    small, base, u_parts, v_parts, w_parts, new_u, new_v = refs[3 * n_col : 3 * n_col + 7]
+    s, tu, tv, cu, sp, out, ru, work, cross, cores, row_parts, sem, row_sem = refs[3 * n_col + 7 :]
     c = at[1]
     root = math.sqrt(n)
     blk = n // n_col
     row_copies = []
     for d in range(n_col):
         rows = pl.ds(pl.multiple_of(block_of(c, d, n_col) * blk, blk), blk)
-        row_copies.append(pltpu.make_async_copy(row_us[d], ru.at[rows], row_sem.at[d]))
+        row_copies.append(tuple(
+            pltpu.make_async_copy(x, ru.at[rows], row_sem.at[d]) for x in (first[d], second[(n_col - d) % n_col])
+        ))
     early, late, outs = [], [], []
     for t in range(tiles):
         early.append((
@@ -252,8 +258,10 @@
             pltpu.make_async_copy(s.at[t], new_u.at[t], sem.at[4 * tiles + t]),
             pltpu.make_async_copy(out.at[t], new_v.at[t], sem.at[5 * tiles + t]),
         ))
-    for x in row_copies:
-        x.start()
+    row_copies[0][0].start()
+    for d in range(1, n_col):
+        pl.when(c < d)(row_copies[d][0].start)
+        pl.when(c >= d)(row_copies[d][1].start)
     for x in early[0] + early[1]:
         x.start()
     total = core_parts[0][...]
@@ -261,7 +269,7 @@
         total = total + p[...]
     cores[...] = total
     for x in row_copies:
-        x.wait()
+        x[0].wait()
 
     def split(at):
         row_parts[at, :] = beside(ru[at, :])
@@ -318,7 +326,7 @@
             x.wait()
 
 
-def recompress(at, core_parts, row_us, small, base, u_parts, v_parts, w_parts):
+def recompress(at, core_parts, first, second, small, base, u_parts, v_parts, w_parts):
     tiles, n, k = base.shape
     n_col = len(core_parts)
     any_ = pl.BlockSpec(memory_space=ANY)
@@ -327,7 +335,7 @@
     split = lambda: VMEM((tiles, n, 2 * k), bf16)
     return pl.pallas_call(
         functools.partial(recompress_kernel, tiles, n, k, n_col),
-        in_specs=[pl.BlockSpec(memory_space=pltpu.SMEM)] + [vmem] * n_col + [any_] * n_col + [vmem] + [any_] * 4,
+        in_specs=[pl.BlockSpec(memory_space=pltpu.SMEM)] + [vmem] * n_col + [any_] * (2 * n_col) + [vmem] + [any_] * 4,
         out_specs=[any_, any_],
         out_shape=[jax.ShapeDtypeStruct(base.shape, f32)] * 2,
         scratch_shapes=[
@@ -338,7 +346,7 @@
         ],
         cost_estimate=pl.CostEstimate(flops=24 * tiles * n * k * k, bytes_accessed=28 * tiles * n * k, transcendentals=0),
         name="recompress",
-    )(at, *core_parts, *row_us, small, base, u_parts, v_parts, w_parts)
+    )(at, *core_parts, *first, *second, small, base, u_parts, v_parts, w_parts)
 
 
 def step(n_row, n_col, tile_u, tile_v, row_panel_u, row_panel_v, col_panel_u, col_panel_v, diag_inverse, sketch):
@@ -353,25 +361,16 @@
     def shift(x, pairs):
         return lax.ppermute(x, "col", pairs)
 
-    def up(x, d):
-        return shift(x, [(a, a + d) for a in range(n_col - d)])
-
-    def down(x, d):
-        return shift(x, [(a, a - d) for a in range(d, n_col)])
-
     def around(x, d):
         return shift(x, [(a, (a + d) % n_col) for a in range(n_col)])
 
     def pick(x, i, axis=0):
         return lax.dynamic_index_in_dim(x, i, axis, keepdims=False)
 
-    row_v = row_panel_v[0]
-    below = [row_v] + [up(row_v, d) for d in range(1, n_col)]
+    row_v, row_u = row_panel_v[0], row_panel_u[0]
+    loads = [jnp.where(c + d < n_col, row_v, row_u) for d in range(1, n_col)]
+    first = [around(x, d) for d, x in enumerate(loads, 1)]
     col_v_mine = jnp.stack([col_panel_v] + [partner(col_panel_v, 2 * e) for e in range(1, chips)])
-    row_u = row_panel_u[0]
-    rises = [up(row_u, d) for d in range(1, n_col)]
-    falls = [down(row_u, d) for d in range(1, n_col)]
-    row_us = [row_u] + [jnp.where(c >= d, rises[d - 1], falls[n_col - d - 1]) for d in range(1, n_col)]
     pair, rows, k = col_panel_u.shape
     cut = col_panel_u.reshape(pair, chips, rows // chips, k)
     cuts = jnp.stack([pick(cut, chip, 1)] + [partner(pick(cut, chip ^ e, 1), 2 * e) for e in range(1, chips)])
@@ -379,15 +378,15 @@
     moved = [pick(cuts, chip ^ c)] + [around(pick(cuts, chip ^ lax.rem(c + d, n_col)), d) for d in range(1, n_col)]
     planes = lax.optimization_barrier(jnp.stack(moved))
     base, u_parts, v_parts = sketch_tiles(tile_u[0], tile_v[0], sketch)
-    sums = solve(at, diag_inverse, below)
-    parts = [sums[0]] + [down(sums[d], d) for d in range(1, n_col)]
+    sums = solve(at, diag_inverse, row_u, [row_v] + first)
+    second = [around(sums[d], n_col - d) for d in range(1, n_col)]
     gathered = [planes] + [partner(planes, 2 * e) for e in range(1, chips)]
     col_u_mine = jnp.stack(gathered)
     col_u_other = partner(col_u_mine, 1)
     w_parts, small = project(n_col, at, col_u_mine, col_u_other, sketch)
-    cores = partial_cores(at, parts, col_v_mine, col_v_other)
+    cores = partial_cores(at, [sums[0]] + second, col_v_mine, col_v_other)
     core_parts = [cores[0]] + [around(cores[d], d) for d in range(1, n_col)]
-    new_u, new_v = recompress(at, core_parts, row_us, small, base, u_parts, v_parts, w_parts)
+    new_u, new_v = recompress(at, core_parts, [row_u] + first, [row_u] + second, small, base, u_parts, v_parts, w_parts)
     return new_u[None], new_v[None]
 
 

time: 190 us -> 175 us (0.921)
  starting transfers between devices: 60.4 us -> 31.5 us
  waiting for transfers between devices: 66.5 us -> 86.4 us
  Pallas kernels: 51.3 us -> 47.1 us
  other arithmetic: 4.6 us -> 1.82 us
    ppermute x18 -> x12, starting transfers between devices: 47 us -> 18.1 us  [shift(): return lax.ppermute(x, 'col', pairs)]
    ppermute x18 -> x12, waiting for transfers between devices: 30.6 us -> 49.3 us  [shift(): return lax.ppermute(x, 'col', pairs)]
    pallas_call x1, Pallas kernels: 5.67 us -> 3.11 us  [solve(): pl.pallas_call(functools.partial(solve_kernel, n_col), in_specs=[pl.Block...]
    select_n x3 -> x1, other arithmetic: 2.25 us -> 0.06 us  [step(): loads = [jnp.where(c + d < n_col, row_v, row_u) for d in range(1, n_col)]]
    unnamed x18 -> x30, local copies, waits for them, and re-layouts: 2.17 us -> 3.87 us
  transfers between devices with their start and end apart: 29 -> 23, of which waited for: 14 -> 12; matrix products, arithmetic and copies ran while one was open for 2% -> 1% of each run, Pallas kernels for 14% -> 13%
where the time goes in v4:
time: 175 us; the launch traced here: 173 us
  waiting for transfers between devices  86.4 us (49%)
  Pallas kernels  47.1 us (27%)
  starting transfers between devices  31.5 us (18%)
  local copies, waits for them, and re-layouts  5.11 us (3%)
  other arithmetic  1.82 us (1%)
    ppermute x12, waiting for transfers between devices, shift(): return lax.ppermute(x, 'col', pairs)  49.3 us
    ppermute x11, waiting for transfers between devices, partner(): return lax.ppermute(x, 'row', [(a, a ^ m) for a in range(n_row)])  37.1 us
    pallas_call x1, Pallas kernels, recompress(): pl.pallas_call(functools.partial(recompress_kernel, tiles, n, k, n_col),...  24.5 us
    ppermute x12, starting transfers between devices, shift(): return lax.ppermute(x, 'col', pairs)  18.1 us
    ppermute x11, starting transfers between devices, partner(): return lax.ppermute(x, 'row', [(a, a ^ m) for a in range(n_row)])  13.5 us
    pallas_call x1, Pallas kernels, sketch_tiles(): pl.pallas_call(sketched, grid=(tiles,), in_specs=[block, block, pl.BlockS...  11.1 us
    pallas_call x1, Pallas kernels, project(): pl.pallas_call(functools.partial(project_kernel, n_col), in_specs=[pl.Blo...  5.07 us
    unnamed x30, local copies, waits for them, and re-layouts  3.87 us
  transfers between devices with their start and end apart: 23, of which 12 were waited for; matrix products, arithmetic and copies ran while one was open for 1% of the time, Pallas kernels for 13%

profile of v4, /device:TPU:0, one launch (start us, length us, event | category | flops | bytes accessed | tf_op | source)
XLA Modules:
  0.0 173.0 jit_solution(10621636730398637454)
XLA Ops:
  0.6 0.0 copy-start.11
  0.7 1.2 dynamic-slice_bitcast_fusion.6
  1.9 3.1 %collective-permute-start.14 = (f32[2,128,128]{2,1,0:T(8,128)S(1)}, f32[2,128,128]{2,1,0:T(8,128)S(1)}, u32[]{:S(2)}, u32[]{:S(2)}) collective-permute-start(f32[2,128,128]{2,1,0:T(8,128)S(1)} %get-tuple-element.37), channel_id=1, source_target_pairs={{0,16},{4,20},{8,24},{12,28},{16,0},{20,4},{24,8},{28,12},{1,17},{... | collective-permute-start | bytes 393224 | tf_op jit(solution)/shard_map/ppermute | solution.py:359
  4.9 1.5 collective-permute-start.13
  6.4 0.0 collective-permute-start.15
  6.5 1.9 %collective-permute-start.6 = (f32[2,512,128]{2,1,0:T(8,128)}, f32[2,512,128]{2,1,0:T(8,128)S(1)}, u32[]{:S(2)}, u32[]{:S(2)}) collective-permute-start(f32[2,512,128]{2,1,0:T(8,128)} %param.13), channel_id=1, source_target_pairs={{0,8},{4,12},{8,0},{12,4},{16,24},{20,28},{24,16},{28,20},{1,9},{5... | collective-permute-start | bytes 1572872 | tf_op jit(solution)/shard_map/ppermute | solution.py:359
  8.4 0.0 collective-permute-done.14
  8.4 2.9 %collective-permute-done.13 = f32[2,128,128]{2,1,0:T(8,128)S(1)} collective-permute-done((f32[2,128,128]{2,1,0:T(8,128)S(1)}, f32[2,128,128]{2,1,0:T(8,128)S(1)}, u32[]{:S(2)}, u32[]{:S(2)}) %collective-permute-start.13) | collective-permute-done | bytes 131104 | tf_op jit(solution)/shard_map/ppermute | solution.py:359
  11.3 2.4 %collective-permute-done.15 = f32[2,128,128]{2,1,0:T(8,128)S(1)} collective-permute-done((f32[2,128,128]{2,1,0:T(8,128)S(1)}, f32[2,128,128]{2,1,0:T(8,128)S(1)}, u32[]{:S(2)}, u32[]{:S(2)}) %collective-permute-start.15) | collective-permute-done | bytes 131104 | tf_op jit(solution)/shard_map/ppermute | solution.py:359
  13.8 3.7 %collective-permute-start.18 = (f32[2,128,128]{2,1,0:T(8,128)S(1)}, f32[2,128,128]{2,1,0:T(8,128)S(1)}, u32[]{:S(2)}, u32[]{:S(2)}) collective-permute-start(f32[2,128,128]{2,1,0:T(8,128)S(1)} %get-tuple-element.33), channel_id=1, source_target_pairs={{0,3},{1,0},{2,1},{3,2},{4,7},{5,4},{6,5},{7,6},{8,11},{9,8},{10,9... | collective-permute-start | bytes 393224 | tf_op jit(solution)/shard_map/ppermute | solution.py:362
  17.4 0.0 copy-done.11
  17.4 2.8 %collective-permute-start.8 = (f32[2,512,128]{2,1,0:T(8,128)S(1)}, f32[2,512,128]{2,1,0:T(8,128)S(1)}, u32[]{:S(2)}, u32[]{:S(2)}) collective-permute-start(f32[2,512,128]{2,1,0:T(8,128)S(1)} %copy-done.11), channel_id=1, source_target_pairs={{0,24},{4,28},{8,16},{12,20},{16,8},{20,12},{24,0},{28,4},{1,25},{... | collective-permute-start | bytes 1572872 | tf_op jit(solution)/shard_map/ppermute | solution.py:359
  20.2 0.5 collective-permute-start.7
  20.8 0.0 collective-permute-start.17
  20.8 0.6 collective-permute-done.18
  21.3 1.0 collective-permute-start.16
  22.3 4.4 %collective-permute-done.17 = f32[2,128,128]{2,1,0:T(8,128)S(1)} collective-permute-done((f32[2,128,128]{2,1,0:T(8,128)S(1)}, f32[2,128,128]{2,1,0:T(8,128)S(1)}, u32[]{:S(2)}, u32[]{:S(2)}) %collective-permute-start.17) | collective-permute-done | bytes 131104 | tf_op jit(solution)/shard_map/ppermute | solution.py:362
  26.7 1.9 %collective-permute-done.16 = f32[2,128,128]{2,1,0:T(8,128)S(1)} collective-permute-done((f32[2,128,128]{2,1,0:T(8,128)S(1)}, f32[2,128,128]{2,1,0:T(8,128)S(1)}, u32[]{:S(2)}, u32[]{:S(2)}) %collective-permute-start.16) | collective-permute-done | bytes 131104 | tf_op jit(solution)/shard_map/ppermute | solution.py:362
  28.6 1.8 %collective-permute-start.21 = (f32[4,2,128,128]{3,2,1,0:T(8,128)S(1)}, f32[4,2,128,128]{3,2,1,0:T(8,128)S(1)}, u32[]{:S(2)}, u32[]{:S(2)}) collective-permute-start(f32[4,2,128,128]{3,2,1,0:T(8,128)S(1)} %pad_maximum_fusion.3), channel_id=1, source_target_pairs={{0,24},{4,28},{8,16},{12,20},{16,8},{20,12},{24,0},{28,4},{1,25},{... | collective-permute-start | bytes 1572872 | tf_op jit(solution)/shard_map/ppermute | solution.py:359
  30.4 1.1 collective-permute-start.20
  31.6 0.0 collective-permute-done.6
  31.6 0.6 collective-permute-start.19
  32.2 4.1 %collective-permute-done.8 = f32[2,512,128]{2,1,0:T(8,128)S(1)} collective-permute-done((f32[2,512,128]{2,1,0:T(8,128)S(1)}, f32[2,512,128]{2,1,0:T(8,128)S(1)}, u32[]{:S(2)}, u32[]{:S(2)}) %collective-permute-start.8) | collective-permute-done | bytes 524320 | tf_op jit(solution)/shard_map/ppermute | solution.py:359
  36.3 20.6 %collective-permute-done.7 = f32[2,512,128]{2,1,0:T(8,128)S(1)} collective-permute-done((f32[2,512,128]{2,1,0:T(8,128)S(1)}, f32[2,512,128]{2,1,0:T(8,128)S(1)}, u32[]{:S(2)}, u32[]{:S(2)}) %collective-permute-start.7) | collective-permute-done | bytes 524320 | tf_op jit(solution)/shard_map/ppermute | solution.py:359
  56.9 0.2 pad_maximum_fusion.refs_4_
  57.0 0.1 collective-permute-start.9
  57.1 0.0 collective-permute-done.21
  57.1 7.1 %collective-permute-done.20 = f32[4,2,128,128]{3,2,1,0:T(8,128)S(1)} collective-permute-done((f32[4,2,128,128]{3,2,1,0:T(8,128)S(1)}, f32[4,2,128,128]{3,2,1,0:T(8,128)S(1)}, u32[]{:S(2)}, u32[]{:S(2)}) %collective-permute-start.20) | collective-permute-done | bytes 524320 | tf_op jit(solution)/shard_map/ppermute | solution.py:359
  64.2 0.0 collective-permute-done.19
  64.2 1.5 pad_maximum_fusion.1.mine
  65.7 0.0 collective-permute-start.22
  65.7 0.1 broadcast_select_fusion
  65.8 0.5 collective-permute-start.2
  66.3 1.6 collective-permute-start
  67.8 0.0 collective-permute-start.1
  67.8 0.1 pad_add_fusion.at
  67.9 13.3 %collective-permute-done.2.refs_3_.refs_7_ = f32[512,128]{1,0:T(8,128)S(1)} collective-permute-done((f32[512,128]{1,0:T(8,128)S(1)}, f32[512,128]{1,0:T(8,128)S(1)}, u32[]{:S(2)}, u32[]{:S(2)}) %collective-permute-start.2) | collective-permute-done | bytes 262176 | tf_op jit(solution)/shard_map/ppermute | solution.py:362
  81.2 0.0 collective-permute-done.refs_1_.refs_5_
  81.2 8.1 %collective-permute-done.1.refs_2_.refs_6_ = f32[512,128]{1,0:T(8,128)S(1)} collective-permute-done((f32[512,128]{1,0:T(8,128)S(1)}, f32[512,128]{1,0:T(8,128)S(1)}, u32[]{:S(2)}, u32[]{:S(2)}) %collective-permute-start.1) | collective-permute-done | bytes 262176 | tf_op jit(solution)/shard_map/ppermute | solution.py:362
  89.3 2.3 %copy-done.10 = f32[512,2048]{1,0:T(8,128)S(1)} copy-done((f32[512,2048]{1,0:T(8,128)S(1)}, f32[512,2048]{1,0:T(8,128)}, u32[]{:S(2)}) %copy-start.10) | copy-done | bytes 4194328
  91.6 3.1 %solve.1 = (f32[512,128]{1,0:T(8,128)S(1)}, f32[512,128]{1,0:T(8,128)S(1)}, f32[512,128]{1,0:T(8,128)S(1)}, f32[512,128]{1,0:T(8,128)S(1)}) custom-call(s32[2]{0:T(128)S(1)} %pad_add_fusion.at, f32[512,2048]{1,0:T(8,128)S(1)} %copy-done.10, f32[512,128]{1,0:T(8,128)S(1)} %bitcast.53, f32[512,128]{1,0:T(8,128)S(1)} %bitcast.54, ...), custom_call_target="tpu_custom_call" | custom-call | flops 1610612736 | bytes 4194304 | tf_op jit(solution)/shard_map/solve/pallas_call | solution.py:191
  94.7 4.4 %collective-permute-start.3 = (f32[512,128]{1,0:T(8,128)S(1)}, f32[512,128]{1,0:T(8,128)S(1)}, u32[]{:S(2)}, u32[]{:S(2)}) collective-permute-start(f32[512,128]{1,0:T(8,128)S(1)} %get-tuple-element.18), channel_id=1, source_target_pairs={{0,3},{1,0},{2,1},{3,2},{4,7},{5,4},{6,5},{7,6},{8,11},{9,8},{10,9... | collective-permute-start | bytes 786440 | tf_op jit(solution)/shard_map/ppermute | solution.py:362
  99.1 0.0 collective-permute-start.4
  99.1 0.6 collective-permute-start.5
  99.8 6.1 %collective-permute-done.3.refs_1_.refs_9_ = f32[512,128]{1,0:T(8,128)S(1)} collective-permute-done((f32[512,128]{1,0:T(8,128)S(1)}, f32[512,128]{1,0:T(8,128)S(1)}, u32[]{:S(2)}, u32[]{:S(2)}) %collective-permute-start.3) | collective-permute-done | bytes 262176 | tf_op jit(solution)/shard_map/ppermute | solution.py:362
  105.9 15.0 %collective-permute-done.4.refs_2_.refs_10_ = f32[512,128]{1,0:T(8,128)S(1)} collective-permute-done((f32[512,128]{1,0:T(8,128)S(1)}, f32[512,128]{1,0:T(8,128)S(1)}, u32[]{:S(2)}, u32[]{:S(2)}) %collective-permute-start.4) | collective-permute-done | bytes 262176 | tf_op jit(solution)/shard_map/ppermute | solution.py:362
  120.9 0.0 collective-permute-done.5.refs_3_.refs_11_
  120.9 0.0 collective-permute-done.9.refs_5_
  120.9 3.3 %partial_cores.1 = (f32[4,128,128]{2,1,0:T(8,128)S(1)}, f32[4,128,128]{2,1,0:T(8,128)}, f32[4,128,128]{2,1,0:T(8,128)S(1)}, f32[4,128,128]{2,1,0:T(8,128)S(1)}) custom-call(s32[2]{0:T(128)S(1)} %pad_add_fusion.at, f32[512,128]{1,0:T(8,128)S(1)} %get-tuple-element.17.refs_0_, f32[512,128]{1,0:T(8,128)S(1)} %collective-permute-done.3.refs_1_.refs_9_, ...), custom_call_target="tpu_custom_call" | custom-call | flops 805306368 | bytes 4194304 | tf_op jit(solution)/shard_map/partial_cores/pallas_call | solution.py:223
  124.2 0.0 copy-done.2
  124.2 0.7 copy-done.7
  124.9 1.5 collective-permute-start.10
  126.4 1.9 %collective-permute-start.11 = (f32[4,128,128]{2,1,0:T(8,128)S(1)}, f32[4,128,128]{2,1,0:T(8,128)S(1)}, u32[]{:S(2)}, u32[]{:S(2)}) collective-permute-start(f32[4,128,128]{2,1,0:T(8,128)S(1)} %get-tuple-element.23), channel_id=1, source_target_pairs={{0,2},{1,3},{2,0},{3,1},{4,6},{5,7},{6,4},{7,5},{8,10},{9,11},{10,... | collective-permute-start | bytes 786440 | tf_op jit(solution)/shard_map/ppermute | solution.py:362
  128.3 2.9 %collective-permute-start.12 = (f32[4,128,128]{2,1,0:T(8,128)S(1)}, f32[4,128,128]{2,1,0:T(8,128)S(1)}, u32[]{:S(2)}, u32[]{:S(2)}) collective-permute-start(f32[4,128,128]{2,1,0:T(8,128)S(1)} %get-tuple-element.24), channel_id=1, source_target_pairs={{0,3},{1,0},{2,1},{3,2},{4,7},{5,4},{6,5},{7,6},{8,11},{9,8},{10,9... | collective-permute-start | bytes 786440 | tf_op jit(solution)/shard_map/ppermute | solution.py:362
  131.3 11.1 %sketch_tiles.1 = (f32[4,2048,128]{2,1,0:T(8,128)}, bf16[4,2048,256]{2,1,0:T(8,128)(2,1)}, bf16[4,2048,256]{2,1,0:T(8,128)(2,1)}) custom-call(f32[4,2048,128]{2,1,0:T(8,128)} %bitcast.55, f32[4,2048,128]{2,1,0:T(8,128)} %bitcast.56, f32[2048,128]{1,0:T(8,128)} %s_ref.3), custom_call_target="tpu_custom_call" | custom-call | flops 1610612736 | bytes 20971520 | tf_op jit(solution)/shard_map/sketch_tiles/pallas_call | solution.py:124
  142.4 0.0 collective-permute-done.22.other
  142.4 5.1 %project.1 = (bf16[4,2048,256]{2,1,0:T(8,128)(2,1)}, f32[4,128,128]{2,1,0:T(8,128)}) custom-call(s32[2]{0:T(128)} %copy-done.9, f32[4,4,2,128,128]{4,3,2,1,0:T(8,128)} %pad_maximum_fusion.1.mine, f32[4,4,2,128,128]{4,3,2,1,0:T(8,128)} %collective-permute-done.22.other, f32[2048,128]{1,0:T(8,128)} %s_ref.3), custom_call_target="tpu_custom_call" | custom-call | flops 805306368 | bytes 8388608 | tf_op jit(solution)/shard_map/project/pallas_call | solution.py:161
  147.4 0.0 collective-permute-done.10.refs_1_
  147.4 0.0 collective-permute-done.11.refs_2_
  147.5 0.0 collective-permute-done.12.refs_3_
  147.5 0.7 copy-done.12
  148.1 0.1 copy-done.13
  148.2 0.1 copy-done.14
  148.3 24.5 %recompress.1 = (f32[4,2048,128]{2,1,0:T(8,128)}, f32[4,2048,128]{2,1,0:T(8,128)}) custom-call(s32[2]{0:T(128)} %copy-done.9, f32[4,128,128]{2,1,0:T(8,128)} %copy-done.7, f32[4,128,128]{2,1,0:T(8,128)} %copy-done.12, f32[4,128,128]{2,1,0:T(8,128)} %copy-done.13, f32[4,128,128]{2,1,0:T(8,128)} %copy-done.14, f32[512,128]{1,0:T(8,128)} %bitcast.51, ...), custom_call_target="tpu_custom_call" | custom-call | flops 3221225472 | bytes 29360128 | tf_op jit(solution)/shard_map/recompress/pallas_call | solution.py:336
  (25 shorter events, 0.2 us)
Async XLA Ops:
  0.6 16.8 %copy-start.11 = (f32[2,512,128]{2,1,0:T(8,128)S(1)}, f32[2,512,128]{2,1,0:T(8,128)}, u32[]{:S(2)}) copy-start(f32[2,512,128]{2,1,0:T(8,128)} %param.13) | copy-start | bytes 1572868
  1.9 6.6 %collective-permute-start.14 = (f32[2,128,128]{2,1,0:T(8,128)S(1)}, f32[2,128,128]{2,1,0:T(8,128)S(1)}, u32[]{:S(2)}, u32[]{:S(2)}) collective-permute-start(f32[2,128,128]{2,1,0:T(8,128)S(1)} %get-tuple-element.37), channel_id=1, source_target_pairs={{0,16},{4,20},{8,24},{12,28},{16,0},{20,4},{24,8},{28,12},{1,17},{... | collective-permute-start | bytes 393224 | tf_op jit(solution)/shard_map/ppermute | solution.py:359
  4.9 6.4 %collective-permute-start.13 = (f32[2,128,128]{2,1,0:T(8,128)S(1)}, f32[2,128,128]{2,1,0:T(8,128)S(1)}, u32[]{:S(2)}, u32[]{:S(2)}) collective-permute-start(f32[2,128,128]{2,1,0:T(8,128)S(1)} %get-tuple-element.38), channel_id=1, source_target_pairs={{0,8},{4,12},{8,0},{12,4},{16,24},{20,28},{24,16},{28,20},{1,9},{5... | collective-permute-start | bytes 393224 | tf_op jit(solution)/shard_map/ppermute | solution.py:359
  6.4 7.3 %collective-permute-start.15 = (f32[2,128,128]{2,1,0:T(8,128)S(1)}, f32[2,128,128]{2,1,0:T(8,128)S(1)}, u32[]{:S(2)}, u32[]{:S(2)}) collective-permute-start(f32[2,128,128]{2,1,0:T(8,128)S(1)} %get-tuple-element.39), channel_id=1, source_target_pairs={{0,24},{4,28},{8,16},{12,20},{16,8},{20,12},{24,0},{28,4},{1,25},{... | collective-permute-start | bytes 393224 | tf_op jit(solution)/shard_map/ppermute | solution.py:359
  6.5 25.1 %collective-permute-start.6 = (f32[2,512,128]{2,1,0:T(8,128)}, f32[2,512,128]{2,1,0:T(8,128)S(1)}, u32[]{:S(2)}, u32[]{:S(2)}) collective-permute-start(f32[2,512,128]{2,1,0:T(8,128)} %param.13), channel_id=1, source_target_pairs={{0,8},{4,12},{8,0},{12,4},{16,24},{20,28},{24,16},{28,20},{1,9},{5... | collective-permute-start | bytes 1572872 | tf_op jit(solution)/shard_map/ppermute | solution.py:359
  13.8 7.5 %collective-permute-start.18 = (f32[2,128,128]{2,1,0:T(8,128)S(1)}, f32[2,128,128]{2,1,0:T(8,128)S(1)}, u32[]{:S(2)}, u32[]{:S(2)}) collective-permute-start(f32[2,128,128]{2,1,0:T(8,128)S(1)} %get-tuple-element.33), channel_id=1, source_target_pairs={{0,3},{1,0},{2,1},{3,2},{4,7},{5,4},{6,5},{7,6},{8,11},{9,8},{10,9... | collective-permute-start | bytes 393224 | tf_op jit(solution)/shard_map/ppermute | solution.py:362
  17.4 18.8 %collective-permute-start.8 = (f32[2,512,128]{2,1,0:T(8,128)S(1)}, f32[2,512,128]{2,1,0:T(8,128)S(1)}, u32[]{:S(2)}, u32[]{:S(2)}) collective-permute-start(f32[2,512,128]{2,1,0:T(8,128)S(1)} %copy-done.11), channel_id=1, source_target_pairs={{0,24},{4,28},{8,16},{12,20},{16,8},{20,12},{24,0},{28,4},{1,25},{... | collective-permute-start | bytes 1572872 | tf_op jit(solution)/shard_map/ppermute | solution.py:359
  20.2 36.6 %collective-permute-start.7 = (f32[2,512,128]{2,1,0:T(8,128)S(1)}, f32[2,512,128]{2,1,0:T(8,128)S(1)}, u32[]{:S(2)}, u32[]{:S(2)}) collective-permute-start(f32[2,512,128]{2,1,0:T(8,128)S(1)} %copy-done.11), channel_id=1, source_target_pairs={{0,16},{4,20},{8,24},{12,28},{16,0},{20,4},{24,8},{28,12},{1,17},{... | collective-permute-start | bytes 1572872 | tf_op jit(solution)/shard_map/ppermute | solution.py:359
  20.8 5.9 %collective-permute-start.17 = (f32[2,128,128]{2,1,0:T(8,128)S(1)}, f32[2,128,128]{2,1,0:T(8,128)S(1)}, u32[]{:S(2)}, u32[]{:S(2)}) collective-permute-start(f32[2,128,128]{2,1,0:T(8,128)S(1)} %get-tuple-element.34), channel_id=1, source_target_pairs={{0,2},{1,3},{2,0},{3,1},{4,6},{5,7},{6,4},{7,5},{8,10},{9,11},{10,... | collective-permute-start | bytes 393224 | tf_op jit(solution)/shard_map/ppermute | solution.py:362
  21.3 7.2 %collective-permute-start.16 = (f32[2,128,128]{2,1,0:T(8,128)S(1)}, f32[2,128,128]{2,1,0:T(8,128)S(1)}, u32[]{:S(2)}, u32[]{:S(2)}) collective-permute-start(f32[2,128,128]{2,1,0:T(8,128)S(1)} %get-tuple-element.35), channel_id=1, source_target_pairs={{0,1},{1,2},{2,3},{3,0},{4,5},{5,6},{6,7},{7,4},{8,9},{9,10},{10,1... | collective-permute-start | bytes 393224 | tf_op jit(solution)/shard_map/ppermute | solution.py:362
  28.6 28.5 %collective-permute-start.21 = (f32[4,2,128,128]{3,2,1,0:T(8,128)S(1)}, f32[4,2,128,128]{3,2,1,0:T(8,128)S(1)}, u32[]{:S(2)}, u32[]{:S(2)}) collective-permute-start(f32[4,2,128,128]{3,2,1,0:T(8,128)S(1)} %pad_maximum_fusion.3), channel_id=1, source_target_pairs={{0,24},{4,28},{8,16},{12,20},{16,8},{20,12},{24,0},{28,4},{1,25},{... | collective-permute-start | bytes 1572872 | tf_op jit(solution)/shard_map/ppermute | solution.py:359
  30.4 33.8 %collective-permute-start.20 = (f32[4,2,128,128]{3,2,1,0:T(8,128)S(1)}, f32[4,2,128,128]{3,2,1,0:T(8,128)S(1)}, u32[]{:S(2)}, u32[]{:S(2)}) collective-permute-start(f32[4,2,128,128]{3,2,1,0:T(8,128)S(1)} %pad_maximum_fusion.3), channel_id=1, source_target_pairs={{0,16},{4,20},{8,24},{12,28},{16,0},{20,4},{24,8},{28,12},{1,17},{... | collective-permute-start | bytes 1572872 | tf_op jit(solution)/shard_map/ppermute | solution.py:359
  31.6 32.7 %collective-permute-start.19 = (f32[4,2,128,128]{3,2,1,0:T(8,128)S(1)}, f32[4,2,128,128]{3,2,1,0:T(8,128)S(1)}, u32[]{:S(2)}, u32[]{:S(2)}) collective-permute-start(f32[4,2,128,128]{3,2,1,0:T(8,128)S(1)} %pad_maximum_fusion.3), channel_id=1, source_target_pairs={{0,8},{4,12},{8,0},{12,4},{16,24},{20,28},{24,16},{28,20},{1,9},{5... | collective-permute-start | bytes 1572872 | tf_op jit(solution)/shard_map/ppermute | solution.py:359
  57.0 63.9 %collective-permute-start.9 = (f32[4,2,512,128]{3,2,1,0:T(8,128)S(1)}, f32[4,2,512,128]{3,2,1,0:T(8,128)}, u32[]{:S(2)}, u32[]{:S(2)}) collective-permute-start(f32[4,2,512,128]{3,2,1,0:T(8,128)S(1)} %pad_maximum_fusion.refs_4_), channel_id=1, source_target_pairs={{0,4},{4,0},{8,12},{12,8},{16,20},{20,16},{24,28},{28,24},{1,5},{5... | collective-permute-start | bytes 6291464 | tf_op jit(solution)/shard_map/ppermute | solution.py:359
  64.2 1.5 copy-start
  64.2 1.5 copy-start.8
  65.7 76.7 %collective-permute-start.22 = (f32[4,4,2,128,128]{4,3,2,1,0:T(8,128)}, f32[4,4,2,128,128]{4,3,2,1,0:T(8,128)}, u32[]{:S(2)}, u32[]{:S(2)}) collective-permute-start(f32[4,4,2,128,128]{4,3,2,1,0:T(8,128)} %pad_maximum_fusion.1.mine), channel_id=1, source_target_pairs={{0,4},{4,0},{8,12},{12,8},{16,20},{20,16},{24,28},{28,24},{1,5},{5... | collective-permute-start | bytes 6291464 | tf_op jit(solution)/shard_map/ppermute | solution.py:359
  65.8 15.5 %collective-permute-start.2 = (f32[512,128]{1,0:T(8,128)S(1)}, f32[512,128]{1,0:T(8,128)S(1)}, u32[]{:S(2)}, u32[]{:S(2)}) collective-permute-start(f32[512,128]{1,0:T(8,128)S(1)} %get-tuple-element.40), channel_id=1, source_target_pairs={{0,3},{1,0},{2,1},{3,2},{4,7},{5,4},{6,5},{7,6},{8,11},{9,8},{10,9... | collective-permute-start | bytes 786440 | tf_op jit(solution)/shard_map/ppermute | solution.py:362
  66.3 15.0 %collective-permute-start = (f32[512,128]{1,0:T(8,128)S(1)}, f32[512,128]{1,0:T(8,128)S(1)}, u32[]{:S(2)}, u32[]{:S(2)}) collective-permute-start(f32[512,128]{1,0:T(8,128)S(1)} %get-tuple-element.41), channel_id=1, source_target_pairs={{0,1},{1,2},{2,3},{3,0},{4,5},{5,6},{6,7},{7,4},{8,9},{9,10},{10,1... | collective-permute-start | bytes 786440 | tf_op jit(solution)/shard_map/ppermute | solution.py:362
  67.8 21.4 %collective-permute-start.1 = (f32[512,128]{1,0:T(8,128)S(1)}, f32[512,128]{1,0:T(8,128)S(1)}, u32[]{:S(2)}, u32[]{:S(2)}) collective-permute-start(f32[512,128]{1,0:T(8,128)S(1)} %get-tuple-element.42), channel_id=1, source_target_pairs={{0,2},{1,3},{2,0},{3,1},{4,6},{5,7},{6,4},{7,5},{8,10},{9,11},{10,... | collective-permute-start | bytes 786440 | tf_op jit(solution)/shard_map/ppermute | solution.py:362
  67.9 53.0 %copy-start.9 = (s32[2]{0:T(128)}, s32[2]{0:T(128)S(1)}, u32[]{:S(2)}) copy-start(s32[2]{0:T(128)S(1)} %pad_add_fusion.at) | copy-start | bytes 28
  81.2 13.5 %copy-start.4 = (f32[512,128]{1,0:T(8,128)}, f32[512,128]{1,0:T(8,128)S(1)}, u32[]{:S(2)}) copy-start(f32[512,128]{1,0:T(8,128)S(1)} %collective-permute-done.2.refs_3_.refs_7_) | copy-start | bytes 786436
  81.2 13.5 %copy-start.5 = (f32[512,128]{1,0:T(8,128)}, f32[512,128]{1,0:T(8,128)S(1)}, u32[]{:S(2)}) copy-start(f32[512,128]{1,0:T(8,128)S(1)} %collective-permute-done.refs_1_.refs_5_) | copy-start | bytes 786436
  89.3 5.4 %copy-start.6 = (f32[512,128]{1,0:T(8,128)}, f32[512,128]{1,0:T(8,128)S(1)}, u32[]{:S(2)}) copy-start(f32[512,128]{1,0:T(8,128)S(1)} %collective-permute-done.1.refs_2_.refs_6_) | copy-start | bytes 786436
  89.3 2.3 %copy-start.10 = (f32[512,2048]{1,0:T(8,128)S(1)}, f32[512,2048]{1,0:T(8,128)}, u32[]{:S(2)}) copy-start(f32[512,2048]{1,0:T(8,128)} %diag.1) | copy-start | bytes 12582916
  94.7 11.2 %collective-permute-start.3 = (f32[512,128]{1,0:T(8,128)S(1)}, f32[512,128]{1,0:T(8,128)S(1)}, u32[]{:S(2)}, u32[]{:S(2)}) collective-permute-start(f32[512,128]{1,0:T(8,128)S(1)} %get-tuple-element.18), channel_id=1, source_target_pairs={{0,3},{1,0},{2,1},{3,2},{4,7},{5,4},{6,5},{7,6},{8,11},{9,8},{10,9... | collective-permute-start | bytes 786440 | tf_op jit(solution)/shard_map/ppermute | solution.py:362
  99.1 21.8 %collective-permute-start.4 = (f32[512,128]{1,0:T(8,128)S(1)}, f32[512,128]{1,0:T(8,128)S(1)}, u32[]{:S(2)}, u32[]{:S(2)}) collective-permute-start(f32[512,128]{1,0:T(8,128)S(1)} %get-tuple-element.19), channel_id=1, source_target_pairs={{0,2},{1,3},{2,0},{3,1},{4,6},{5,7},{6,4},{7,5},{8,10},{9,11},{10,... | collective-permute-start | bytes 786440 | tf_op jit(solution)/shard_map/ppermute | solution.py:362
  99.1 21.8 %collective-permute-start.5 = (f32[512,128]{1,0:T(8,128)S(1)}, f32[512,128]{1,0:T(8,128)S(1)}, u32[]{:S(2)}, u32[]{:S(2)}) collective-permute-start(f32[512,128]{1,0:T(8,128)S(1)} %get-tuple-element.20), channel_id=1, source_target_pairs={{0,1},{1,2},{2,3},{3,0},{4,5},{5,6},{6,7},{7,4},{8,9},{9,10},{10,1... | collective-permute-start | bytes 786440 | tf_op jit(solution)/shard_map/ppermute | solution.py:362
  105.9 18.3 %copy-start.1 = (f32[512,128]{1,0:T(8,128)}, f32[512,128]{1,0:T(8,128)S(1)}, u32[]{:S(2)}) copy-start(f32[512,128]{1,0:T(8,128)S(1)} %collective-permute-done.3.refs_1_.refs_9_) | copy-start | bytes 786436
  120.9 3.4 %copy-start.2 = (f32[512,128]{1,0:T(8,128)}, f32[512,128]{1,0:T(8,128)S(1)}, u32[]{:S(2)}) copy-start(f32[512,128]{1,0:T(8,128)S(1)} %collective-permute-done.4.refs_2_.refs_10_) | copy-start | bytes 786436
  120.9 3.4 %copy-start.3 = (f32[512,128]{1,0:T(8,128)}, f32[512,128]{1,0:T(8,128)S(1)}, u32[]{:S(2)}) copy-start(f32[512,128]{1,0:T(8,128)S(1)} %collective-permute-done.5.refs_3_.refs_11_) | copy-start | bytes 786436
  124.2 0.7 copy-start.7
  124.9 22.5 %collective-permute-start.10 = (f32[4,128,128]{2,1,0:T(8,128)}, f32[4,128,128]{2,1,0:T(8,128)S(1)}, u32[]{:S(2)}, u32[]{:S(2)}) collective-permute-start(f32[4,128,128]{2,1,0:T(8,128)} %get-tuple-element.22), channel_id=1, source_target_pairs={{0,1},{1,2},{2,3},{3,0},{4,5},{5,6},{6,7},{7,4},{8,9},{9,10},{10,1... | collective-permute-start | bytes 786440 | tf_op jit(solution)/shard_map/ppermute | solution.py:362
  126.4 21.0 %collective-permute-start.11 = (f32[4,128,128]{2,1,0:T(8,128)S(1)}, f32[4,128,128]{2,1,0:T(8,128)S(1)}, u32[]{:S(2)}, u32[]{:S(2)}) collective-permute-start(f32[4,128,128]{2,1,0:T(8,128)S(1)} %get-tuple-element.23), channel_id=1, source_target_pairs={{0,2},{1,3},{2,0},{3,1},{4,6},{5,7},{6,4},{7,5},{8,10},{9,11},{10,... | collective-permute-start | bytes 786440 | tf_op jit(solution)/shard_map/ppermute | solution.py:362
  128.3 19.1 %collective-permute-start.12 = (f32[4,128,128]{2,1,0:T(8,128)S(1)}, f32[4,128,128]{2,1,0:T(8,128)S(1)}, u32[]{:S(2)}, u32[]{:S(2)}) collective-permute-start(f32[4,128,128]{2,1,0:T(8,128)S(1)} %get-tuple-element.24), channel_id=1, source_target_pairs={{0,3},{1,0},{2,1},{3,2},{4,7},{5,4},{6,5},{7,6},{8,11},{9,8},{10,9... | collective-permute-start | bytes 786440 | tf_op jit(solution)/shard_map/ppermute | solution.py:362
  147.4 0.7 copy-start.12
  147.4 0.8 copy-start.13
  147.5 0.9 copy-start.14

commit v5 on v4

--- a/solution.py
+++ b/solution.py
@@ -94,42 +94,60 @@
                 work[t, top + b :, :] = work[t, top + b :, :] - update[top + b :, :]
 
 
-def rows_loop(n, step, body):
-    def one(i, carry):
-        body(pl.ds(pl.multiple_of(i * step, step), step))
-        return carry
-
-    lax.fori_loop(0, n // step, one, 0)
-
-
-def sketched(u_ref, v_ref, s_ref, out_ref, u_parts, v_parts):
+def quadrants(x):
+    x = fold(x)
+    h = x.shape[0] // 2
+    return x[:h] + x[h:]
+
+
+def sketched(u_ref, v_ref, s_ref, out_ref, v_parts, u_parts, cross):
     v = beside(v_ref[0])
     v_parts[0] = v
-    x = fold(mm(v, beside(s_ref[...]), TN))
-    h = x.shape[0] // 2
-    rhs = doubled_rows(x[:h] + x[h:])
-
-    def body(at):
-        u = beside(u_ref[0, at, :])
-        u_parts[0, at, :] = u
-        out_ref[0, at, :] = fold(mm(u, rhs, NN))
-
-    rows_loop(u_ref.shape[1], 512, body)
-
-
-def sketch_tiles(tile_u, tile_v, sketch):
-    tiles, n, k = tile_u.shape
-    block = pl.BlockSpec((1, n, k), lambda i: (i, 0, 0))
-    parts = pl.BlockSpec((1, n, 2 * k), lambda i: (i, 0, 0))
+    rhs = doubled_rows(quadrants(mm(v, beside(s_ref[...]), TN)))
+    u = beside(u_ref[0])
+    u_parts[0] = u
+    x = fold(mm(u, rhs, NN))
+    out_ref[0] = x
+    cross[0] = quadrants(mm(beside(x), u, TN))
+
+
+def sketch_tiles(tile_u, tile_v, sketch, begin, end):
+    _, n, k = tile_u.shape
+    tiles = end - begin
+    block = pl.BlockSpec((1, n, k), lambda i: (i + begin, 0, 0))
+    own = lambda *dims: pl.BlockSpec((1, *dims), lambda i: (i, 0, 0))
     return pl.pallas_call(
         sketched,
         grid=(tiles,),
         in_specs=[block, block, pl.BlockSpec((n, k), lambda i: (0, 0))],
-        out_specs=[block, parts, parts],
-        out_shape=[jax.ShapeDtypeStruct(tile_u.shape, f32)] + [jax.ShapeDtypeStruct((tiles, n, 2 * k), bf16)] * 2,
+        out_specs=[own(n, k), own(n, 2 * k), own(n, 2 * k), own(k, k)],
+        out_shape=[jax.ShapeDtypeStruct((tiles, n, k), f32)]
+        + [jax.ShapeDtypeStruct((tiles, n, 2 * k), bf16)] * 2
+        + [jax.ShapeDtypeStruct((tiles, k, k), f32)],
+        compiler_params=pltpu.CompilerParams(vmem_limit_bytes=36 * 1024 * 1024),
         cost_estimate=pl.CostEstimate(flops=6 * tiles * n * k * k * 2, bytes_accessed=20 * tiles * n * k, transcendentals=0),
         name="sketch_tiles",
     )(tile_u, tile_v, sketch)
+
+
+def split_kernel(diag, parts):
+    rows = diag.shape[0]
+    for b in range(parts.shape[0]):
+        parts[b] = beside(diag[:, b * rows : (b + 1) * rows])
+
+
+def split_diag(diag):
+    rows, n = diag.shape
+    vmem = pl.BlockSpec(memory_space=VMEM)
+    return pl.pallas_call(
+        split_kernel,
+        in_specs=[vmem],
+        out_specs=vmem,
+        out_shape=jax.ShapeDtypeStruct((n // rows, rows, 2 * rows), bf16),
+        compiler_params=pltpu.CompilerParams(vmem_limit_bytes=36 * 1024 * 1024),
+        cost_estimate=pl.CostEstimate(flops=4 * rows * n, bytes_accessed=8 * rows * n, transcendentals=0),
+        name="split_diag",
+    )(diag)
 
 
 def block_of(c, d, n):
@@ -163,6 +181,7 @@
         in_specs=[pl.BlockSpec(memory_space=pltpu.SMEM)] + [vmem] * 3,
         out_specs=[vmem] * 2,
         out_shape=[jax.ShapeDtypeStruct((tiles, n, 2 * k), bf16), jax.ShapeDtypeStruct((tiles, k, k), f32)],
+        compiler_params=pltpu.CompilerParams(vmem_limit_bytes=36 * 1024 * 1024),
         cost_estimate=pl.CostEstimate(flops=6 * tiles * n * k * k, bytes_accessed=8 * tiles * n * k, transcendentals=0),
         name="project",
     )(at, mine, other, sketch)
@@ -171,16 +190,14 @@
 def solve_kernel(n_col, at, diag, own_u, *refs):
     xs, outs = refs[:n_col], refs[n_col:]
     c = at[1]
-    rows = diag.shape[0]
     solved = None
     for d in range(n_col):
-        cols = pl.ds(pl.multiple_of(jnp.maximum(c - d, 0) * rows, rows), rows)
         x = xs[d][...] if d == 0 else jnp.where(c >= d, xs[d][...], 0.0)
-        part = product(diag[:, cols], x)
+        part = fold(mm(diag[jnp.maximum(c - d, 0)], doubled_rows(x), NN))
         solved = part if solved is None else solved + part
+    lhs = beside(solved)
     for d in range(n_col):
-        cols = pl.ds(pl.multiple_of(jnp.maximum(c - d, 0) * rows, rows), rows)
-        x = product_tn(solved, diag[:, cols]).T
+        x = quadrants(mm(lhs, diag[jnp.maximum(c - d, 0)], TN)).T
         outs[d][...] = x if d == 0 else jnp.where(c >= d, x, own_u[...])
 
 
@@ -231,77 +248,93 @@
     )(at, *parts, mine, other)
 
 
-def recompress_kernel(tiles, n, k, n_col, at, *refs):
-    core_parts, first, second = refs[:n_col], refs[n_col : 2 * n_col], refs[2 * n_col : 3 * n_col]
-    small, base, u_parts, v_parts, w_parts, new_u, new_v = refs[3 * n_col : 3 * n_col + 7]
-    s, tu, tv, cu, sp, out, ru, work, cross, cores, row_parts, sem, row_sem = refs[3 * n_col + 7 :]
+def prepare_kernel(n_col, at, *refs):
+    first, second = refs[:n_col], refs[n_col : 2 * n_col]
+    halves_in, (row_parts, with_row, row_row) = refs[2 * n_col : -3], refs[-3:]
     c = at[1]
-    root = math.sqrt(n)
-    blk = n // n_col
-    row_copies = []
+    blk = first[0].shape[0]
     for d in range(n_col):
         rows = pl.ds(pl.multiple_of(block_of(c, d, n_col) * blk, blk), blk)
-        row_copies.append(tuple(
-            pltpu.make_async_copy(x, ru.at[rows], row_sem.at[d]) for x in (first[d], second[(n_col - d) % n_col])
-        ))
+        x = first[0][...] if d == 0 else jnp.where(c < d, first[d][...], second[n_col - d][...])
+        row_parts[rows, :] = beside(x)
+    row = row_parts[...]
+    row_row[...] = quadrants(mm(row, row, TN))
+    t = 0
+    for i in range(0, len(halves_in), 2):
+        base, u_parts = halves_in[i : i + 2]
+        for j in range(base.shape[0]):
+            x = mm(row, jnp.concatenate([beside(base[j]), u_parts[j]], axis=1), TN)
+            k = x.shape[0] // 2
+            with_row[t] = jnp.concatenate([quadrants(x[:, : 2 * k]), quadrants(x[:, 2 * k :])], axis=1)
+            t += 1
+
+
+def prepare(at, first, second, groups):
+    n_col = len(first)
+    blk, k = first[0].shape
+    n = n_col * blk
+    tiles = sum(base.shape[0] for base, _ in groups)
+    vmem = pl.BlockSpec(memory_space=VMEM)
+    return pl.pallas_call(
+        functools.partial(prepare_kernel, n_col),
+        in_specs=[pl.BlockSpec(memory_space=pltpu.SMEM)] + [vmem] * (2 * n_col + 2 * len(groups)),
+        out_specs=[vmem] * 3,
+        out_shape=[
+            jax.ShapeDtypeStruct((n, 2 * k), bf16),
+            jax.ShapeDtypeStruct((tiles, k, 2 * k), f32),
+            jax.ShapeDtypeStruct((k, k), f32),
+        ],
+        compiler_params=pltpu.CompilerParams(vmem_limit_bytes=36 * 1024 * 1024),
+        cost_estimate=pl.CostEstimate(flops=12 * tiles * n * k * k, bytes_accessed=8 * tiles * n * k, transcendentals=0),
+        name="prepare",
+    )(at, *first, *second, *[x for pair in groups for x in pair])
+
+
+def recompress_kernel(n, k, n_col, sizes, *refs):
+    tiles = sum(sizes)
+    place = [(g, j) for g, size in enumerate(sizes) for j in range(size)]
+    groups = len(sizes)
+    core_parts, refs = refs[:n_col], refs[n_col:]
+    (small, with_row, row_row), refs = refs[:3], refs[3:]
+    crosses, refs = refs[:groups], refs[groups:]
+    bases, v_parts, refs = refs[:groups], refs[groups : 2 * groups], refs[2 * groups :]
+    (w_parts, row_in, new_u, new_v), refs = refs[:4], refs[4:]
+    s, tv, cu, sp, out, work, cross, cores, row_parts, sem, row_sem = refs
+    root = math.sqrt(n)
+    row_copy = pltpu.make_async_copy(row_in, row_parts, row_sem)
     early, late, outs = [], [], []
-    for t in range(tiles):
-        early.append((
-            pltpu.make_async_copy(base.at[t], s.at[t], sem.at[t]),
-            pltpu.make_async_copy(u_parts.at[t], tu.at[t], sem.at[tiles + t]),
-        ))
+    for t, (g, j) in enumerate(place):
+        early.append(pltpu.make_async_copy(bases[g].at[j], s.at[t], sem.at[t]))
         late.append((
-            pltpu.make_async_copy(v_parts.at[t], tv.at[t], sem.at[2 * tiles + t]),
-            pltpu.make_async_copy(w_parts.at[t], cu.at[t], sem.at[3 * tiles + t]),
+            pltpu.make_async_copy(v_parts[g].at[j], tv.at[t], sem.at[tiles + t]),
+            pltpu.make_async_copy(w_parts.at[t], cu.at[t], sem.at[2 * tiles + t]),
         ))
         outs.append((
-            pltpu.make_async_copy(s.at[t], new_u.at[t], sem.at[4 * tiles + t]),
-            pltpu.make_async_copy(out.at[t], new_v.at[t], sem.at[5 * tiles + t]),
+            pltpu.make_async_copy(s.at[t], new_u.at[t], sem.at[3 * tiles + t]),
+            pltpu.make_async_copy(out.at[t], new_v.at[t], sem.at[4 * tiles + t]),
         ))
-    row_copies[0][0].start()
-    for d in range(1, n_col):
-        pl.when(c < d)(row_copies[d][0].start)
-        pl.when(c >= d)(row_copies[d][1].start)
-    for x in early[0] + early[1]:
+    row_copy.start()
+    for x in early:
         x.start()
     total = core_parts[0][...]
     for p in core_parts[1:]:
         total = total + p[...]
     cores[...] = total
-    for x in row_copies:
-        x[0].wait()
-
-    def split(at):
-        row_parts[at, :] = beside(ru[at, :])
-
-    rows_loop(n, 512, split)
-    for t in range(tiles):
-        for x in early[t]:
-            x.wait()
-        for x in (early + late)[t + 2]:
-            x.start()
-        rhs = doubled_rows(-product(cores[t], small[t]))
-        work[t] = jnp.zeros((k, 2 * k), f32)
-        cross[t] = jnp.zeros((k, 2 * k), f32)
-
-        def gather(at, t=t, rhs=rhs):
-            part = beside(s[t, at, :] + fold(mm(row_parts[at, :], rhs, NN)))
-            sp[t, at, :] = part
-            x = mm(part, jnp.concatenate([part, tu[t, at, :], row_parts[at, :]], axis=1), TN)
-            x = x[:k] + x[k:]
-            work[t, :, :k] += fold(x[:, : 2 * k])
-            cross[t, :, :k] += fold(x[:, 2 * k : 4 * k])
-            cross[t, :, k:] += fold(x[:, 4 * k :])
-
-        gather(pl.ds(0, n))
-    for pair in late[2:]:
-        for x in pair:
-            x.start()
     eye = jnp.where(
         lax.broadcasted_iota(jnp.int32, (k, k), 0) == lax.broadcasted_iota(jnp.int32, (k, k), 1), 1.0, 0.0
     ).astype(f32)
-    for t in range(tiles):
+    mixes = [-product(cores[t], small[t]) for t in range(tiles)]
+    row_copy.wait()
+    for t, (g, j) in enumerate(place):
+        early[t].wait()
+        part = beside(s[t] + fold(mm(row_parts[...], doubled_rows(mixes[t]), NN)))
+        sp[t] = part
+        work[t, :, :k] = quadrants(mm(part, part, TN))
         work[t, :, k:] = eye
+        x = product_tn(mixes[t], jnp.concatenate([with_row[t, :, k:], row_row[...]], axis=1))
+        cross[t] = x + jnp.concatenate([crosses[g][j], with_row[t, :, :k].T], axis=1)
+        for x in late[t]:
+            x.start()
     eliminate(work, tiles, k)
     for t in range(tiles):
         inverse = work[t, :, k:]
@@ -312,41 +345,39 @@
         c12 = jnp.concatenate([doubled_columns(c1), doubled_columns(c2)], axis=1)
         for x in late[t]:
             x.wait()
-
-        def finish(at, t=t, by=by, c12=c12):
-            s[t, at, :] = fold(mm(sp[t, at, :], by, NT))
-            lhs = jnp.concatenate([tv[t, at, :], cu[t, at, :]], axis=1)
-            out[t, at, :] = fold(mm(lhs, c12, NT))
-
-        finish(pl.ds(0, n))
-        for x in outs[t]:
-            x.start()
+        s[t] = fold(mm(sp[t], by, NT))
+        outs[t][0].start()
+        out[t] = fold(mm(jnp.concatenate([tv[t], cu[t]], axis=1), c12, NT))
+        outs[t][1].start()
     for pair in outs:
         for x in pair:
             x.wait()
 
 
-def recompress(at, core_parts, first, second, small, base, u_parts, v_parts, w_parts):
-    tiles, n, k = base.shape
+def recompress(core_parts, small, with_row, row_row, crosses, bases, v_parts, w_parts, row_parts):
+    tiles, n, k2 = w_parts.shape
+    k = k2 // 2
     n_col = len(core_parts)
+    sizes = [x.shape[0] for x in bases]
+    groups = len(sizes)
     any_ = pl.BlockSpec(memory_space=ANY)
     vmem = pl.BlockSpec(memory_space=VMEM)
     full = lambda: VMEM((tiles, n, k), f32)
     split = lambda: VMEM((tiles, n, 2 * k), bf16)
     return pl.pallas_call(
-        functools.partial(recompress_kernel, tiles, n, k, n_col),
-        in_specs=[pl.BlockSpec(memory_space=pltpu.SMEM)] + [vmem] * n_col + [any_] * (2 * n_col) + [vmem] + [any_] * 4,
+        functools.partial(recompress_kernel, n, k, n_col, sizes),
+        in_specs=[vmem] * (n_col + 3 + groups) + [any_] * (2 * groups + 2),
         out_specs=[any_, any_],
-        out_shape=[jax.ShapeDtypeStruct(base.shape, f32)] * 2,
+        out_shape=[jax.ShapeDtypeStruct((tiles, n, k), f32)] * 2,
         scratch_shapes=[
-            full(), split(), split(), split(), split(), full(), VMEM((n, k), f32),
+            full(), split(), split(), split(), full(),
             VMEM((tiles, k, 2 * k), f32), VMEM((tiles, k, 2 * k), f32), VMEM((tiles, k, k), f32),
             VMEM((n, 2 * k), bf16),
-            pltpu.SemaphoreType.DMA((6 * tiles,)), pltpu.SemaphoreType.DMA((n_col,)),
+            pltpu.SemaphoreType.DMA((5 * tiles,)), pltpu.SemaphoreType.DMA,
         ],
         cost_estimate=pl.CostEstimate(flops=24 * tiles * n * k * k, bytes_accessed=28 * tiles * n * k, transcendentals=0),
         name="recompress",
-    )(at, *core_parts, *first, *second, small, base, u_parts, v_parts, w_parts)
+    )(*core_parts, small, with_row, row_row, *crosses, *bases, *v_parts, w_parts, row_parts)
 
 
 def step(n_row, n_col, tile_u, tile_v, row_panel_u, row_panel_v, col_panel_u, col_panel_v, diag_inverse, sketch):
@@ -377,8 +408,13 @@
     col_v_other = partner(col_v_mine, 1)
     moved = [pick(cuts, chip ^ c)] + [around(pick(cuts, chip ^ lax.rem(c + d, n_col)), d) for d in range(1, n_col)]
     planes = lax.optimization_barrier(jnp.stack(moved))
-    base, u_parts, v_parts = sketch_tiles(tile_u[0], tile_v[0], sketch)
-    sums = solve(at, diag_inverse, row_u, [row_v] + first)
+    tiles = tile_u.shape[1]
+    diag = split_diag(diag_inverse)
+    groups = []
+    for begin, end in ((0, tiles // 2), (tiles // 2, tiles)):
+        groups.append(sketch_tiles(tile_u[0], tile_v[0], sketch, begin, end))
+    bases, v_parts, u_parts, crosses = zip(*groups)
+    sums = solve(at, diag, row_u, [row_v] + first)
     second = [around(sums[d], n_col - d) for d in range(1, n_col)]
     gathered = [planes] + [partner(planes, 2 * e) for e in range(1, chips)]
     col_u_mine = jnp.stack(gathered)
@@ -386,7 +422,8 @@
     w_parts, small = project(n_col, at, col_u_mine, col_u_other, sketch)
     cores = partial_cores(at, [sums[0]] + second, col_v_mine, col_v_other)
     core_parts = [cores[0]] + [around(cores[d], d) for d in range(1, n_col)]
-    new_u, new_v = recompress(at, core_parts, [row_u] + first, [row_u] + second, small, base, u_parts, v_parts, w_parts)
+    row_parts, with_row, row_row = prepare(at, [row_u] + first, [row_u] + second, list(zip(bases, u_parts)))
+    new_u, new_v = recompress(core_parts, small, with_row, row_row, crosses, bases, v_parts, w_parts, row_parts)
     return new_u[None], new_v[None]
 
 

time: 175 us -> 168 us (0.960)
  waiting for transfers between devices: 86.4 us -> 77.5 us
  local copies, waits for them, and re-layouts: 5.11 us -> 10.5 us
  Pallas kernels: 47.1 us -> 43 us
    ppermute x12, waiting for transfers between devices: 49.3 us -> 41.6 us  [shift(): return lax.ppermute(x, 'col', pairs)]
    unnamed x30 -> x48, local copies, waits for them, and re-layouts: 3.87 us -> 9.23 us
    pallas_call x1 -> x2, Pallas kernels: 11.1 us -> 5.97 us  [sketch_tiles(): pl.pallas_call(sketched, grid=(tiles,), in_specs=[block, block, pl.BlockS...]
    pallas_call x1 -> x3, Pallas kernels: 24.5 us -> 26.3 us  [the longest x1 22.3 us: recompress(): pl.pallas_call(functools.partial(recompress_kernel, n, k, n_col, sizes),...]
where the time goes in v5:
time: 168 us; the launch traced here: 166 us
  waiting for transfers between devices  77.5 us (46%)
  Pallas kernels  43 us (26%)
  starting transfers between devices  31.7 us (19%)
  local copies, waits for them, and re-layouts  10.5 us (6%)
  other arithmetic  1.89 us (1%)
    ppermute x12, waiting for transfers between devices, shift(): return lax.ppermute(x, 'col', pairs)  41.6 us
    ppermute x11, waiting for transfers between devices, partner(): return lax.ppermute(x, 'row', [(a, a ^ m) for a in range(n_row)])  35.9 us
    pallas_call x1, Pallas kernels, recompress(): pl.pallas_call(functools.partial(recompress_kernel, n, k, n_col, sizes),...  22.3 us
    ppermute x12, starting transfers between devices, shift(): return lax.ppermute(x, 'col', pairs)  18.3 us
    ppermute x11, starting transfers between devices, partner(): return lax.ppermute(x, 'row', [(a, a ^ m) for a in range(n_row)])  13.5 us
    unnamed x48, local copies, waits for them, and re-layouts  9.23 us
    pallas_call x2, Pallas kernels, sketch_tiles(): pl.pallas_call(sketched, grid=(tiles,), in_specs=[block, block, pl.BlockS...  5.97 us
    pallas_call x1, Pallas kernels, project(): pl.pallas_call(functools.partial(project_kernel, n_col), in_specs=[pl.Blo...  4 us
  transfers between devices with their start and end apart: 23, of which 12 were waited for; matrix products, arithmetic and copies ran while one was open for 1% of the time, Pallas kernels for 13%

profile of v5, /device:TPU:0, one launch (start us, length us, event | category | flops | bytes accessed | tf_op | source)
XLA Modules:
  0.0 165.7 jit_solution(8818343092175720315)
XLA Ops:
  0.6 0.0 copy-start.20
  0.7 1.2 dynamic-slice_bitcast_fusion.6
  1.9 3.1 %collective-permute-start.14 = (f32[2,128,128]{2,1,0:T(8,128)S(1)}, f32[2,128,128]{2,1,0:T(8,128)S(1)}, u32[]{:S(2)}, u32[]{:S(2)}) collective-permute-start(f32[2,128,128]{2,1,0:T(8,128)S(1)} %get-tuple-element.53), channel_id=1, source_target_pairs={{0,16},{4,20},{8,24},{12,28},{16,0},{20,4},{24,8},{28,12},{1,17},{... | collective-permute-start | bytes 393224 | tf_op jit(solution)/shard_map/ppermute | solution.py:390
  4.9 1.5 collective-permute-start.13
  6.4 0.0 collective-permute-start.15
  6.5 1.9 %collective-permute-start.6 = (f32[2,512,128]{2,1,0:T(8,128)}, f32[2,512,128]{2,1,0:T(8,128)S(1)}, u32[]{:S(2)}, u32[]{:S(2)}) collective-permute-start(f32[2,512,128]{2,1,0:T(8,128)} %param.13), channel_id=1, source_target_pairs={{0,8},{4,12},{8,0},{12,4},{16,24},{20,28},{24,16},{28,20},{1,9},{5... | collective-permute-start | bytes 1572872 | tf_op jit(solution)/shard_map/ppermute | solution.py:390
  8.4 0.0 collective-permute-done.14
  8.4 2.9 %collective-permute-done.13 = f32[2,128,128]{2,1,0:T(8,128)S(1)} collective-permute-done((f32[2,128,128]{2,1,0:T(8,128)S(1)}, f32[2,128,128]{2,1,0:T(8,128)S(1)}, u32[]{:S(2)}, u32[]{:S(2)}) %collective-permute-start.13) | collective-permute-done | bytes 131104 | tf_op jit(solution)/shard_map/ppermute | solution.py:390
  11.3 2.4 %collective-permute-done.15 = f32[2,128,128]{2,1,0:T(8,128)S(1)} collective-permute-done((f32[2,128,128]{2,1,0:T(8,128)S(1)}, f32[2,128,128]{2,1,0:T(8,128)S(1)}, u32[]{:S(2)}, u32[]{:S(2)}) %collective-permute-start.15) | collective-permute-done | bytes 131104 | tf_op jit(solution)/shard_map/ppermute | solution.py:390
  13.8 3.7 %collective-permute-start.18 = (f32[2,128,128]{2,1,0:T(8,128)S(1)}, f32[2,128,128]{2,1,0:T(8,128)S(1)}, u32[]{:S(2)}, u32[]{:S(2)}) collective-permute-start(f32[2,128,128]{2,1,0:T(8,128)S(1)} %get-tuple-element.49), channel_id=1, source_target_pairs={{0,3},{1,0},{2,1},{3,2},{4,7},{5,4},{6,5},{7,6},{8,11},{9,8},{10,9... | collective-permute-start | bytes 393224 | tf_op jit(solution)/shard_map/ppermute | solution.py:393
  17.4 2.8 %collective-permute-start.8 = (f32[2,512,128]{2,1,0:T(8,128)S(1)}, f32[2,512,128]{2,1,0:T(8,128)S(1)}, u32[]{:S(2)}, u32[]{:S(2)}) collective-permute-start(f32[2,512,128]{2,1,0:T(8,128)S(1)} %copy-done.20), channel_id=1, source_target_pairs={{0,24},{4,28},{8,16},{12,20},{16,8},{20,12},{24,0},{28,4},{1,25},{... | collective-permute-start | bytes 1572872 | tf_op jit(solution)/shard_map/ppermute | solution.py:390
  20.2 0.5 collective-permute-start.7
  20.8 0.0 collective-permute-start.17
  20.8 0.6 collective-permute-done.18
  21.3 1.0 collective-permute-start.16
  22.3 4.4 %collective-permute-done.17 = f32[2,128,128]{2,1,0:T(8,128)S(1)} collective-permute-done((f32[2,128,128]{2,1,0:T(8,128)S(1)}, f32[2,128,128]{2,1,0:T(8,128)S(1)}, u32[]{:S(2)}, u32[]{:S(2)}) %collective-permute-start.17) | collective-permute-done | bytes 131104 | tf_op jit(solution)/shard_map/ppermute | solution.py:393
  26.7 1.9 %collective-permute-done.16 = f32[2,128,128]{2,1,0:T(8,128)S(1)} collective-permute-done((f32[2,128,128]{2,1,0:T(8,128)S(1)}, f32[2,128,128]{2,1,0:T(8,128)S(1)}, u32[]{:S(2)}, u32[]{:S(2)}) %collective-permute-start.16) | collective-permute-done | bytes 131104 | tf_op jit(solution)/shard_map/ppermute | solution.py:393
  28.6 1.8 %collective-permute-start.21 = (f32[4,2,128,128]{3,2,1,0:T(8,128)S(1)}, f32[4,2,128,128]{3,2,1,0:T(8,128)S(1)}, u32[]{:S(2)}, u32[]{:S(2)}) collective-permute-start(f32[4,2,128,128]{3,2,1,0:T(8,128)S(1)} %pad_maximum_fusion.3), channel_id=1, source_target_pairs={{0,24},{4,28},{8,16},{12,20},{16,8},{20,12},{24,0},{28,4},{1,25},{... | collective-permute-start | bytes 1572872 | tf_op jit(solution)/shard_map/ppermute | solution.py:390
  30.4 1.1 collective-permute-start.20
  31.6 0.0 collective-permute-done.6
  31.6 0.6 collective-permute-start.19
  32.2 4.1 %collective-permute-done.8 = f32[2,512,128]{2,1,0:T(8,128)S(1)} collective-permute-done((f32[2,512,128]{2,1,0:T(8,128)S(1)}, f32[2,512,128]{2,1,0:T(8,128)S(1)}, u32[]{:S(2)}, u32[]{:S(2)}) %collective-permute-start.8) | collective-permute-done | bytes 524320 | tf_op jit(solution)/shard_map/ppermute | solution.py:390
  36.3 20.6 %collective-permute-done.7 = f32[2,512,128]{2,1,0:T(8,128)S(1)} collective-permute-done((f32[2,512,128]{2,1,0:T(8,128)S(1)}, f32[2,512,128]{2,1,0:T(8,128)S(1)}, u32[]{:S(2)}, u32[]{:S(2)}) %collective-permute-start.7) | collective-permute-done | bytes 524320 | tf_op jit(solution)/shard_map/ppermute | solution.py:390
  56.9 1.5 pad_maximum_fusion.refs_4_
  58.3 0.0 collective-permute-start.9
  58.3 0.0 collective-permute-done.21
  58.3 5.9 %collective-permute-done.20 = f32[4,2,128,128]{3,2,1,0:T(8,128)S(1)} collective-permute-done((f32[4,2,128,128]{3,2,1,0:T(8,128)S(1)}, f32[4,2,128,128]{3,2,1,0:T(8,128)S(1)}, u32[]{:S(2)}, u32[]{:S(2)}) %collective-permute-start.20) | collective-permute-done | bytes 524320 | tf_op jit(solution)/shard_map/ppermute | solution.py:390
  64.2 0.0 collective-permute-done.19
  64.2 0.2 pad_maximum_fusion.1.mine
  64.5 0.1 collective-permute-start.22
  64.5 0.6 copy-done.7
  65.2 0.1 copy-done.16
  65.2 0.1 broadcast_select_fusion
  65.3 0.5 collective-permute-start.2
  65.8 1.6 collective-permute-start
  67.4 2.2 %copy-done.5 = f32[512,2048]{1,0:T(8,128)S(1)} copy-done((f32[512,2048]{1,0:T(8,128)S(1)}, f32[512,2048]{1,0:T(8,128)}, u32[]{:S(2)}) %copy-start.5) | copy-done | bytes 4194328
  69.6 0.5 split_diag.1.diag
  70.1 0.1 pad_add_fusion.at
  70.1 9.9 %collective-permute-done.2.refs_3_ = f32[512,128]{1,0:T(8,128)S(1)} collective-permute-done((f32[512,128]{1,0:T(8,128)S(1)}, f32[512,128]{1,0:T(8,128)S(1)}, u32[]{:S(2)}, u32[]{:S(2)}) %collective-permute-start.2) | collective-permute-done | bytes 262176 | tf_op jit(solution)/shard_map/ppermute | solution.py:393
  80.1 8.0 %collective-permute-done.1.refs_2_ = f32[512,128]{1,0:T(8,128)S(1)} collective-permute-done((f32[512,128]{1,0:T(8,128)S(1)}, f32[512,128]{1,0:T(8,128)S(1)}, u32[]{:S(2)}, u32[]{:S(2)}) %collective-permute-start.1) | collective-permute-done | bytes 262176 | tf_op jit(solution)/shard_map/ppermute | solution.py:393
  88.1 3.1 %solve.1 = (f32[512,128]{1,0:T(8,128)S(1)}, f32[512,128]{1,0:T(8,128)S(1)}, f32[512,128]{1,0:T(8,128)S(1)}, f32[512,128]{1,0:T(8,128)S(1)}) custom-call(s32[2]{0:T(128)S(1)} %pad_add_fusion.at, bf16[4,512,1024]{2,1,0:T(8,128)(2,1)S(1)} %split_diag.1.diag, f32[512,128]{1,0:T(8,128)S(1)} %bitcast.55, f32[512,128]{1,0:T(8,128)S(1)} %bitcast.58, ...), custom_call_target="tpu_custom_call" | custom-call | flops 1610612736 | bytes 4194304 | tf_op jit(solution)/shard_map/solve/pallas_call | solution.py:208
  91.2 4.4 %collective-permute-start.3 = (f32[512,128]{1,0:T(8,128)S(1)}, f32[512,128]{1,0:T(8,128)S(1)}, u32[]{:S(2)}, u32[]{:S(2)}) collective-permute-start(f32[512,128]{1,0:T(8,128)S(1)} %get-tuple-element.26), channel_id=1, source_target_pairs={{0,3},{1,0},{2,1},{3,2},{4,7},{5,4},{6,5},{7,6},{8,11},{9,8},{10,9... | collective-permute-start | bytes 786440 | tf_op jit(solution)/shard_map/ppermute | solution.py:393
  95.6 0.0 collective-permute-start.4
  95.6 0.6 collective-permute-start.5
  96.3 2.9 %sketch_tiles.3 = (f32[2,2048,128]{2,1,0:T(8,128)S(1)}, bf16[2,2048,256]{2,1,0:T(8,128)(2,1)S(1)}, bf16[2,2048,256]{2,1,0:T(8,128)(2,1)S(1)}, f32[2,128,128]{2,1,0:T(8,128)S(1)}) custom-call(f32[4,2048,128]{2,1,0:T(8,128)S(1)} %bitcast.51, f32[4,2048,128]{2,1,0:T(8,128)S(1)} %bitcast.53, f32[2048,128]{1,0:T(8,128)S(1)} %copy-done.2), custom_call_target="tpu_custom_call" | custom-call | flops 805306368 | bytes 10485760 | tf_op jit(solution)/shard_map/sketch_tiles/pallas_call | solution.py:119
  99.2 0.0 copy-start.10
  99.2 1.3 copy-done.10
  100.5 1.9 %collective-permute-done.3.refs_1_.refs_5_ = f32[512,128]{1,0:T(8,128)S(1)} collective-permute-done((f32[512,128]{1,0:T(8,128)S(1)}, f32[512,128]{1,0:T(8,128)S(1)}, u32[]{:S(2)}, u32[]{:S(2)}) %collective-permute-start.3) | collective-permute-done | bytes 262176 | tf_op jit(solution)/shard_map/ppermute | solution.py:393
  102.4 14.9 %collective-permute-done.4.refs_2_.refs_6_ = f32[512,128]{1,0:T(8,128)S(1)} collective-permute-done((f32[512,128]{1,0:T(8,128)S(1)}, f32[512,128]{1,0:T(8,128)S(1)}, u32[]{:S(2)}, u32[]{:S(2)}) %collective-permute-start.4) | collective-permute-done | bytes 262176 | tf_op jit(solution)/shard_map/ppermute | solution.py:393
  117.3 3.6 %partial_cores.1 = (f32[4,128,128]{2,1,0:T(8,128)S(1)}, f32[4,128,128]{2,1,0:T(8,128)S(1)}, f32[4,128,128]{2,1,0:T(8,128)S(1)}, f32[4,128,128]{2,1,0:T(8,128)S(1)}) custom-call(s32[2]{0:T(128)S(1)} %pad_add_fusion.at, f32[512,128]{1,0:T(8,128)S(1)} %get-tuple-element.25.refs_0_, f32[512,128]{1,0:T(8,128)S(1)} %collective-permute-done.3.refs_1_.refs_5_, ...), custom_call_target="tpu_custom_call" | custom-call | flops 805306368 | bytes 4194304 | tf_op jit(solution)/shard_map/partial_cores/pallas_call | solution.py:240
  121.0 1.6 collective-permute-start.10
  122.6 2.0 %collective-permute-start.11 = (f32[4,128,128]{2,1,0:T(8,128)S(1)}, f32[4,128,128]{2,1,0:T(8,128)S(1)}, u32[]{:S(2)}, u32[]{:S(2)}) collective-permute-start(f32[4,128,128]{2,1,0:T(8,128)S(1)} %get-tuple-element.31), channel_id=1, source_target_pairs={{0,2},{1,3},{2,0},{3,1},{4,6},{5,7},{6,4},{7,5},{8,10},{9,11},{10,... | collective-permute-start | bytes 786440 | tf_op jit(solution)/shard_map/ppermute | solution.py:393
  124.6 2.8 %collective-permute-start.12 = (f32[4,128,128]{2,1,0:T(8,128)S(1)}, f32[4,128,128]{2,1,0:T(8,128)S(1)}, u32[]{:S(2)}, u32[]{:S(2)}) collective-permute-start(f32[4,128,128]{2,1,0:T(8,128)S(1)} %get-tuple-element.32), channel_id=1, source_target_pairs={{0,3},{1,0},{2,1},{3,2},{4,7},{5,4},{6,5},{7,6},{8,11},{9,8},{10,9... | collective-permute-start | bytes 786440 | tf_op jit(solution)/shard_map/ppermute | solution.py:393
  127.5 3.1 %sketch_tiles.2 = (f32[2,2048,128]{2,1,0:T(8,128)S(1)}, bf16[2,2048,256]{2,1,0:T(8,128)(2,1)S(1)}, bf16[2,2048,256]{2,1,0:T(8,128)(2,1)S(1)}, f32[2,128,128]{2,1,0:T(8,128)S(1)}) custom-call(f32[4,2048,128]{2,1,0:T(8,128)S(1)} %bitcast.52, f32[4,2048,128]{2,1,0:T(8,128)S(1)} %bitcast.54, f32[2048,128]{1,0:T(8,128)S(1)} %copy-done.2), custom_call_target="tpu_custom_call" | custom-call | flops 805306368 | bytes 10485760 | tf_op jit(solution)/shard_map/sketch_tiles/pallas_call | solution.py:119
  130.6 1.4 copy-done.9
  132.0 3.6 %prepare.1 = (bf16[2048,256]{1,0:T(8,128)(2,1)S(1)}, f32[4,128,256]{2,1,0:T(8,128)S(1)}, f32[128,128]{1,0:T(8,128)S(1)}) custom-call(s32[2]{0:T(128)S(1)} %pad_add_fusion.at, f32[512,128]{1,0:T(8,128)S(1)} %bitcast.56, f32[512,128]{1,0:T(8,128)S(1)} %collective-permute-done.refs_1_, f32[512,128]{1,0:T(8,128)S(1)} %collective-permute-done.1.refs_2_, ...), custom_call_target="tpu_custom_call" | custom-call | flops 1610612736 | bytes 8388608 | tf_op jit(solution)/shard_map/prepare/pallas_call | solution.py:278
  135.6 4.0 %project.1 = (bf16[4,2048,256]{2,1,0:T(8,128)(2,1)S(1)}, f32[4,128,128]{2,1,0:T(8,128)S(1)}) custom-call(s32[2]{0:T(128)S(1)} %pad_add_fusion.at, f32[4,4,2,128,128]{4,3,2,1,0:T(8,128)S(1)} %pad_maximum_fusion.1.mine, f32[4,4,2,128,128]{4,3,2,1,0:T(8,128)} %collective-permute-done.22.other, f32[2048,128]{1,0:T(8,128)S(1)} %copy-done.2), custom_call_target="tpu_custom_call" | custom-call | flops 805306368 | bytes 8388608 | tf_op jit(solution)/shard_map/project/pallas_call | solution.py:179
  139.7 2.0 %copy-done.6 = bf16[4,2048,256]{2,1,0:T(8,128)(2,1)} copy-done((bf16[4,2048,256]{2,1,0:T(8,128)(2,1)}, bf16[4,2048,256]{2,1,0:T(8,128)(2,1)S(1)}, u32[]{:S(2)}) %copy-start.6) | copy-done | bytes 4194328
  141.6 0.7 copy-done.15
  142.3 0.0 collective-permute-done.12.refs_3_
  142.4 0.7 copy-done.21
  143.0 0.1 copy-done.22
  143.1 0.1 copy-done.23
  143.2 22.3 %recompress.1 = (f32[4,2048,128]{2,1,0:T(8,128)}, f32[4,2048,128]{2,1,0:T(8,128)}) custom-call(f32[4,128,128]{2,1,0:T(8,128)} %copy-done.14, f32[4,128,128]{2,1,0:T(8,128)} %copy-done.21, f32[4,128,128]{2,1,0:T(8,128)} %copy-done.22, f32[4,128,128]{2,1,0:T(8,128)} %copy-done.23, f32[4,128,128]{2,1,0:T(8,128)} %copy-done.15, f32[4,128,256]{2,1,0:T(8,128)} %copy-done.13, ...), custom_call_target="tpu_custom_call" | custom-call | flops 3221225472 | bytes 29360128 | tf_op jit(solution)/shard_map/recompress/pallas_call | solution.py:367
  (46 shorter events, 0.2 us)
Async XLA Ops:
  0.6 16.8 %copy-start.20 = (f32[2,512,128]{2,1,0:T(8,128)S(1)}, f32[2,512,128]{2,1,0:T(8,128)}, u32[]{:S(2)}) copy-start(f32[2,512,128]{2,1,0:T(8,128)} %param.13) | copy-start | bytes 1572868
  1.9 6.6 %collective-permute-start.14 = (f32[2,128,128]{2,1,0:T(8,128)S(1)}, f32[2,128,128]{2,1,0:T(8,128)S(1)}, u32[]{:S(2)}, u32[]{:S(2)}) collective-permute-start(f32[2,128,128]{2,1,0:T(8,128)S(1)} %get-tuple-element.53), channel_id=1, source_target_pairs={{0,16},{4,20},{8,24},{12,28},{16,0},{20,4},{24,8},{28,12},{1,17},{... | collective-permute-start | bytes 393224 | tf_op jit(solution)/shard_map/ppermute | solution.py:390
  4.9 6.4 %collective-permute-start.13 = (f32[2,128,128]{2,1,0:T(8,128)S(1)}, f32[2,128,128]{2,1,0:T(8,128)S(1)}, u32[]{:S(2)}, u32[]{:S(2)}) collective-permute-start(f32[2,128,128]{2,1,0:T(8,128)S(1)} %get-tuple-element.54), channel_id=1, source_target_pairs={{0,8},{4,12},{8,0},{12,4},{16,24},{20,28},{24,16},{28,20},{1,9},{5... | collective-permute-start | bytes 393224 | tf_op jit(solution)/shard_map/ppermute | solution.py:390
  6.4 7.3 %collective-permute-start.15 = (f32[2,128,128]{2,1,0:T(8,128)S(1)}, f32[2,128,128]{2,1,0:T(8,128)S(1)}, u32[]{:S(2)}, u32[]{:S(2)}) collective-permute-start(f32[2,128,128]{2,1,0:T(8,128)S(1)} %get-tuple-element.55), channel_id=1, source_target_pairs={{0,24},{4,28},{8,16},{12,20},{16,8},{20,12},{24,0},{28,4},{1,25},{... | collective-permute-start | bytes 393224 | tf_op jit(solution)/shard_map/ppermute | solution.py:390
  6.5 25.1 %collective-permute-start.6 = (f32[2,512,128]{2,1,0:T(8,128)}, f32[2,512,128]{2,1,0:T(8,128)S(1)}, u32[]{:S(2)}, u32[]{:S(2)}) collective-permute-start(f32[2,512,128]{2,1,0:T(8,128)} %param.13), channel_id=1, source_target_pairs={{0,8},{4,12},{8,0},{12,4},{16,24},{20,28},{24,16},{28,20},{1,9},{5... | collective-permute-start | bytes 1572872 | tf_op jit(solution)/shard_map/ppermute | solution.py:390
  13.8 7.5 %collective-permute-start.18 = (f32[2,128,128]{2,1,0:T(8,128)S(1)}, f32[2,128,128]{2,1,0:T(8,128)S(1)}, u32[]{:S(2)}, u32[]{:S(2)}) collective-permute-start(f32[2,128,128]{2,1,0:T(8,128)S(1)} %get-tuple-element.49), channel_id=1, source_target_pairs={{0,3},{1,0},{2,1},{3,2},{4,7},{5,4},{6,5},{7,6},{8,11},{9,8},{10,9... | collective-permute-start | bytes 393224 | tf_op jit(solution)/shard_map/ppermute | solution.py:393
  17.4 18.8 %collective-permute-start.8 = (f32[2,512,128]{2,1,0:T(8,128)S(1)}, f32[2,512,128]{2,1,0:T(8,128)S(1)}, u32[]{:S(2)}, u32[]{:S(2)}) collective-permute-start(f32[2,512,128]{2,1,0:T(8,128)S(1)} %copy-done.20), channel_id=1, source_target_pairs={{0,24},{4,28},{8,16},{12,20},{16,8},{20,12},{24,0},{28,4},{1,25},{... | collective-permute-start | bytes 1572872 | tf_op jit(solution)/shard_map/ppermute | solution.py:390
  20.2 36.6 %collective-permute-start.7 = (f32[2,512,128]{2,1,0:T(8,128)S(1)}, f32[2,512,128]{2,1,0:T(8,128)S(1)}, u32[]{:S(2)}, u32[]{:S(2)}) collective-permute-start(f32[2,512,128]{2,1,0:T(8,128)S(1)} %copy-done.20), channel_id=1, source_target_pairs={{0,16},{4,20},{8,24},{12,28},{16,0},{20,4},{24,8},{28,12},{1,17},{... | collective-permute-start | bytes 1572872 | tf_op jit(solution)/shard_map/ppermute | solution.py:390
  20.8 5.9 %collective-permute-start.17 = (f32[2,128,128]{2,1,0:T(8,128)S(1)}, f32[2,128,128]{2,1,0:T(8,128)S(1)}, u32[]{:S(2)}, u32[]{:S(2)}) collective-permute-start(f32[2,128,128]{2,1,0:T(8,128)S(1)} %get-tuple-element.50), channel_id=1, source_target_pairs={{0,2},{1,3},{2,0},{3,1},{4,6},{5,7},{6,4},{7,5},{8,10},{9,11},{10,... | collective-permute-start | bytes 393224 | tf_op jit(solution)/shard_map/ppermute | solution.py:393
  21.3 7.2 %collective-permute-start.16 = (f32[2,128,128]{2,1,0:T(8,128)S(1)}, f32[2,128,128]{2,1,0:T(8,128)S(1)}, u32[]{:S(2)}, u32[]{:S(2)}) collective-permute-start(f32[2,128,128]{2,1,0:T(8,128)S(1)} %get-tuple-element.51), channel_id=1, source_target_pairs={{0,1},{1,2},{2,3},{3,0},{4,5},{5,6},{6,7},{7,4},{8,9},{9,10},{10,1... | collective-permute-start | bytes 393224 | tf_op jit(solution)/shard_map/ppermute | solution.py:393
  28.6 29.7 %collective-permute-start.21 = (f32[4,2,128,128]{3,2,1,0:T(8,128)S(1)}, f32[4,2,128,128]{3,2,1,0:T(8,128)S(1)}, u32[]{:S(2)}, u32[]{:S(2)}) collective-permute-start(f32[4,2,128,128]{3,2,1,0:T(8,128)S(1)} %pad_maximum_fusion.3), channel_id=1, source_target_pairs={{0,24},{4,28},{8,16},{12,20},{16,8},{20,12},{24,0},{28,4},{1,25},{... | collective-permute-start | bytes 1572872 | tf_op jit(solution)/shard_map/ppermute | solution.py:390
  30.4 33.8 %collective-permute-start.20 = (f32[4,2,128,128]{3,2,1,0:T(8,128)S(1)}, f32[4,2,128,128]{3,2,1,0:T(8,128)S(1)}, u32[]{:S(2)}, u32[]{:S(2)}) collective-permute-start(f32[4,2,128,128]{3,2,1,0:T(8,128)S(1)} %pad_maximum_fusion.3), channel_id=1, source_target_pairs={{0,16},{4,20},{8,24},{12,28},{16,0},{20,4},{24,8},{28,12},{1,17},{... | collective-permute-start | bytes 1572872 | tf_op jit(solution)/shard_map/ppermute | solution.py:390
  31.6 32.7 %collective-permute-start.19 = (f32[4,2,128,128]{3,2,1,0:T(8,128)S(1)}, f32[4,2,128,128]{3,2,1,0:T(8,128)S(1)}, u32[]{:S(2)}, u32[]{:S(2)}) collective-permute-start(f32[4,2,128,128]{3,2,1,0:T(8,128)S(1)} %pad_maximum_fusion.3), channel_id=1, source_target_pairs={{0,8},{4,12},{8,0},{12,4},{16,24},{20,28},{24,16},{28,20},{1,9},{5... | collective-permute-start | bytes 1572872 | tf_op jit(solution)/shard_map/ppermute | solution.py:390
  58.3 59.0 %collective-permute-start.9 = (f32[4,2,512,128]{3,2,1,0:T(8,128)}, f32[4,2,512,128]{3,2,1,0:T(8,128)}, u32[]{:S(2)}, u32[]{:S(2)}) collective-permute-start(f32[4,2,512,128]{3,2,1,0:T(8,128)} %pad_maximum_fusion.refs_4_), channel_id=1, source_target_pairs={{0,4},{4,0},{8,12},{12,8},{16,20},{20,16},{24,28},{28,24},{1,5},{5... | collective-permute-start | bytes 6291464 | tf_op jit(solution)/shard_map/ppermute | solution.py:390
  64.2 1.0 copy-start.7
  64.2 1.0 copy-start.16
  64.5 71.2 %collective-permute-start.22 = (f32[4,4,2,128,128]{4,3,2,1,0:T(8,128)S(1)}, f32[4,4,2,128,128]{4,3,2,1,0:T(8,128)}, u32[]{:S(2)}, u32[]{:S(2)}) collective-permute-start(f32[4,4,2,128,128]{4,3,2,1,0:T(8,128)S(1)} %pad_maximum_fusion.1.mine), channel_id=1, source_target_pairs={{0,4},{4,0},{8,12},{12,8},{16,20},{20,16},{24,28},{28,24},{1,5},{5... | collective-permute-start | bytes 6291464 | tf_op jit(solution)/shard_map/ppermute | solution.py:390
  65.3 14.8 %collective-permute-start.2 = (f32[512,128]{1,0:T(8,128)S(1)}, f32[512,128]{1,0:T(8,128)S(1)}, u32[]{:S(2)}, u32[]{:S(2)}) collective-permute-start(f32[512,128]{1,0:T(8,128)S(1)} %get-tuple-element.56), channel_id=1, source_target_pairs={{0,3},{1,0},{2,1},{3,2},{4,7},{5,4},{6,5},{7,6},{8,11},{9,8},{10,9... | collective-permute-start | bytes 786440 | tf_op jit(solution)/shard_map/ppermute | solution.py:393
  65.8 14.3 %collective-permute-start = (f32[512,128]{1,0:T(8,128)S(1)}, f32[512,128]{1,0:T(8,128)S(1)}, u32[]{:S(2)}, u32[]{:S(2)}) collective-permute-start(f32[512,128]{1,0:T(8,128)S(1)} %get-tuple-element.57), channel_id=1, source_target_pairs={{0,1},{1,2},{2,3},{3,0},{4,5},{5,6},{6,7},{7,4},{8,9},{9,10},{10,1... | collective-permute-start | bytes 786440 | tf_op jit(solution)/shard_map/ppermute | solution.py:393
  67.4 20.7 %collective-permute-start.1 = (f32[512,128]{1,0:T(8,128)S(1)}, f32[512,128]{1,0:T(8,128)S(1)}, u32[]{:S(2)}, u32[]{:S(2)}) collective-permute-start(f32[512,128]{1,0:T(8,128)S(1)} %get-tuple-element.58), channel_id=1, source_target_pairs={{0,2},{1,3},{2,0},{3,1},{4,6},{5,7},{6,4},{7,5},{8,10},{9,11},{10,... | collective-permute-start | bytes 786440 | tf_op jit(solution)/shard_map/ppermute | solution.py:393
  67.4 2.2 %copy-start.5 = (f32[512,2048]{1,0:T(8,128)S(1)}, f32[512,2048]{1,0:T(8,128)}, u32[]{:S(2)}) copy-start(f32[512,2048]{1,0:T(8,128)} %diag.1) | copy-start | bytes 12582916
  69.6 26.7 %copy-start.1 = (f32[1,4,2048,128]{3,2,1,0:T(8,128)S(1)}, f32[1,4,2048,128]{3,2,1,0:T(8,128)}, u32[]{:S(2)}) copy-start(f32[1,4,2048,128]{3,2,1,0:T(8,128)} %param.9) | copy-start | bytes 12582916
  88.1 8.2 %copy-start = (f32[1,4,2048,128]{3,2,1,0:T(8,128)S(1)}, f32[1,4,2048,128]{3,2,1,0:T(8,128)}, u32[]{:S(2)}) copy-start(f32[1,4,2048,128]{3,2,1,0:T(8,128)} %param.8) | copy-start | bytes 12582916
  88.1 8.2 %copy-start.2 = (f32[2048,128]{1,0:T(8,128)S(1)}, f32[2048,128]{1,0:T(8,128)}, u32[]{:S(2)}) copy-start(f32[2048,128]{1,0:T(8,128)} %s_ref.5) | copy-start | bytes 3145732
  91.2 11.2 %collective-permute-start.3 = (f32[512,128]{1,0:T(8,128)S(1)}, f32[512,128]{1,0:T(8,128)S(1)}, u32[]{:S(2)}, u32[]{:S(2)}) collective-permute-start(f32[512,128]{1,0:T(8,128)S(1)} %get-tuple-element.26), channel_id=1, source_target_pairs={{0,3},{1,0},{2,1},{3,2},{4,7},{5,4},{6,5},{7,6},{8,11},{9,8},{10,9... | collective-permute-start | bytes 786440 | tf_op jit(solution)/shard_map/ppermute | solution.py:393
  95.6 21.7 %collective-permute-start.4 = (f32[512,128]{1,0:T(8,128)S(1)}, f32[512,128]{1,0:T(8,128)S(1)}, u32[]{:S(2)}, u32[]{:S(2)}) collective-permute-start(f32[512,128]{1,0:T(8,128)S(1)} %get-tuple-element.27), channel_id=1, source_target_pairs={{0,2},{1,3},{2,0},{3,1},{4,6},{5,7},{6,4},{7,5},{8,10},{9,11},{10,... | collective-permute-start | bytes 786440 | tf_op jit(solution)/shard_map/ppermute | solution.py:393
  95.6 21.7 %collective-permute-start.5 = (f32[512,128]{1,0:T(8,128)S(1)}, f32[512,128]{1,0:T(8,128)S(1)}, u32[]{:S(2)}, u32[]{:S(2)}) collective-permute-start(f32[512,128]{1,0:T(8,128)S(1)} %get-tuple-element.28), channel_id=1, source_target_pairs={{0,1},{1,2},{2,3},{3,0},{4,5},{5,6},{6,7},{7,4},{8,9},{9,10},{10,1... | collective-permute-start | bytes 786440 | tf_op jit(solution)/shard_map/ppermute | solution.py:393
  99.2 1.3 copy-start.10
  100.5 20.5 %copy-start.8 = (bf16[2,2048,256]{2,1,0:T(8,128)(2,1)}, bf16[2,2048,256]{2,1,0:T(8,128)(2,1)S(1)}, u32[]{:S(2)}) copy-start(bf16[2,2048,256]{2,1,0:T(8,128)(2,1)S(1)} %get-tuple-element.43.refs_12_) | copy-start | bytes 6291460
  100.5 20.5 %copy-start.17 = (f32[2,128,128]{2,1,0:T(8,128)}, f32[2,128,128]{2,1,0:T(8,128)S(1)}, u32[]{:S(2)}) copy-start(f32[2,128,128]{2,1,0:T(8,128)S(1)} %get-tuple-element.41.refs_8_) | copy-start | bytes 393220
  100.5 31.5 %copy-start.3 = (f32[2,2048,128]{2,1,0:T(8,128)}, f32[2,2048,128]{2,1,0:T(8,128)S(1)}, u32[]{:S(2)}) copy-start(f32[2,2048,128]{2,1,0:T(8,128)S(1)} %get-tuple-element.36.refs_10_) | copy-start | bytes 6291460
  121.0 9.6 %copy-start.14 = (f32[4,128,128]{2,1,0:T(8,128)}, f32[4,128,128]{2,1,0:T(8,128)S(1)}, u32[]{:S(2)}) copy-start(f32[4,128,128]{2,1,0:T(8,128)S(1)} %get-tuple-element.29.refs_0_) | copy-start | bytes 786436
  121.0 21.3 %collective-permute-start.10 = (f32[4,128,128]{2,1,0:T(8,128)S(1)}, f32[4,128,128]{2,1,0:T(8,128)S(1)}, u32[]{:S(2)}, u32[]{:S(2)}) collective-permute-start(f32[4,128,128]{2,1,0:T(8,128)S(1)} %get-tuple-element.30), channel_id=1, source_target_pairs={{0,1},{1,2},{2,3},{3,0},{4,5},{5,6},{6,7},{7,4},{8,9},{9,10},{10,1... | collective-permute-start | bytes 786440 | tf_op jit(solution)/shard_map/ppermute | solution.py:393
  122.6 19.7 %collective-permute-start.11 = (f32[4,128,128]{2,1,0:T(8,128)S(1)}, f32[4,128,128]{2,1,0:T(8,128)S(1)}, u32[]{:S(2)}, u32[]{:S(2)}) collective-permute-start(f32[4,128,128]{2,1,0:T(8,128)S(1)} %get-tuple-element.31), channel_id=1, source_target_pairs={{0,2},{1,3},{2,0},{3,1},{4,6},{5,7},{6,4},{7,5},{8,10},{9,11},{10,... | collective-permute-start | bytes 786440 | tf_op jit(solution)/shard_map/ppermute | solution.py:393
  124.6 7.4 %copy-start.11 = (bf16[2,2048,256]{2,1,0:T(8,128)(2,1)S(1)}, bf16[2,2048,256]{2,1,0:T(8,128)(2,1)}, u32[]{:S(2)}) copy-start(bf16[2,2048,256]{2,1,0:T(8,128)(2,1)} %copy-done.10) | copy-start | bytes 6291460
  124.6 17.7 %collective-permute-start.12 = (f32[4,128,128]{2,1,0:T(8,128)S(1)}, f32[4,128,128]{2,1,0:T(8,128)S(1)}, u32[]{:S(2)}, u32[]{:S(2)}) collective-permute-start(f32[4,128,128]{2,1,0:T(8,128)S(1)} %get-tuple-element.32), channel_id=1, source_target_pairs={{0,3},{1,0},{2,1},{3,2},{4,7},{5,4},{6,5},{7,6},{8,11},{9,8},{10,9... | collective-permute-start | bytes 786440 | tf_op jit(solution)/shard_map/ppermute | solution.py:393
  130.6 1.4 copy-start.9
  132.0 3.6 %copy-start.4 = (f32[2,2048,128]{2,1,0:T(8,128)}, f32[2,2048,128]{2,1,0:T(8,128)S(1)}, u32[]{:S(2)}) copy-start(f32[2,2048,128]{2,1,0:T(8,128)S(1)} %get-tuple-element.34.refs_8_.refs_9_) | copy-start | bytes 6291460
  132.0 3.6 %copy-start.18 = (f32[2,128,128]{2,1,0:T(8,128)}, f32[2,128,128]{2,1,0:T(8,128)S(1)}, u32[]{:S(2)}) copy-start(f32[2,128,128]{2,1,0:T(8,128)S(1)} %get-tuple-element.40.refs_7_) | copy-start | bytes 393220
  135.6 4.1 %copy-start.12 = (bf16[2048,256]{1,0:T(8,128)(2,1)}, bf16[2048,256]{1,0:T(8,128)(2,1)S(1)}, u32[]{:S(2)}) copy-start(bf16[2048,256]{1,0:T(8,128)(2,1)S(1)} %get-tuple-element.45.refs_14_) | copy-start | bytes 3145732
  135.6 4.1 %copy-start.13 = (f32[4,128,256]{2,1,0:T(8,128)}, f32[4,128,256]{2,1,0:T(8,128)S(1)}, u32[]{:S(2)}) copy-start(f32[4,128,256]{2,1,0:T(8,128)S(1)} %get-tuple-element.38.refs_5_) | copy-start | bytes 1572868
  135.6 4.1 %copy-start.19 = (f32[128,128]{1,0:T(8,128)}, f32[128,128]{1,0:T(8,128)S(1)}, u32[]{:S(2)}) copy-start(f32[128,128]{1,0:T(8,128)S(1)} %get-tuple-element.39.refs_6_) | copy-start | bytes 196612
  139.6 2.0 %copy-start.6 = (bf16[4,2048,256]{2,1,0:T(8,128)(2,1)}, bf16[4,2048,256]{2,1,0:T(8,128)(2,1)S(1)}, u32[]{:S(2)}) copy-start(bf16[4,2048,256]{2,1,0:T(8,128)(2,1)S(1)} %get-tuple-element.44.refs_13_) | copy-start | bytes 12582916
  141.6 0.7 copy-start.15
  142.3 0.7 copy-start.21
  142.3 0.8 copy-start.22
  142.4 0.9 copy-start.23

commit v6 on v5

--- a/solution.py
+++ b/solution.py
@@ -61,7 +61,7 @@
 
 
 def eliminate(work, tiles, k):
-    b = 8
+    b = 16 if k % 16 == 0 else 8
     row = lax.broadcasted_iota(jnp.int32, (b, k), 0)
     for top in range(0, k, b):
         left, right, cols, scale = [], [], [], []
@@ -124,7 +124,7 @@
         out_shape=[jax.ShapeDtypeStruct((tiles, n, k), f32)]
         + [jax.ShapeDtypeStruct((tiles, n, 2 * k), bf16)] * 2
         + [jax.ShapeDtypeStruct((tiles, k, k), f32)],
-        compiler_params=pltpu.CompilerParams(vmem_limit_bytes=36 * 1024 * 1024),
+        compiler_params=pltpu.CompilerParams(vmem_limit_bytes=57 * 1024 * 1024),
         cost_estimate=pl.CostEstimate(flops=6 * tiles * n * k * k * 2, bytes_accessed=20 * tiles * n * k, transcendentals=0),
         name="sketch_tiles",
     )(tile_u, tile_v, sketch)
@@ -299,9 +299,10 @@
     crosses, refs = refs[:groups], refs[groups:]
     bases, v_parts, refs = refs[:groups], refs[groups : 2 * groups], refs[2 * groups :]
     (w_parts, row_in, new_u, new_v), refs = refs[:4], refs[4:]
-    s, tv, cu, sp, out, work, cross, cores, row_parts, sem, row_sem = refs
+    s, tv, cu, sp, out, work, cross, cores, arrived, row_parts, sem, row_sem = refs
     root = math.sqrt(n)
-    row_copy = pltpu.make_async_copy(row_in, row_parts, row_sem)
+    core_copies = [pltpu.make_async_copy(x, arrived.at[d], row_sem.at[1 + d]) for d, x in enumerate(core_parts)]
+    row_copy = pltpu.make_async_copy(row_in, row_parts, row_sem.at[0])
     early, late, outs = [], [], []
     for t, (g, j) in enumerate(place):
         early.append(pltpu.make_async_copy(bases[g].at[j], s.at[t], sem.at[t]))
@@ -313,12 +314,16 @@
             pltpu.make_async_copy(s.at[t], new_u.at[t], sem.at[3 * tiles + t]),
             pltpu.make_async_copy(out.at[t], new_v.at[t], sem.at[4 * tiles + t]),
         ))
+    for x in core_copies:
+        x.start()
     row_copy.start()
     for x in early:
         x.start()
-    total = core_parts[0][...]
-    for p in core_parts[1:]:
-        total = total + p[...]
+    for x in core_copies:
+        x.wait()
+    total = arrived[0]
+    for d in range(1, n_col):
+        total = total + arrived[d]
     cores[...] = total
     eye = jnp.where(
         lax.broadcasted_iota(jnp.int32, (k, k), 0) == lax.broadcasted_iota(jnp.int32, (k, k), 1), 1.0, 0.0
@@ -366,15 +371,16 @@
     split = lambda: VMEM((tiles, n, 2 * k), bf16)
     return pl.pallas_call(
         functools.partial(recompress_kernel, n, k, n_col, sizes),
-        in_specs=[vmem] * (n_col + 3 + groups) + [any_] * (2 * groups + 2),
+        in_specs=[any_] * n_col + [vmem] * (3 + groups) + [any_] * (2 * groups + 2),
         out_specs=[any_, any_],
         out_shape=[jax.ShapeDtypeStruct((tiles, n, k), f32)] * 2,
         scratch_shapes=[
             full(), split(), split(), split(), full(),
             VMEM((tiles, k, 2 * k), f32), VMEM((tiles, k, 2 * k), f32), VMEM((tiles, k, k), f32),
-            VMEM((n, 2 * k), bf16),
-            pltpu.SemaphoreType.DMA((5 * tiles,)), pltpu.SemaphoreType.DMA,
+            VMEM((n_col, tiles, k, k), f32), VMEM((n, 2 * k), bf16),
+            pltpu.SemaphoreType.DMA((5 * tiles,)), pltpu.SemaphoreType.DMA((1 + n_col,)),
         ],
+        compiler_params=pltpu.CompilerParams(vmem_limit_bytes=44 * 1024 * 1024),
         cost_estimate=pl.CostEstimate(flops=24 * tiles * n * k * k, bytes_accessed=28 * tiles * n * k, transcendentals=0),
         name="recompress",
     )(*core_parts, small, with_row, row_row, *crosses, *bases, *v_parts, w_parts, row_parts)
@@ -411,7 +417,7 @@
     tiles = tile_u.shape[1]
     diag = split_diag(diag_inverse)
     groups = []
-    for begin, end in ((0, tiles // 2), (tiles // 2, tiles)):
+    for begin, end in ((0, 3 * tiles // 4), (3 * tiles // 4, tiles)):
         groups.append(sketch_tiles(tile_u[0], tile_v[0], sketch, begin, end))
     bases, v_parts, u_parts, crosses = zip(*groups)
     sums = solve(at, diag, row_u, [row_v] + first)

time: 168 us -> 169 us (level)
  waiting for transfers between devices: 77.5 us -> 73.1 us
  Pallas kernels: 43 us -> 47.1 us
  local copies, waits for them, and re-layouts: 10.5 us -> 13.3 us
    pallas_call x2, Pallas kernels: 5.97 us -> 13 us  [sketch_tiles(): pl.pallas_call(sketched, grid=(tiles,), in_specs=[block, block, pl.BlockS...]
    ppermute x12, waiting for transfers between devices: 41.6 us -> 37.2 us  [shift(): return lax.ppermute(x, 'col', pairs)]
    pallas_call x1, Pallas kernels: 22.3 us -> 19.1 us  [recompress(): pl.pallas_call(functools.partial(recompress_kernel, n, k, n_col, sizes),...]
    unnamed x48 -> x40, local copies, waits for them, and re-layouts: 9.23 us -> 12.1 us
  transfers between devices with their start and end apart: 23 -> 23, of which waited for: 12 -> 11; matrix products, arithmetic and copies ran while one was open for 1% -> 1% of each run, Pallas kernels for 13% -> 17%
where the time goes in v6:
time: 169 us; the launch traced here: 168 us
  waiting for transfers between devices  73.1 us (43%)
  Pallas kernels  47.1 us (28%)
  starting transfers between devices  31.7 us (19%)
  local copies, waits for them, and re-layouts  13.3 us (8%)
  other arithmetic  1.91 us (1%)
    ppermute x12, waiting for transfers between devices, shift(): return lax.ppermute(x, 'col', pairs)  37.2 us
    ppermute x11, waiting for transfers between devices, partner(): return lax.ppermute(x, 'row', [(a, a ^ m) for a in range(n_row)])  35.9 us
    pallas_call x1, Pallas kernels, recompress(): pl.pallas_call(functools.partial(recompress_kernel, n, k, n_col, sizes),...  19.1 us
    ppermute x12, starting transfers between devices, shift(): return lax.ppermute(x, 'col', pairs)  18.2 us
    ppermute x11, starting transfers between devices, partner(): return lax.ppermute(x, 'row', [(a, a ^ m) for a in range(n_row)])  13.5 us
    pallas_call x2, Pallas kernels, sketch_tiles(): pl.pallas_call(sketched, grid=(tiles,), in_specs=[block, block, pl.BlockS...  13 us
    unnamed x40, local copies, waits for them, and re-layouts  12.1 us
    pallas_call x1, Pallas kernels, partial_cores(): pl.pallas_call(functools.partial(cores_kernel, n_col), in_specs=[pl.Block...  4.33 us
  transfers between devices with their start and end apart: 23, of which 11 were waited for; matrix products, arithmetic and copies ran while one was open for 1% of the time, Pallas kernels for 17%

profile of v6, /device:TPU:0, one launch (start us, length us, event | category | flops | bytes accessed | tf_op | source)
XLA Modules:
  0.0 168.2 jit_solution(16245324266526391501)
XLA Ops:
  0.6 0.0 copy-start.19
  0.7 1.2 dynamic-slice_bitcast_fusion.6
  1.9 3.1 %collective-permute-start.14 = (f32[2,128,128]{2,1,0:T(8,128)S(1)}, f32[2,128,128]{2,1,0:T(8,128)S(1)}, u32[]{:S(2)}, u32[]{:S(2)}) collective-permute-start(f32[2,128,128]{2,1,0:T(8,128)S(1)} %get-tuple-element.53), channel_id=1, source_target_pairs={{0,16},{4,20},{8,24},{12,28},{16,0},{20,4},{24,8},{28,12},{1,17},{... | collective-permute-start | bytes 393224 | tf_op jit(solution)/shard_map/ppermute | solution.py:396
  4.9 1.5 collective-permute-start.13
  6.4 0.0 collective-permute-start.15
  6.5 1.9 %collective-permute-start.6 = (f32[2,512,128]{2,1,0:T(8,128)}, f32[2,512,128]{2,1,0:T(8,128)S(1)}, u32[]{:S(2)}, u32[]{:S(2)}) collective-permute-start(f32[2,512,128]{2,1,0:T(8,128)} %param.13), channel_id=1, source_target_pairs={{0,8},{4,12},{8,0},{12,4},{16,24},{20,28},{24,16},{28,20},{1,9},{5... | collective-permute-start | bytes 1572872 | tf_op jit(solution)/shard_map/ppermute | solution.py:396
  8.4 0.0 collective-permute-done.14
  8.4 2.9 %collective-permute-done.13 = f32[2,128,128]{2,1,0:T(8,128)S(1)} collective-permute-done((f32[2,128,128]{2,1,0:T(8,128)S(1)}, f32[2,128,128]{2,1,0:T(8,128)S(1)}, u32[]{:S(2)}, u32[]{:S(2)}) %collective-permute-start.13) | collective-permute-done | bytes 131104 | tf_op jit(solution)/shard_map/ppermute | solution.py:396
  11.3 2.4 %collective-permute-done.15 = f32[2,128,128]{2,1,0:T(8,128)S(1)} collective-permute-done((f32[2,128,128]{2,1,0:T(8,128)S(1)}, f32[2,128,128]{2,1,0:T(8,128)S(1)}, u32[]{:S(2)}, u32[]{:S(2)}) %collective-permute-start.15) | collective-permute-done | bytes 131104 | tf_op jit(solution)/shard_map/ppermute | solution.py:396
  13.8 3.7 %collective-permute-start.18 = (f32[2,128,128]{2,1,0:T(8,128)S(1)}, f32[2,128,128]{2,1,0:T(8,128)S(1)}, u32[]{:S(2)}, u32[]{:S(2)}) collective-permute-start(f32[2,128,128]{2,1,0:T(8,128)S(1)} %get-tuple-element.49), channel_id=1, source_target_pairs={{0,3},{1,0},{2,1},{3,2},{4,7},{5,4},{6,5},{7,6},{8,11},{9,8},{10,9... | collective-permute-start | bytes 393224 | tf_op jit(solution)/shard_map/ppermute | solution.py:399
  17.4 2.8 %collective-permute-start.8 = (f32[2,512,128]{2,1,0:T(8,128)S(1)}, f32[2,512,128]{2,1,0:T(8,128)S(1)}, u32[]{:S(2)}, u32[]{:S(2)}) collective-permute-start(f32[2,512,128]{2,1,0:T(8,128)S(1)} %copy-done.19), channel_id=1, source_target_pairs={{0,24},{4,28},{8,16},{12,20},{16,8},{20,12},{24,0},{28,4},{1,25},{... | collective-permute-start | bytes 1572872 | tf_op jit(solution)/shard_map/ppermute | solution.py:396
  20.2 0.5 collective-permute-start.7
  20.8 0.0 collective-permute-start.17
  20.8 0.6 collective-permute-done.18
  21.3 1.0 collective-permute-start.16
  22.3 4.4 %collective-permute-done.17 = f32[2,128,128]{2,1,0:T(8,128)S(1)} collective-permute-done((f32[2,128,128]{2,1,0:T(8,128)S(1)}, f32[2,128,128]{2,1,0:T(8,128)S(1)}, u32[]{:S(2)}, u32[]{:S(2)}) %collective-permute-start.17) | collective-permute-done | bytes 131104 | tf_op jit(solution)/shard_map/ppermute | solution.py:399
  26.7 1.9 %collective-permute-done.16 = f32[2,128,128]{2,1,0:T(8,128)S(1)} collective-permute-done((f32[2,128,128]{2,1,0:T(8,128)S(1)}, f32[2,128,128]{2,1,0:T(8,128)S(1)}, u32[]{:S(2)}, u32[]{:S(2)}) %collective-permute-start.16) | collective-permute-done | bytes 131104 | tf_op jit(solution)/shard_map/ppermute | solution.py:399
  28.6 1.8 %collective-permute-start.21 = (f32[4,2,128,128]{3,2,1,0:T(8,128)S(1)}, f32[4,2,128,128]{3,2,1,0:T(8,128)S(1)}, u32[]{:S(2)}, u32[]{:S(2)}) collective-permute-start(f32[4,2,128,128]{3,2,1,0:T(8,128)S(1)} %pad_maximum_fusion.3), channel_id=1, source_target_pairs={{0,24},{4,28},{8,16},{12,20},{16,8},{20,12},{24,0},{28,4},{1,25},{... | collective-permute-start | bytes 1572872 | tf_op jit(solution)/shard_map/ppermute | solution.py:396
  30.4 1.1 collective-permute-start.20
  31.6 0.0 collective-permute-done.6
  31.6 0.6 collective-permute-start.19
  32.2 4.1 %collective-permute-done.8 = f32[2,512,128]{2,1,0:T(8,128)S(1)} collective-permute-done((f32[2,512,128]{2,1,0:T(8,128)S(1)}, f32[2,512,128]{2,1,0:T(8,128)S(1)}, u32[]{:S(2)}, u32[]{:S(2)}) %collective-permute-start.8) | collective-permute-done | bytes 524320 | tf_op jit(solution)/shard_map/ppermute | solution.py:396
  36.3 20.6 %collective-permute-done.7 = f32[2,512,128]{2,1,0:T(8,128)S(1)} collective-permute-done((f32[2,512,128]{2,1,0:T(8,128)S(1)}, f32[2,512,128]{2,1,0:T(8,128)S(1)}, u32[]{:S(2)}, u32[]{:S(2)}) %collective-permute-start.7) | collective-permute-done | bytes 524320 | tf_op jit(solution)/shard_map/ppermute | solution.py:396
  56.9 1.5 pad_maximum_fusion.refs_4_
  58.4 0.0 collective-permute-start.9
  58.4 0.0 collective-permute-done.21
  58.4 5.9 %collective-permute-done.20 = f32[4,2,128,128]{3,2,1,0:T(8,128)S(1)} collective-permute-done((f32[4,2,128,128]{3,2,1,0:T(8,128)S(1)}, f32[4,2,128,128]{3,2,1,0:T(8,128)S(1)}, u32[]{:S(2)}, u32[]{:S(2)}) %collective-permute-start.20) | collective-permute-done | bytes 524320 | tf_op jit(solution)/shard_map/ppermute | solution.py:396
  64.2 0.0 collective-permute-done.19
  64.2 0.2 pad_maximum_fusion.1.mine
  64.5 0.1 collective-permute-start.22
  64.5 0.6 copy-done.7
  65.2 0.1 copy-done.10
  65.2 0.1 broadcast_select_fusion
  65.3 0.5 collective-permute-start.2
  65.8 1.6 collective-permute-start
  67.4 0.0 collective-permute-start.1
  67.4 2.2 %copy-done.2 = f32[512,2048]{1,0:T(8,128)S(1)} copy-done((f32[512,2048]{1,0:T(8,128)S(1)}, f32[512,2048]{1,0:T(8,128)}, u32[]{:S(2)}) %copy-start.2) | copy-done | bytes 4194328
  69.6 0.5 split_diag.1.diag
  70.1 0.1 pad_add_fusion.at
  70.1 10.0 %collective-permute-done.2.refs_3_ = f32[512,128]{1,0:T(8,128)S(1)} collective-permute-done((f32[512,128]{1,0:T(8,128)S(1)}, f32[512,128]{1,0:T(8,128)S(1)}, u32[]{:S(2)}, u32[]{:S(2)}) %collective-permute-start.2) | collective-permute-done | bytes 262176 | tf_op jit(solution)/shard_map/ppermute | solution.py:399
  80.1 0.0 collective-permute-done.refs_1_
  80.1 8.0 %collective-permute-done.1.refs_2_ = f32[512,128]{1,0:T(8,128)S(1)} collective-permute-done((f32[512,128]{1,0:T(8,128)S(1)}, f32[512,128]{1,0:T(8,128)S(1)}, u32[]{:S(2)}, u32[]{:S(2)}) %collective-permute-start.1) | collective-permute-done | bytes 262176 | tf_op jit(solution)/shard_map/ppermute | solution.py:399
  88.1 3.1 %solve.1 = (f32[512,128]{1,0:T(8,128)S(1)}, f32[512,128]{1,0:T(8,128)S(1)}, f32[512,128]{1,0:T(8,128)S(1)}, f32[512,128]{1,0:T(8,128)S(1)}) custom-call(s32[2]{0:T(128)S(1)} %pad_add_fusion.at, bf16[4,512,1024]{2,1,0:T(8,128)(2,1)S(1)} %split_diag.1.diag, f32[512,128]{1,0:T(8,128)S(1)} %bitcast.51, f32[512,128]{1,0:T(8,128)S(1)} %bitcast.54, ...), custom_call_target="tpu_custom_call" | custom-call | flops 1610612736 | bytes 4194304 | tf_op jit(solution)/shard_map/solve/pallas_call | solution.py:208
  91.2 4.4 %collective-permute-start.3 = (f32[512,128]{1,0:T(8,128)S(1)}, f32[512,128]{1,0:T(8,128)S(1)}, u32[]{:S(2)}, u32[]{:S(2)}) collective-permute-start(f32[512,128]{1,0:T(8,128)S(1)} %get-tuple-element.26), channel_id=1, source_target_pairs={{0,3},{1,0},{2,1},{3,2},{4,7},{5,4},{6,5},{7,6},{8,11},{9,8},{10,9... | collective-permute-start | bytes 786440 | tf_op jit(solution)/shard_map/ppermute | solution.py:399
  95.6 0.0 collective-permute-start.4
  95.6 0.6 collective-permute-start.5
  96.3 8.6 %sketch_tiles.2 = (f32[3,2048,128]{2,1,0:T(8,128)}, bf16[3,2048,256]{2,1,0:T(8,128)(2,1)}, bf16[3,2048,256]{2,1,0:T(8,128)(2,1)}, f32[3,128,128]{2,1,0:T(8,128)}) custom-call(f32[4,2048,128]{2,1,0:T(8,128)} %bitcast.55, f32[4,2048,128]{2,1,0:T(8,128)} %bitcast.57, f32[2048,128]{1,0:T(8,128)} %s_ref.5), custom_call_target="tpu_custom_call" | custom-call | flops 1207959552 | bytes 15728640 | tf_op jit(solution)/shard_map/sketch_tiles/pallas_call | solution.py:119
  104.9 12.4 %collective-permute-done.4.refs_2_.refs_6_ = f32[512,128]{1,0:T(8,128)S(1)} collective-permute-done((f32[512,128]{1,0:T(8,128)S(1)}, f32[512,128]{1,0:T(8,128)S(1)}, u32[]{:S(2)}, u32[]{:S(2)}) %collective-permute-start.4) | collective-permute-done | bytes 262176 | tf_op jit(solution)/shard_map/ppermute | solution.py:399
  117.3 4.3 %partial_cores.1 = (f32[4,128,128]{2,1,0:T(8,128)S(1)}, f32[4,128,128]{2,1,0:T(8,128)}, f32[4,128,128]{2,1,0:T(8,128)}, f32[4,128,128]{2,1,0:T(8,128)}) custom-call(s32[2]{0:T(128)S(1)} %pad_add_fusion.at, f32[512,128]{1,0:T(8,128)S(1)} %get-tuple-element.25.refs_0_, f32[512,128]{1,0:T(8,128)S(1)} %collective-permute-done.3.refs_1_.refs_5_, ...), custom_call_target="tpu_custom_call" | custom-call | flops 805306368 | bytes 4194304 | tf_op jit(solution)/shard_map/partial_cores/pallas_call | solution.py:240
  121.7 1.6 collective-permute-start.10
  123.3 1.9 %collective-permute-start.11 = (f32[4,128,128]{2,1,0:T(8,128)}, f32[4,128,128]{2,1,0:T(8,128)S(1)}, u32[]{:S(2)}, u32[]{:S(2)}) collective-permute-start(f32[4,128,128]{2,1,0:T(8,128)} %get-tuple-element.31), channel_id=1, source_target_pairs={{0,2},{1,3},{2,0},{3,1},{4,6},{5,7},{6,4},{7,5},{8,10},{9,11},{10,... | collective-permute-start | bytes 786440 | tf_op jit(solution)/shard_map/ppermute | solution.py:399
  125.2 2.9 %collective-permute-start.12 = (f32[4,128,128]{2,1,0:T(8,128)}, f32[4,128,128]{2,1,0:T(8,128)}, u32[]{:S(2)}, u32[]{:S(2)}) collective-permute-start(f32[4,128,128]{2,1,0:T(8,128)} %get-tuple-element.32), channel_id=1, source_target_pairs={{0,3},{1,0},{2,1},{3,2},{4,7},{5,4},{6,5},{7,6},{8,11},{9,8},{10,9... | collective-permute-start | bytes 786440 | tf_op jit(solution)/shard_map/ppermute | solution.py:399
  128.1 4.4 %sketch_tiles.3 = (f32[1,2048,128]{2,1,0:T(8,128)}, bf16[1,2048,256]{2,1,0:T(8,128)(2,1)}, bf16[1,2048,256]{2,1,0:T(8,128)(2,1)}, f32[1,128,128]{2,1,0:T(8,128)}) custom-call(f32[4,2048,128]{2,1,0:T(8,128)} %bitcast.56, f32[4,2048,128]{2,1,0:T(8,128)} %bitcast.58, f32[2048,128]{1,0:T(8,128)} %s_ref.5), custom_call_target="tpu_custom_call" | custom-call | flops 402653184 | bytes 5242880 | tf_op jit(solution)/shard_map/sketch_tiles/pallas_call | solution.py:119
  132.6 1.2 copy-done.4
  133.8 1.9 %copy-done.6 = bf16[3,2048,256]{2,1,0:T(8,128)(2,1)S(1)} copy-done((bf16[3,2048,256]{2,1,0:T(8,128)(2,1)S(1)}, bf16[3,2048,256]{2,1,0:T(8,128)(2,1)}, u32[]{:S(2)}) %copy-start.6) | copy-done | bytes 3145752
  135.7 1.2 copy-done.8
  136.9 0.9 copy-done.12
  137.8 0.9 copy-done.14
  138.8 0.9 copy-done.16
  139.7 3.5 %prepare.1 = (bf16[2048,256]{1,0:T(8,128)(2,1)S(1)}, f32[4,128,256]{2,1,0:T(8,128)S(1)}, f32[128,128]{1,0:T(8,128)S(1)}) custom-call(s32[2]{0:T(128)S(1)} %pad_add_fusion.at, f32[512,128]{1,0:T(8,128)S(1)} %bitcast.52, f32[512,128]{1,0:T(8,128)S(1)} %copy-done.14, f32[512,128]{1,0:T(8,128)S(1)} %copy-done.16, f32[512,128]{1,0:T(8,128)S(1)} %copy-done.12, ...), custom_call_target="tpu_custom_call" | custom-call | flops 1610612736 | bytes 8388608 | tf_op jit(solution)/shard_map/prepare/pallas_call | solution.py:278
  143.4 3.6 %project.1 = (bf16[4,2048,256]{2,1,0:T(8,128)(2,1)S(1)}, f32[4,128,128]{2,1,0:T(8,128)S(1)}) custom-call(s32[2]{0:T(128)S(1)} %pad_add_fusion.at, f32[4,4,2,128,128]{4,3,2,1,0:T(8,128)S(1)} %pad_maximum_fusion.1.mine, f32[4,4,2,128,128]{4,3,2,1,0:T(8,128)} %collective-permute-done.22.other, f32[2048,128]{1,0:T(8,128)S(1)} %copy-done.1), custom_call_target="tpu_custom_call" | custom-call | flops 805306368 | bytes 8388608 | tf_op jit(solution)/shard_map/project/pallas_call | solution.py:179
  146.9 2.0 %copy-done.3 = bf16[4,2048,256]{2,1,0:T(8,128)(2,1)} copy-done((bf16[4,2048,256]{2,1,0:T(8,128)(2,1)}, bf16[4,2048,256]{2,1,0:T(8,128)(2,1)S(1)}, u32[]{:S(2)}) %copy-start.3) | copy-done | bytes 4194328
  148.9 0.0 collective-permute-done.10.refs_1_
  149.0 19.1 %recompress.1 = (f32[4,2048,128]{2,1,0:T(8,128)}, f32[4,2048,128]{2,1,0:T(8,128)}) custom-call(f32[4,128,128]{2,1,0:T(8,128)S(1)} %get-tuple-element.29.refs_0_, f32[4,128,128]{2,1,0:T(8,128)S(1)} %collective-permute-done.10.refs_1_, f32[4,128,128]{2,1,0:T(8,128)S(1)} %collective-permute-done.11.refs_2_, f32[4,128,128]{2,1,0:T(8,128)} %collective-permute-done.12.refs_3_, ...), custom_call_target="tpu_custom_call" | custom-call | flops 3221225472 | bytes 29360128 | tf_op jit(solution)/shard_map/recompress/pallas_call | solution.py:372
  (38 shorter events, 0.2 us)
Async XLA Ops:
  0.6 16.8 %copy-start.19 = (f32[2,512,128]{2,1,0:T(8,128)S(1)}, f32[2,512,128]{2,1,0:T(8,128)}, u32[]{:S(2)}) copy-start(f32[2,512,128]{2,1,0:T(8,128)} %param.13) | copy-start | bytes 1572868
  1.9 6.6 %collective-permute-start.14 = (f32[2,128,128]{2,1,0:T(8,128)S(1)}, f32[2,128,128]{2,1,0:T(8,128)S(1)}, u32[]{:S(2)}, u32[]{:S(2)}) collective-permute-start(f32[2,128,128]{2,1,0:T(8,128)S(1)} %get-tuple-element.53), channel_id=1, source_target_pairs={{0,16},{4,20},{8,24},{12,28},{16,0},{20,4},{24,8},{28,12},{1,17},{... | collective-permute-start | bytes 393224 | tf_op jit(solution)/shard_map/ppermute | solution.py:396
  4.9 6.4 %collective-permute-start.13 = (f32[2,128,128]{2,1,0:T(8,128)S(1)}, f32[2,128,128]{2,1,0:T(8,128)S(1)}, u32[]{:S(2)}, u32[]{:S(2)}) collective-permute-start(f32[2,128,128]{2,1,0:T(8,128)S(1)} %get-tuple-element.54), channel_id=1, source_target_pairs={{0,8},{4,12},{8,0},{12,4},{16,24},{20,28},{24,16},{28,20},{1,9},{5... | collective-permute-start | bytes 393224 | tf_op jit(solution)/shard_map/ppermute | solution.py:396
  6.4 7.3 %collective-permute-start.15 = (f32[2,128,128]{2,1,0:T(8,128)S(1)}, f32[2,128,128]{2,1,0:T(8,128)S(1)}, u32[]{:S(2)}, u32[]{:S(2)}) collective-permute-start(f32[2,128,128]{2,1,0:T(8,128)S(1)} %get-tuple-element.55), channel_id=1, source_target_pairs={{0,24},{4,28},{8,16},{12,20},{16,8},{20,12},{24,0},{28,4},{1,25},{... | collective-permute-start | bytes 393224 | tf_op jit(solution)/shard_map/ppermute | solution.py:396
  6.5 25.1 %collective-permute-start.6 = (f32[2,512,128]{2,1,0:T(8,128)}, f32[2,512,128]{2,1,0:T(8,128)S(1)}, u32[]{:S(2)}, u32[]{:S(2)}) collective-permute-start(f32[2,512,128]{2,1,0:T(8,128)} %param.13), channel_id=1, source_target_pairs={{0,8},{4,12},{8,0},{12,4},{16,24},{20,28},{24,16},{28,20},{1,9},{5... | collective-permute-start | bytes 1572872 | tf_op jit(solution)/shard_map/ppermute | solution.py:396
  13.8 7.5 %collective-permute-start.18 = (f32[2,128,128]{2,1,0:T(8,128)S(1)}, f32[2,128,128]{2,1,0:T(8,128)S(1)}, u32[]{:S(2)}, u32[]{:S(2)}) collective-permute-start(f32[2,128,128]{2,1,0:T(8,128)S(1)} %get-tuple-element.49), channel_id=1, source_target_pairs={{0,3},{1,0},{2,1},{3,2},{4,7},{5,4},{6,5},{7,6},{8,11},{9,8},{10,9... | collective-permute-start | bytes 393224 | tf_op jit(solution)/shard_map/ppermute | solution.py:399
  17.4 18.8 %collective-permute-start.8 = (f32[2,512,128]{2,1,0:T(8,128)S(1)}, f32[2,512,128]{2,1,0:T(8,128)S(1)}, u32[]{:S(2)}, u32[]{:S(2)}) collective-permute-start(f32[2,512,128]{2,1,0:T(8,128)S(1)} %copy-done.19), channel_id=1, source_target_pairs={{0,24},{4,28},{8,16},{12,20},{16,8},{20,12},{24,0},{28,4},{1,25},{... | collective-permute-start | bytes 1572872 | tf_op jit(solution)/shard_map/ppermute | solution.py:396
  20.2 36.6 %collective-permute-start.7 = (f32[2,512,128]{2,1,0:T(8,128)S(1)}, f32[2,512,128]{2,1,0:T(8,128)S(1)}, u32[]{:S(2)}, u32[]{:S(2)}) collective-permute-start(f32[2,512,128]{2,1,0:T(8,128)S(1)} %copy-done.19), channel_id=1, source_target_pairs={{0,16},{4,20},{8,24},{12,28},{16,0},{20,4},{24,8},{28,12},{1,17},{... | collective-permute-start | bytes 1572872 | tf_op jit(solution)/shard_map/ppermute | solution.py:396
  20.8 5.9 %collective-permute-start.17 = (f32[2,128,128]{2,1,0:T(8,128)S(1)}, f32[2,128,128]{2,1,0:T(8,128)S(1)}, u32[]{:S(2)}, u32[]{:S(2)}) collective-permute-start(f32[2,128,128]{2,1,0:T(8,128)S(1)} %get-tuple-element.50), channel_id=1, source_target_pairs={{0,2},{1,3},{2,0},{3,1},{4,6},{5,7},{6,4},{7,5},{8,10},{9,11},{10,... | collective-permute-start | bytes 393224 | tf_op jit(solution)/shard_map/ppermute | solution.py:399
  21.3 7.2 %collective-permute-start.16 = (f32[2,128,128]{2,1,0:T(8,128)S(1)}, f32[2,128,128]{2,1,0:T(8,128)S(1)}, u32[]{:S(2)}, u32[]{:S(2)}) collective-permute-start(f32[2,128,128]{2,1,0:T(8,128)S(1)} %get-tuple-element.51), channel_id=1, source_target_pairs={{0,1},{1,2},{2,3},{3,0},{4,5},{5,6},{6,7},{7,4},{8,9},{9,10},{10,1... | collective-permute-start | bytes 393224 | tf_op jit(solution)/shard_map/ppermute | solution.py:399
  28.6 29.8 %collective-permute-start.21 = (f32[4,2,128,128]{3,2,1,0:T(8,128)S(1)}, f32[4,2,128,128]{3,2,1,0:T(8,128)S(1)}, u32[]{:S(2)}, u32[]{:S(2)}) collective-permute-start(f32[4,2,128,128]{3,2,1,0:T(8,128)S(1)} %pad_maximum_fusion.3), channel_id=1, source_target_pairs={{0,24},{4,28},{8,16},{12,20},{16,8},{20,12},{24,0},{28,4},{1,25},{... | collective-permute-start | bytes 1572872 | tf_op jit(solution)/shard_map/ppermute | solution.py:396
  30.4 33.8 %collective-permute-start.20 = (f32[4,2,128,128]{3,2,1,0:T(8,128)S(1)}, f32[4,2,128,128]{3,2,1,0:T(8,128)S(1)}, u32[]{:S(2)}, u32[]{:S(2)}) collective-permute-start(f32[4,2,128,128]{3,2,1,0:T(8,128)S(1)} %pad_maximum_fusion.3), channel_id=1, source_target_pairs={{0,16},{4,20},{8,24},{12,28},{16,0},{20,4},{24,8},{28,12},{1,17},{... | collective-permute-start | bytes 1572872 | tf_op jit(solution)/shard_map/ppermute | solution.py:396
  31.6 32.7 %collective-permute-start.19 = (f32[4,2,128,128]{3,2,1,0:T(8,128)S(1)}, f32[4,2,128,128]{3,2,1,0:T(8,128)S(1)}, u32[]{:S(2)}, u32[]{:S(2)}) collective-permute-start(f32[4,2,128,128]{3,2,1,0:T(8,128)S(1)} %pad_maximum_fusion.3), channel_id=1, source_target_pairs={{0,8},{4,12},{8,0},{12,4},{16,24},{20,28},{24,16},{28,20},{1,9},{5... | collective-permute-start | bytes 1572872 | tf_op jit(solution)/shard_map/ppermute | solution.py:396
  58.4 59.0 %collective-permute-start.9 = (f32[4,2,512,128]{3,2,1,0:T(8,128)}, f32[4,2,512,128]{3,2,1,0:T(8,128)}, u32[]{:S(2)}, u32[]{:S(2)}) collective-permute-start(f32[4,2,512,128]{3,2,1,0:T(8,128)} %pad_maximum_fusion.refs_4_), channel_id=1, source_target_pairs={{0,4},{4,0},{8,12},{12,8},{16,20},{20,16},{24,28},{28,24},{1,5},{5... | collective-permute-start | bytes 6291464 | tf_op jit(solution)/shard_map/ppermute | solution.py:396
  64.2 1.0 copy-start.7
  64.2 1.0 copy-start.10
  64.5 78.9 %collective-permute-start.22 = (f32[4,4,2,128,128]{4,3,2,1,0:T(8,128)S(1)}, f32[4,4,2,128,128]{4,3,2,1,0:T(8,128)}, u32[]{:S(2)}, u32[]{:S(2)}) collective-permute-start(f32[4,4,2,128,128]{4,3,2,1,0:T(8,128)S(1)} %pad_maximum_fusion.1.mine), channel_id=1, source_target_pairs={{0,4},{4,0},{8,12},{12,8},{16,20},{20,16},{24,28},{28,24},{1,5},{5... | collective-permute-start | bytes 6291464 | tf_op jit(solution)/shard_map/ppermute | solution.py:396
  65.3 14.8 %collective-permute-start.2 = (f32[512,128]{1,0:T(8,128)S(1)}, f32[512,128]{1,0:T(8,128)S(1)}, u32[]{:S(2)}, u32[]{:S(2)}) collective-permute-start(f32[512,128]{1,0:T(8,128)S(1)} %get-tuple-element.56), channel_id=1, source_target_pairs={{0,3},{1,0},{2,1},{3,2},{4,7},{5,4},{6,5},{7,6},{8,11},{9,8},{10,9... | collective-permute-start | bytes 786440 | tf_op jit(solution)/shard_map/ppermute | solution.py:399
  65.8 14.3 %collective-permute-start = (f32[512,128]{1,0:T(8,128)S(1)}, f32[512,128]{1,0:T(8,128)S(1)}, u32[]{:S(2)}, u32[]{:S(2)}) collective-permute-start(f32[512,128]{1,0:T(8,128)S(1)} %get-tuple-element.57), channel_id=1, source_target_pairs={{0,1},{1,2},{2,3},{3,0},{4,5},{5,6},{6,7},{7,4},{8,9},{9,10},{10,1... | collective-permute-start | bytes 786440 | tf_op jit(solution)/shard_map/ppermute | solution.py:399
  67.4 20.7 %collective-permute-start.1 = (f32[512,128]{1,0:T(8,128)S(1)}, f32[512,128]{1,0:T(8,128)S(1)}, u32[]{:S(2)}, u32[]{:S(2)}) collective-permute-start(f32[512,128]{1,0:T(8,128)S(1)} %get-tuple-element.58), channel_id=1, source_target_pairs={{0,2},{1,3},{2,0},{3,1},{4,6},{5,7},{6,4},{7,5},{8,10},{9,11},{10,... | collective-permute-start | bytes 786440 | tf_op jit(solution)/shard_map/ppermute | solution.py:399
  67.4 2.2 %copy-start.2 = (f32[512,2048]{1,0:T(8,128)S(1)}, f32[512,2048]{1,0:T(8,128)}, u32[]{:S(2)}) copy-start(f32[512,2048]{1,0:T(8,128)} %diag.1) | copy-start | bytes 12582916
  80.1 11.1 %copy-start.11 = (f32[512,128]{1,0:T(8,128)}, f32[512,128]{1,0:T(8,128)S(1)}, u32[]{:S(2)}) copy-start(f32[512,128]{1,0:T(8,128)S(1)} %collective-permute-done.2.refs_3_) | copy-start | bytes 786436
  80.1 11.1 %copy-start.13 = (f32[512,128]{1,0:T(8,128)}, f32[512,128]{1,0:T(8,128)S(1)}, u32[]{:S(2)}) copy-start(f32[512,128]{1,0:T(8,128)S(1)} %collective-permute-done.refs_1_) | copy-start | bytes 786436
  88.1 3.1 %copy-start.15 = (f32[512,128]{1,0:T(8,128)}, f32[512,128]{1,0:T(8,128)S(1)}, u32[]{:S(2)}) copy-start(f32[512,128]{1,0:T(8,128)S(1)} %collective-permute-done.1.refs_2_) | copy-start | bytes 786436
  91.2 13.7 %collective-permute-start.3 = (f32[512,128]{1,0:T(8,128)S(1)}, f32[512,128]{1,0:T(8,128)S(1)}, u32[]{:S(2)}, u32[]{:S(2)}) collective-permute-start(f32[512,128]{1,0:T(8,128)S(1)} %get-tuple-element.26), channel_id=1, source_target_pairs={{0,3},{1,0},{2,1},{3,2},{4,7},{5,4},{6,5},{7,6},{8,11},{9,8},{10,9... | collective-permute-start | bytes 786440 | tf_op jit(solution)/shard_map/ppermute | solution.py:399
  95.6 21.7 %collective-permute-start.4 = (f32[512,128]{1,0:T(8,128)S(1)}, f32[512,128]{1,0:T(8,128)S(1)}, u32[]{:S(2)}, u32[]{:S(2)}) collective-permute-start(f32[512,128]{1,0:T(8,128)S(1)} %get-tuple-element.27), channel_id=1, source_target_pairs={{0,2},{1,3},{2,0},{3,1},{4,6},{5,7},{6,4},{7,5},{8,10},{9,11},{10,... | collective-permute-start | bytes 786440 | tf_op jit(solution)/shard_map/ppermute | solution.py:399
  95.6 21.7 %collective-permute-start.5 = (f32[512,128]{1,0:T(8,128)S(1)}, f32[512,128]{1,0:T(8,128)S(1)}, u32[]{:S(2)}, u32[]{:S(2)}) collective-permute-start(f32[512,128]{1,0:T(8,128)S(1)} %get-tuple-element.28), channel_id=1, source_target_pairs={{0,1},{1,2},{2,3},{3,0},{4,5},{5,6},{6,7},{7,4},{8,9},{9,10},{10,1... | collective-permute-start | bytes 786440 | tf_op jit(solution)/shard_map/ppermute | solution.py:399
  121.7 27.2 %collective-permute-start.10 = (f32[4,128,128]{2,1,0:T(8,128)}, f32[4,128,128]{2,1,0:T(8,128)S(1)}, u32[]{:S(2)}, u32[]{:S(2)}) collective-permute-start(f32[4,128,128]{2,1,0:T(8,128)} %get-tuple-element.30), channel_id=1, source_target_pairs={{0,1},{1,2},{2,3},{3,0},{4,5},{5,6},{6,7},{7,4},{8,9},{9,10},{10,1... | collective-permute-start | bytes 786440 | tf_op jit(solution)/shard_map/ppermute | solution.py:399
  123.3 25.6 %collective-permute-start.11 = (f32[4,128,128]{2,1,0:T(8,128)}, f32[4,128,128]{2,1,0:T(8,128)S(1)}, u32[]{:S(2)}, u32[]{:S(2)}) collective-permute-start(f32[4,128,128]{2,1,0:T(8,128)} %get-tuple-element.31), channel_id=1, source_target_pairs={{0,2},{1,3},{2,0},{3,1},{4,6},{5,7},{6,4},{7,5},{8,10},{9,11},{10,... | collective-permute-start | bytes 786440 | tf_op jit(solution)/shard_map/ppermute | solution.py:399
  125.2 23.7 %collective-permute-start.12 = (f32[4,128,128]{2,1,0:T(8,128)}, f32[4,128,128]{2,1,0:T(8,128)}, u32[]{:S(2)}, u32[]{:S(2)}) collective-permute-start(f32[4,128,128]{2,1,0:T(8,128)} %get-tuple-element.32), channel_id=1, source_target_pairs={{0,3},{1,0},{2,1},{3,2},{4,7},{5,4},{6,5},{7,6},{8,11},{9,8},{10,9... | collective-permute-start | bytes 786440 | tf_op jit(solution)/shard_map/ppermute | solution.py:399
  128.1 4.4 %copy-start = (f32[3,2048,128]{2,1,0:T(8,128)S(1)}, f32[3,2048,128]{2,1,0:T(8,128)}, u32[]{:S(2)}) copy-start(f32[3,2048,128]{2,1,0:T(8,128)} %get-tuple-element.34.refs_8_.refs_9_) | copy-start | bytes 9437188
  132.6 1.2 copy-start.4
  133.8 1.9 %copy-start.6 = (bf16[3,2048,256]{2,1,0:T(8,128)(2,1)S(1)}, bf16[3,2048,256]{2,1,0:T(8,128)(2,1)}, u32[]{:S(2)}) copy-start(bf16[3,2048,256]{2,1,0:T(8,128)(2,1)} %get-tuple-element.35.refs_9_) | copy-start | bytes 9437188
  135.7 1.2 copy-start.8
  136.9 0.9 copy-start.12
  137.8 0.9 copy-start.14
  138.8 0.9 copy-start.16
  139.7 3.6 %copy-start.1 = (f32[2048,128]{1,0:T(8,128)S(1)}, f32[2048,128]{1,0:T(8,128)}, u32[]{:S(2)}) copy-start(f32[2048,128]{1,0:T(8,128)} %s_ref.5) | copy-start | bytes 3145732
  143.3 5.6 %copy-start.5 = (f32[1,2048,128]{2,1,0:T(8,128)S(1)}, f32[1,2048,128]{2,1,0:T(8,128)}, u32[]{:S(2)}) copy-start(f32[1,2048,128]{2,1,0:T(8,128)} %get-tuple-element.36.refs_10_) | copy-start | bytes 3145732
  143.3 5.6 %copy-start.9 = (bf16[1,2048,256]{2,1,0:T(8,128)(2,1)S(1)}, bf16[1,2048,256]{2,1,0:T(8,128)(2,1)}, u32[]{:S(2)}) copy-start(bf16[1,2048,256]{2,1,0:T(8,128)(2,1)} %get-tuple-element.43.refs_12_) | copy-start | bytes 3145732
  143.3 5.6 %copy-start.17 = (f32[3,128,128]{2,1,0:T(8,128)S(1)}, f32[3,128,128]{2,1,0:T(8,128)}, u32[]{:S(2)}) copy-start(f32[3,128,128]{2,1,0:T(8,128)} %get-tuple-element.40.refs_7_) | copy-start | bytes 589828
  143.3 5.6 %copy-start.18 = (f32[1,128,128]{2,1,0:T(8,128)S(1)}, f32[1,128,128]{2,1,0:T(8,128)}, u32[]{:S(2)}) copy-start(f32[1,128,128]{2,1,0:T(8,128)} %get-tuple-element.41.refs_8_) | copy-start | bytes 196612
  146.9 2.0 %copy-start.3 = (bf16[4,2048,256]{2,1,0:T(8,128)(2,1)}, bf16[4,2048,256]{2,1,0:T(8,128)(2,1)S(1)}, u32[]{:S(2)}) copy-start(bf16[4,2048,256]{2,1,0:T(8,128)(2,1)S(1)} %get-tuple-element.44.refs_13_) | copy-start | bytes 12582916
